TPU v7x, 32 devices: a whole 2x2x4 slice. The times are simulated.
32 devices in a mesh: rep: 8 (over z, y), shard: 4 (over x, core).
Axes of the slice: x: 2, y: 2, z: 4, core: 2. Of those that a mesh axis runs over, the one named last changes fastest.
Arguments:
- memory: float32 [32768, 256], P(('rep', 'shard')), may hold values from -4 to 4
- anchor_rows: int32 [8, 3, 1024], P('rep', None, 'shard'), may hold values from 0 to 255, as said below
- target_rows: int32 [8, 3, 1024], P('rep', None, 'shard'), may hold values from 0 to 255, as said below
- event_times: int32 [8, 3, 1024], P('rep', None, 'shard'), may hold values from 0 to 1023
- block_ids: int32 [8, 3, 4], P(None, None, 'shard'), may hold values from 0 to 127
- frequency: float32 [100], replicated, may hold values from 0.001 to 0.3
- phase: float32 [100], replicated, may hold values from -3.140625 to 3.140625
- w_source: bfloat16 [256, 256], replicated, may hold values from -0.375 to 0.375
- w_other: bfloat16 [256, 256], replicated, may hold values from -0.375 to 0.375
- w_time: bfloat16 [100, 256], replicated, may hold values from -0.625 to 0.625
- b_message: float32 [256], replicated, may hold values from -3 to 3
- w_input: bfloat16 [256, 768], replicated, may hold values from -0.375 to 0.375
- w_hidden: bfloat16 [256, 768], replicated, may hold values from -0.375 to 0.375
- b_gates: float32 [768], replicated, may hold values from -3 to 3
Outputs:
- memory_out: float32 [32768, 256], P(('rep', 'shard'))
Inputs may be any that keep to these rules, and one draw needn't show every extreme that they name: Position j names row j % 64 of the block of shard column j // 64 chosen by block_ids[g, b, j // 64]; in each group and batch, each position block j // 64 is named by exactly 512 of the 2048 entries of anchor_rows and target_rows together. `target_rows`: as for anchor_rows. `block_ids`: value q in shard column s names block q % 16 of the memory rows of the device with rep index q // 16 and shard index s; that device owns rows ((q // 16) * 4 + s) * 16 * 64 onwards, 1024 of them.
All inputs are finite; a program needn't handle non-finite values.
Results may differ from a plain program's by a relative error of at most 0.00093.
Values may be sent and summed in bfloat16 or wider, within the bound.
No kernel may reach another device: no remote copies, remote signals or barrier semaphores. Data moves between devices by JAX's collectives and lax.ppermute only.
A program may use at most 64 MiB of HBM per device.

v0:
```python
import functools

import jax
import jax.numpy as jnp
from jax import lax
from jax.experimental import pallas as pl
from jax.experimental.pallas import tpu as pltpu
from jax.sharding import PartitionSpec as P

BLK = 64
LANES = 128
COUNT_ROWS = 8
STEPS = 6400.0
VMEM = pl.BlockSpec(memory_space=pltpu.VMEM)
SMEM = pl.BlockSpec(memory_space=pltpu.SMEM)
HBM = pl.BlockSpec(memory_space=pltpu.HBM)
ALL_ROOM = pltpu.CompilerParams(vmem_limit_bytes=60 << 20)
ROOM = pltpu.CompilerParams(vmem_limit_bytes=12 << 20)


NT = (((1,), (1,)), ((), ()))


def bdot(a, b, dims=None):
    if dims is None:
        return jnp.dot(a, b, preferred_element_type=jnp.float32)
    return lax.dot_general(a, b, dims, preferred_element_type=jnp.float32)


def partner(i, k, n):
    return i ^ k if n & (n - 1) == 0 else (i + k) % n


def slot_of(column, me, n):
    return column ^ me if n & (n - 1) == 0 else lax.rem(column - me + n, n)


def share(block, n):
    got = [block]
    for k in range(1, n):
        got.append(lax.ppermute(block, "shard", [(partner(i, k, n), i) for i in range(n)]))
    return got


def bit_order(n):
    top = n.bit_length() - 1
    return [0] + list(range(top - 1, 0, -1))


def cube_lists(n):
    left, steps = list(range(n)), []
    for bit in bit_order(n):
        left = [j for j in left if not j >> bit & 1]
        steps.append((bit, left))
    return steps


def pick_kernel(batches, count, n_lists, ids_ref, mem_ref, *refs):
    lists, refs = refs[:n_lists], refs[n_lists:]
    n_small = (len(refs) - 2 * batches - 3) // 2
    small, refs = refs[:n_small], refs[n_small:]
    first_ref, idx_ref, refs = refs[0], refs[1], refs[2:]
    halves, small_out, refs = refs[: 2 * batches - 2], refs[2 * batches - 2 : 2 * batches - 2 + n_small], refs[-3:]
    bufs, sems, list_sems = refs
    groups = ids_ref.shape[2]
    bit, kept = cube_lists(groups)[0]
    me = lax.axis_index("rep")
    plan = [(0, g, first_ref, g) for g in range(groups)]
    for b in range(1, batches):
        keep_ref, send_ref = halves[2 * b - 2 : 2 * b]
        plan += [(b, me ^ (j | 1 << bit), send_ref, k) for k, j in enumerate(kept)]
        plan += [(b, me ^ j, keep_ref, k) for k, j in enumerate(kept)]
    copies = []
    for k, (b, g, _, _) in enumerate(plan):
        cp = pltpu.make_async_copy(mem_ref.at[lax.rem(ids_ref[b, 0, g], count)], bufs.at[k], sems.at[k])
        cp.start()
        copies.append(cp)
    moves = [(ref, idx_ref.at[k]) for k, ref in enumerate(lists)] + list(zip(small, small_out))
    rest = [pltpu.make_async_copy(src, dst, list_sems.at[k]) for k, (src, dst) in enumerate(moves)]
    for cp in rest:
        cp.start()
    for k, (_, _, out_ref, at) in enumerate(plan):
        copies[k].wait()
        out_ref[at] = bufs[k].astype(jnp.bfloat16)
    for cp in rest:
        cp.wait()


def pick(ids, mem, lists, small):
    count, rows, width = mem.shape
    batches, _, groups = ids.shape
    half = jax.ShapeDtypeStruct((groups // 2, rows, width), jnp.bfloat16)
    first, idx, *out = pl.pallas_call(
        functools.partial(pick_kernel, batches, count, len(lists)),
        out_shape=[
            jax.ShapeDtypeStruct((groups, rows, width), jnp.bfloat16),
            jax.ShapeDtypeStruct((len(lists), *lists[0].shape), jnp.int32),
        ]
        + [half] * (2 * batches - 2)
        + [jax.ShapeDtypeStruct(x.shape, x.dtype) for x in small],
        in_specs=[SMEM] + [HBM] * (1 + len(lists) + len(small)),
        out_specs=[VMEM] * (2 + 2 * batches - 2 + len(small)),
        scratch_shapes=[
            pltpu.VMEM((batches * groups, rows, width), mem.dtype),
            pltpu.SemaphoreType.DMA((batches * groups,)),
            pltpu.SemaphoreType.DMA((len(lists) + len(small),)),
        ],
        compiler_params=ALL_ROOM,
        cost_estimate=pl.CostEstimate(flops=20_000_000, bytes_accessed=1_000_000, transcendentals=0),
        name="pick",
    )(ids, mem, *lists, *small)
    halves = [out[2 * b : 2 * b + 2] for b in range(batches - 1)]
    return first, idx, halves, out[2 * batches - 2 :]


def from_partner(ids_ref, b, count, j, bit, me):
    owner = lax.div(ids_ref[b, 0, me ^ j], count)
    return (lax.shift_right_logical(owner ^ me, bit) & 1) == 1


def merge_kernel(b, step, count, ids_ref, keep_in, got_ref, keep_ref, send_ref):
    steps = cube_lists(ids_ref.shape[2])
    me = lax.axis_index("rep")
    (bit, kept), (_, after) = steps[step], steps[step + 1]
    for i, j in enumerate(kept):
        out_ref = keep_ref if j in after else send_ref
        k = after.index(j if j in after else j ^ (1 << steps[step + 1][0]))
        other = from_partner(ids_ref, b, count, j, bit, me)

        @pl.when(other)
        def _():
            out_ref[k] = got_ref[i]

        @pl.when(jnp.logical_not(other))
        def _():
            out_ref[k] = keep_in[i]


def merge(b, step, ids, count, keep, got):
    half, rows, width = keep.shape
    return pl.pallas_call(
        functools.partial(merge_kernel, b, step, count),
        out_shape=[jax.ShapeDtypeStruct((half // 2, rows, width), keep.dtype)] * 2,
        in_specs=[SMEM, VMEM, VMEM],
        out_specs=[VMEM] * 2,
        compiler_params=ROOM,
        cost_estimate=pl.CostEstimate(flops=1_000_000, bytes_accessed=300_000, transcendentals=0),
        name="merge",
    )(ids, keep, got)


def cube(b, ids, keep, send, count):
    groups = ids.shape[2]
    bits = bit_order(groups)
    for step, bit in enumerate(bits):
        got = lax.ppermute(send, "rep", [(i, i ^ 1 << bit) for i in range(groups)])
        if step < len(bits) - 1:
            keep, send = merge(b, step, ids, count, keep, got)
    return keep, got


def cosine(x):
    turns = jnp.floor(x * 0.15915494309189535 + 0.5)
    r = x - turns * 6.28125
    r = r - turns * 0.00193500518798828125
    r = r - turns * 3.0199159819567e-07
    h = r * 0.5
    s = h * h
    c = -1.1470745597729725e-11
    c = c * s + 2.08767569878681e-09
    c = c * s - 2.755731922398589e-07
    c = c * s + 2.48015873015873e-05
    c = c * s - 0.001388888888888889
    c = c * s + 0.041666666666666664
    c = c * s - 0.5
    c = c * s + 1.0
    return 2.0 * c * c - 1.0


def own_and_other(idx, b):
    anchor, target, moment = (
        [r[k, b][:, at : at + LANES] for r in idx for at in range(0, r.shape[3], LANES)] for k in range(3)
    )
    return (jnp.concatenate(x, 0) for x in (anchor + target, target + anchor, moment + moment))


def prep_kernel(b, shards, *refs):
    idx, refs = refs[:shards], refs[shards:]
    freq_ref, phase_ref, cols_ref, row_ref, enc_ref, *tally_ref, pack = refs
    me = lax.axis_index("shard")
    entries = cols_ref.shape[0]
    lines = pack.shape[0]
    up = lax.broadcasted_iota(jnp.int32, (LANES, LANES), 0)
    across = lax.broadcasted_iota(jnp.int32, (LANES, LANES), 1)
    before = (up < across).astype(jnp.float32).astype(jnp.bfloat16)
    ones = jnp.ones((LANES, LANES), jnp.bfloat16)
    lup = lax.broadcasted_iota(jnp.int32, (lines, lines), 0)
    lac = lax.broadcasted_iota(jnp.int32, (lines, lines), 1)
    above = (lac < lup).astype(jnp.float32).astype(jnp.bfloat16)
    order = lax.broadcasted_iota(jnp.int32, (entries, LANES), 0).astype(jnp.float32)
    own, other, moment = own_and_other(idx, b)
    mine = lax.shift_right_logical(own, 6) == me
    minef = mine.astype(jnp.float32).astype(jnp.bfloat16)
    rank = bdot(minef, before) + bdot(above, bdot(minef, ones).astype(jnp.bfloat16))
    rank = jnp.where(mine, rank, -1.0)
    place = slot_of(lax.shift_right_logical(other, 6), me, shards) * BLK + (other & (BLK - 1))
    digits = [
        own & (BLK - 1),
        place & 255,
        lax.shift_right_logical(place, 8),
        moment & 255,
        lax.shift_right_logical(moment, 8),
    ]
    for i, d in enumerate(digits):
        pack[:, i, :] = d.astype(jnp.float32)
    pack[:, 5, :] = jnp.zeros((lines, LANES), jnp.float32)
    pack[:, 6, :] = jnp.zeros((lines, LANES), jnp.float32)
    pack[:, 7, :] = rank

    def step(r, total):
        line = pack[r]
        hot = (line[7:8, :] == order).astype(jnp.float32).astype(jnp.bfloat16)
        return total + bdot(hot, line.astype(jnp.bfloat16), NT)

    cols = lax.fori_loop(0, lines, step, jnp.zeros((entries, 8), jnp.float32), unroll=min(lines, 16))
    wide = jnp.concatenate([cols, jnp.zeros((entries, LANES - 8), jnp.float32)], 1).astype(jnp.bfloat16)
    cols_ref[...] = wide
    eye = (
        lax.broadcasted_iota(jnp.int32, (8, LANES), 0) == lax.broadcasted_iota(jnp.int32, (8, LANES), 1)
    ).astype(jnp.float32).astype(jnp.bfloat16)
    row_ref[...] = bdot(eye, wide, NT)
    time = cols[:, 3:4] + 256.0 * cols[:, 4:5]
    enc_ref[...] = cosine(time * freq_ref[...] + phase_ref[...]).astype(jnp.bfloat16)
    if tally_ref:
        width = tally_ref[0].shape[1]
        line = lax.broadcasted_iota(jnp.int32, (COUNT_ROWS, LANES), 0)
        local = lax.broadcasted_iota(jnp.int32, (LANES, LANES), 0)
        tally = jnp.zeros((COUNT_ROWS, LANES), jnp.float32)
        for e in range(idx[0].shape[1]):
            rows, _, _ = own_and_other(idx, e)
            rows = rows - me * BLK
            hits = jnp.zeros((LANES, LANES), jnp.float32)
            for r in range(lines):
                hits = hits + jnp.where(rows[r : r + 1, :] == local, 1.0, 0.0)
            count = bdot(jnp.ones((COUNT_ROWS, LANES), jnp.bfloat16), hits.astype(jnp.bfloat16), NT)
            tally = jnp.where(line == e, count, tally)
        tally = jnp.concatenate([tally] * (width // LANES), 1)
        tally_ref[0][...] = tally.astype(jnp.int32).astype(jnp.int16)


def prep(b, idx, freq, phase, entries, width):
    lines = 2 * len(idx) * idx[0].shape[3] // LANES
    out = [
        jax.ShapeDtypeStruct((entries, LANES), jnp.bfloat16),
        jax.ShapeDtypeStruct((8, entries), jnp.float32),
        jax.ShapeDtypeStruct((entries, freq.shape[1]), jnp.bfloat16),
    ]
    if b == 0:
        out.append(jax.ShapeDtypeStruct((COUNT_ROWS, width), jnp.int16))
    return pl.pallas_call(
        functools.partial(prep_kernel, b, len(idx)),
        out_shape=out,
        in_specs=[VMEM] * (len(idx) + 2),
        out_specs=[VMEM] * len(out),
        scratch_shapes=[pltpu.VMEM((lines, 8, LANES), jnp.float32)],
        compiler_params=ROOM,
        cost_estimate=pl.CostEstimate(flops=100_000_000, bytes_accessed=1_000_000, transcendentals=0),
        name="prep",
    )(*idx, freq, phase)


def batch_kernel(n, tallies, cols_ref, row_ref, enc_ref, ws_ref, wo_ref, wt_ref, bm_ref, wi_ref, wh_ref, bg_ref, *rest):
    counts, blocks, out_ref = rest[:tallies], rest[tallies : tallies + n], rest[-1]
    width = out_ref.shape[2]
    entries = cols_ref.shape[0]
    table = jnp.concatenate([blk[...] for blk in blocks], 0)
    mine = blocks[0][...]
    chunk = min(entries, 256)
    total = jnp.zeros((BLK, width), jnp.float32)
    tally = jnp.zeros((BLK, LANES), jnp.float32)
    for c in range(entries // chunk):
        at = slice(c * chunk, (c + 1) * chunk)
        cols = cols_ref[at, :].astype(jnp.float32)
        own_hot = (
            lax.broadcasted_iota(jnp.int32, (chunk, BLK), 1).astype(jnp.float32) == cols[:, 0:1]
        ).astype(jnp.float32).astype(jnp.bfloat16)
        place = cols[:, 1:2] + 256.0 * cols[:, 2:3]
        other_hot = (
            lax.broadcasted_iota(jnp.int32, (chunk, n * BLK), 1).astype(jnp.float32) == place
        ).astype(jnp.float32).astype(jnp.bfloat16)
        own = bdot(own_hot, mine).astype(jnp.bfloat16)
        other = bdot(other_hot, table).astype(jnp.bfloat16)
        message = bdot(own, ws_ref[...]) + bdot(other, wo_ref[...])
        message = message + (bdot(enc_ref[at, :], wt_ref[...]) + bm_ref[...])
        message = jnp.maximum(message, 0.0).astype(jnp.bfloat16)

        def gate(part):
            cut = slice(part * width, (part + 1) * width)
            return bdot(message, wi_ref[:, cut]), bdot(own, wh_ref[:, cut]), bg_ref[:, cut]

        gi, gh, bias = gate(0)
        reset = 0.5 * jnp.tanh(0.5 * (gi + gh + bias)) + 0.5
        gi, gh, bias = gate(2)
        candidate = jnp.tanh(gi + bias + reset * gh)
        gi, gh, bias = gate(1)
        keep = 0.5 - 0.5 * jnp.tanh(0.5 * (gi + gh + bias))
        delta = (keep * (candidate - own.astype(jnp.float32))).astype(jnp.bfloat16)
        back_hot = (
            lax.broadcasted_iota(jnp.int32, (BLK, chunk), 0).astype(jnp.float32) == row_ref[0:1, at]
        ).astype(jnp.float32).astype(jnp.bfloat16)
        total = total + bdot(back_hot, delta)
        tally = tally + bdot(back_hot, jnp.ones((chunk, LANES), jnp.bfloat16))
    scale = STEPS / jnp.maximum(tally, 1.0)
    mean = total * jnp.concatenate([scale] * (width // LANES), 1)
    out = jnp.round(mean).astype(jnp.int32).astype(jnp.int16)
    if counts:
        out = jnp.concatenate([out, counts[0][...]], 0)
    for g in range(out_ref.shape[0]):
        out_ref[g] = out


def batch_step(blocks, entry, counts, weights, groups):
    width = blocks[0].shape[1]
    args = (*entry, *weights, *counts, *blocks)
    rows = BLK + (COUNT_ROWS if counts else 0)
    return pl.pallas_call(
        functools.partial(batch_kernel, len(blocks), len(counts)),
        out_shape=jax.ShapeDtypeStruct((groups, rows, width), jnp.int16),
        in_specs=[VMEM] * len(args),
        out_specs=VMEM,
        cost_estimate=pl.CostEstimate(flops=100_000_000, bytes_accessed=4_000_000, transcendentals=400_000),
        compiler_params=ROOM,
        name="batch",
    )(*args)


def column(row):
    up = lax.broadcasted_iota(jnp.int32, (BLK, LANES), 0)
    across = lax.broadcasted_iota(jnp.int32, (BLK, LANES), 1)
    return jnp.sum(jnp.where(up == across, row[:, :LANES], 0.0), axis=1, keepdims=True)


def gather_hits(ids_ref, delta, counts, b, block, first, total, tally):
    total[...] = jnp.zeros_like(total)
    tally[...] = jnp.zeros_like(tally)
    for g in range(first, delta.shape[0]):

        @pl.when(ids_ref[b, 0, g] == block)
        def _():
            count = column(counts[g, BLK : BLK + COUNT_ROWS, :].astype(jnp.int32).astype(jnp.float32)[b : b + 1])
            tally[...] += jnp.broadcast_to(count, tally.shape)
            total[...] += delta[g, :BLK, :].astype(jnp.int32).astype(jnp.float32) * (count * (1.0 / STEPS))


def gain(total, tally):
    scale = 1.0 / jnp.maximum(tally[...], 1.0)
    return total[...] * jnp.concatenate([scale] * (total.shape[1] // LANES), 1)


def next_kernel(b, count, ids_ref, *refs):
    (*rest, out_ref, value, total, tally) = refs
    starts, deltas = rest[: len(rest) - b], rest[len(rest) - b :]
    groups = ids_ref.shape[2]
    me = lax.axis_index("rep")
    mine = ids_ref[b, 0, me]
    if len(starts) == 1:
        value[...] = starts[0][lax.div(mine, count)].astype(jnp.float32)
    else:
        other = from_partner(ids_ref, b, count, 0, bit_order(groups)[-1], me)
        value[...] = starts[0][0].astype(jnp.float32)

        @pl.when(other)
        def _():
            value[...] = starts[1][0].astype(jnp.float32)

    for e in range(b):
        hit = ids_ref[e, 0, 0] == mine
        for g in range(1, groups):
            hit = jnp.logical_or(hit, ids_ref[e, 0, g] == mine)

        @pl.when(hit)
        def _():
            gather_hits(ids_ref, deltas[e], deltas[0], e, mine, 0, total, tally)
            value[...] += gain(total, tally)

    out_ref[...] = value[...].astype(jnp.bfloat16)


def scratch(rows, width):
    return [pltpu.VMEM((rows, width), jnp.float32), pltpu.VMEM((rows, LANES), jnp.float32)]


def next_block(b, count, ids, starts, deltas):
    rows, width = BLK, starts[0].shape[2]
    return pl.pallas_call(
        functools.partial(next_kernel, b, count),
        out_shape=jax.ShapeDtypeStruct((rows, width), jnp.bfloat16),
        in_specs=[SMEM] + [VMEM] * (len(starts) + len(deltas)),
        out_specs=VMEM,
        scratch_shapes=[pltpu.VMEM((rows, width), jnp.float32)] + scratch(rows, width),
        compiler_params=ROOM,
        name="next_block",
    )(ids, *starts, *deltas)


def is_fresh(ids_ref, b, g, count, me):
    block = ids_ref[b, 0, g]
    fresh = lax.div(block, count) == me
    for e in range(g):
        fresh = jnp.logical_and(fresh, ids_ref[b, 0, e] != block)
    return block, fresh


def settle_kernel(count, ids_ref, mem_ref, *rest):
    deltas, (out_ref, last_ref, total, tally, sem) = rest[:-5], rest[-5:]
    groups = deltas[0].shape[0]
    me = lax.axis_index("rep")
    cp = pltpu.make_async_copy(mem_ref, out_ref, sem)
    cp.start()
    cp.wait()
    for b, delta in enumerate(deltas):
        for g in range(groups):
            block, fresh = is_fresh(ids_ref, b, g, count, me)

            @pl.when(fresh)
            def _():
                gather_hits(ids_ref, delta, deltas[0], b, block, g, total, tally)
                place = lax.rem(block, count)
                out_ref[place] += gain(total, tally)

    for g in range(groups):
        last_ref[g] = out_ref[lax.rem(ids_ref[len(deltas), 0, g], count)]


def settle(count, ids, mem, deltas):
    rows, width = mem.shape[1:]
    return pl.pallas_call(
        functools.partial(settle_kernel, count),
        out_shape=[
            jax.ShapeDtypeStruct(mem.shape, mem.dtype),
            jax.ShapeDtypeStruct((deltas[0].shape[0], rows, width), mem.dtype),
        ],
        in_specs=[SMEM, HBM] + [VMEM] * len(deltas),
        out_specs=[VMEM] * 2,
        scratch_shapes=scratch(rows, width) + [pltpu.SemaphoreType.DMA],
        cost_estimate=pl.CostEstimate(flops=20_000_000, bytes_accessed=3_000_000, transcendentals=0),
        compiler_params=ROOM,
        name="settle",
    )(ids, mem, *deltas)


def finish_kernel(b, count, ids_ref, mem_ref, last_ref, counts, delta, out_ref, bufs, total, tally, sems):
    me = lax.axis_index("rep")
    for g in range(delta.shape[0]):
        block, fresh = is_fresh(ids_ref, b, g, count, me)

        @pl.when(fresh)
        def _():
            gather_hits(ids_ref, delta, counts, b, block, g, total, tally)
            bufs[g] = last_ref[g] + gain(total, tally)
            pltpu.make_async_copy(bufs.at[g], out_ref.at[lax.rem(block, count)], sems.at[g]).start()

    for g in range(delta.shape[0]):
        block, fresh = is_fresh(ids_ref, b, g, count, me)

        @pl.when(fresh)
        def _():
            pltpu.make_async_copy(bufs.at[g], out_ref.at[lax.rem(block, count)], sems.at[g]).wait()


def finish(b, count, ids, mem, last, counts, delta):
    groups, rows, width = last.shape
    return pl.pallas_call(
        functools.partial(finish_kernel, b, count),
        out_shape=jax.ShapeDtypeStruct(mem.shape, mem.dtype),
        in_specs=[SMEM, HBM, VMEM, VMEM, VMEM],
        out_specs=HBM,
        input_output_aliases={1: 0},
        scratch_shapes=[pltpu.VMEM(last.shape, jnp.float32)]
        + scratch(rows, width)
        + [pltpu.SemaphoreType.DMA((groups,))],
        compiler_params=ROOM,
        name="finish",
    )(ids, mem, last, counts, delta)


def exchange(x):
    return lax.all_to_all(x, "rep", split_axis=0, concat_axis=0, tiled=True)


def local(
    memory,
    anchor_rows,
    target_rows,
    event_times,
    block_ids,
    frequency,
    phase,
    w_source,
    w_other,
    w_time,
    b_message,
    w_input,
    w_hidden,
    b_gates,
):
    width = memory.shape[1]
    count = memory.shape[0] // BLK
    groups, batches = block_ids.shape[0], block_ids.shape[1]
    shards = lax.axis_size("shard")
    entries = 2 * anchor_rows.shape[2]
    ids = jnp.transpose(block_ids, (1, 2, 0))
    mem = memory.reshape(count, BLK, width)
    raw = [jnp.swapaxes(x, 0, 1) for x in (anchor_rows, target_rows, event_times)]
    small = (frequency.reshape(1, -1), phase.reshape(1, -1), b_message.reshape(1, -1))
    sent, idx, halves, (freq, shift, bm) = pick(ids, mem, raw, small)
    weights = (w_source, w_other, w_time, bm, w_input, w_hidden, b_gates.reshape(1, -1))
    starts = [(exchange(sent),)]
    starts += [cube(b, ids, *halves[b - 1], count) for b in range(1, batches)]
    idx = share(idx, shards)
    entry, counts = [], ()
    for b in range(batches):
        out = prep(b, idx, freq, shift, entries, width)
        entry.append(out[:3])
        counts = counts or out[3:]
    deltas = []
    for b in range(batches):
        block = next_block(b, count, ids, starts[b], deltas)
        blocks = share(block, shards)
        sent = batch_step(blocks, entry[b], counts if b == 0 else (), weights, groups)
        deltas.append(exchange(sent))
    mem, last = settle(count, ids, mem, deltas[:-1])
    mem = finish(batches - 1, count, ids, mem, last, deltas[0], deltas[-1])
    return mem.reshape(memory.shape)


def solution(mesh):
    in_specs = (
        P(("rep", "shard"), None),
        P("rep", None, "shard"),
        P("rep", None, "shard"),
        P("rep", None, "shard"),
        P(None, None, "shard"),
        P(),
        P(),
        P(),
        P(),
        P(),
        P(),
        P(),
        P(),
        P(),
    )
    out_specs = P(("rep", "shard"), None)
    return jax.shard_map(local, mesh=mesh, in_specs=in_specs, out_specs=out_specs, check_vma=False)
```

profile of v0, /device:TPU:0, one launch (start us, length us, event | category | flops | bytes accessed | tf_op | source)
XLA Modules:
  0.0 108.6 jit_solution(15628759178997916579)
XLA Ops:
  0.0 3.3 %pick.1 = (bf16[8,64,256]{2,1,0:T(8,128)(2,1)}, s32[3,3,1,256]{3,2,1,0:T(1,128)}, bf16[4,64,256]{2,1,0:T(8,128)(2,1)}, bf16[4,64,256]{2,1,0:T(8,128)(2,1)}, bf16...) custom-call(s32[3,1,8]{2,1,0:T(1,128)} %bitcast.11, ...), custom_call_target="tpu_custom_call" | custom-call | flops 20000000 | bytes 1000000 | tf_op jit(solution)/shard_map/pick/pallas_call | solution.py:93
  3.3 0.0 copy-start.6
  3.3 0.0 copy-start.13
  3.3 0.0 copy-start.2
  3.4 0.0 copy-start.5
  3.4 16.4 %all_to_all.20.refs_0_ = bf16[8,64,256]{2,1,0:T(8,128)(2,1)S(1)} all-to-all(bf16[8,64,256]{2,1,0:T(8,128)(2,1)} %get-tuple-element.42), channel_id=1, replica_groups=mesh['rep'=8,'shard'=4] {'rep'}, dimensions={0} | all-to-all | bytes 524288 | tf_op jit(solution)/shard_map/all_to_all | solution.py:488
  19.7 0.6 next_block.3.rest_1_
  20.3 0.1 collective-permute-start.5
  20.4 1.6 %collective-permute-start.4 = (bf16[64,256]{1,0:T(8,128)(2,1)S(1)}, bf16[64,256]{1,0:T(8,128)(2,1)S(1)}, u32[]{:S(2)}, u32[]{:S(2)}) collective-permute-start(bf16[64,256]{1,0:T(8,128)(2,1)S(1)} %next_block.3.rest_1_), channel_id=1, source_target_pairs={{2,0},{3,1},{0,2},{1,3},{6,4},{7,5},{4,6},{5,7},{10,8},{11,9},{8,1... | collective-permute-start | bytes 98312 | tf_op jit(solution)/shard_map/ppermute | solution.py:41
  22.0 0.3 collective-permute-start.3
  22.3 1.1 %collective-permute-start.2 = (s32[3,3,1,256]{3,2,1,0:T(1,128)S(1)}, s32[3,3,1,256]{3,2,1,0:T(1,128)S(1)}, u32[]{:S(2)}, u32[]{:S(2)}) collective-permute-start(s32[3,3,1,256]{3,2,1,0:T(1,128)S(1)} %copy-done.10), channel_id=1, source_target_pairs={{3,0},{2,1},{1,2},{0,3},{7,4},{6,5},{5,6},{4,7},{11,8},{10,9},{9,1... | collective-permute-start | bytes 27656 | tf_op jit(solution)/shard_map/ppermute | solution.py:41
  23.4 0.8 collective-permute-start.1
  24.1 1.2 %collective-permute-done.2.refs_3_ = s32[3,3,1,256]{3,2,1,0:T(1,128)S(1)} collective-permute-done((s32[3,3,1,256]{3,2,1,0:T(1,128)S(1)}, s32[3,3,1,256]{3,2,1,0:T(1,128)S(1)}, u32[]{:S(2)}, u32[]{:S(2)}) %collective-permute-start.2) | collective-permute-done | bytes 9248 | tf_op jit(solution)/shard_map/ppermute | solution.py:41
  25.3 0.2 collective-permute-start
  25.6 1.4 %collective-permute-done.1.refs_2_ = s32[3,3,1,256]{3,2,1,0:T(1,128)S(1)} collective-permute-done((s32[3,3,1,256]{3,2,1,0:T(1,128)S(1)}, s32[3,3,1,256]{3,2,1,0:T(1,128)S(1)}, u32[]{:S(2)}, u32[]{:S(2)}) %collective-permute-start.1) | collective-permute-done | bytes 9248 | tf_op jit(solution)/shard_map/ppermute | solution.py:41
  27.0 0.0 collective-permute-done.refs_1_
  27.0 0.0 copy-start.3
  27.1 0.0 copy-start.4
  27.1 1.7 %prep.3 = (bf16[512,128]{1,0:T(8,128)(2,1)S(1)}, f32[8,512]{1,0:T(8,128)S(1)}, bf16[512,100]{1,0:T(8,128)(2,1)S(1)}, s16[8,256]{1,0:T(8,128)(2,1)S(1)}) custom-call(s32[3,3,1,256]{3,2,1,0:T(1,128)S(1)} %copy-done.10, s32[3,3,1,256]{3,2,1,0:T(1,128)S(1)} %collective-permute-done.refs_1_, s32[3,3,1,256]{3,2,1,0:T(1,128)S(1)} %collective-permute-done.1.refs_2_, ...), custom_call_target="tpu_custom_call" | custom-call | flops 100000000 | bytes 1000000 | tf_op jit(solution)/shard_map/prep/pallas_call | solution.py:260
  28.8 0.0 collective-permute-done.5.rest_4_
  28.8 0.0 collective-permute-done.4.rest_3_
  28.8 0.0 collective-permute-done.3.rest_2_
  28.9 0.6 copy-done.9
  29.5 2.5 %batch.3 = s16[8,72,256]{2,1,0:T(8,128)(2,1)} custom-call(bf16[512,128]{1,0:T(8,128)(2,1)S(1)} %get-tuple-element.37.cols_ref, f32[8,512]{1,0:T(8,128)S(1)} %get-tuple-element.38.row_ref, bf16[512,100]{1,0:T(8,128)(2,1)S(1)} %get-tuple-element.39.enc_ref, bf16[256,256]{1,0:T(8,128)(2,1)S(1)} %copy-done.3, bf16[256,256]{1,0:T(8,128)(2,1)S(1)} %copy-done.4, ...), custom_call_target="tpu_custom_call" | custom-call | flops 100000000 | bytes 4000000 | tf_op jit(solution)/shard_map/batch/pallas_call | solution.py:326
  32.0 3.7 %all-to-all-start.1 = ((s16[8,72,256]{2,1,0:T(8,128)(2,1)}), s16[8,72,256]{2,1,0:T(8,128)(2,1)S(1)}, u32[]{:S(2)}, u32[]{:S(2)}) async-start(s16[8,72,256]{2,1,0:T(8,128)(2,1)} %batch.3), calls=%async_computation.1 | async-start | bytes 589824 | tf_op jit(solution)/shard_map/all_to_all | solution.py:488
  35.7 2.0 %collective-permute-start.6 = (bf16[4,64,256]{2,1,0:T(8,128)(2,1)S(1)}, bf16[4,64,256]{2,1,0:T(8,128)(2,1)S(1)}, u32[]{:S(2)}, u32[]{:S(2)}) collective-permute-start(bf16[4,64,256]{2,1,0:T(8,128)(2,1)S(1)} %copy-done.15), channel_id=1, source_target_pairs={{0,4},{4,0},{8,12},{12,8},{16,20},{20,16},{24,28},{28,24},{1,5},{5... | collective-permute-start | bytes 393224 | tf_op jit(solution)/shard_map/ppermute | solution.py:156
  37.7 5.8 %collective-permute-done.6.got_ref = bf16[4,64,256]{2,1,0:T(8,128)(2,1)S(1)} collective-permute-done((bf16[4,64,256]{2,1,0:T(8,128)(2,1)S(1)}, bf16[4,64,256]{2,1,0:T(8,128)(2,1)S(1)}, u32[]{:S(2)}, u32[]{:S(2)}) %collective-permute-start.6) | collective-permute-done | bytes 131104 | tf_op jit(solution)/shard_map/ppermute | solution.py:156
  43.5 0.6 merge.4
  44.2 2.8 %collective-permute-start.7 = (bf16[2,64,256]{2,1,0:T(8,128)(2,1)S(1)}, bf16[2,64,256]{2,1,0:T(8,128)(2,1)S(1)}, u32[]{:S(2)}, u32[]{:S(2)}) collective-permute-start(bf16[2,64,256]{2,1,0:T(8,128)(2,1)S(1)} %get-tuple-element.49), channel_id=1, source_target_pairs={{0,16},{4,20},{8,24},{12,28},{16,0},{20,4},{24,8},{28,12},{1,17},{... | collective-permute-start | bytes 196616 | tf_op jit(solution)/shard_map/ppermute | solution.py:156
  47.0 2.5 %collective-permute-done.7.got_ref = bf16[2,64,256]{2,1,0:T(8,128)(2,1)S(1)} collective-permute-done((bf16[2,64,256]{2,1,0:T(8,128)(2,1)S(1)}, bf16[2,64,256]{2,1,0:T(8,128)(2,1)S(1)}, u32[]{:S(2)}, u32[]{:S(2)}) %collective-permute-start.7) | collective-permute-done | bytes 65568 | tf_op jit(solution)/shard_map/ppermute | solution.py:156
  49.5 0.6 merge.5
  50.1 1.5 %collective-permute-start.8 = (bf16[1,64,256]{2,1,0:T(8,128)(2,1)S(1)}, bf16[1,64,256]{2,1,0:T(8,128)(2,1)S(1)}, u32[]{:S(2)}, u32[]{:S(2)}) collective-permute-start(bf16[1,64,256]{2,1,0:T(8,128)(2,1)S(1)} %get-tuple-element.51), channel_id=1, source_target_pairs={{0,8},{4,12},{8,0},{12,4},{16,24},{20,28},{24,16},{28,20},{1,9},{5... | collective-permute-start | bytes 98312 | tf_op jit(solution)/shard_map/ppermute | solution.py:156
  51.6 2.5 %collective-permute-done.8.refs_1_ = bf16[1,64,256]{2,1,0:T(8,128)(2,1)S(1)} collective-permute-done((bf16[1,64,256]{2,1,0:T(8,128)(2,1)S(1)}, bf16[1,64,256]{2,1,0:T(8,128)(2,1)S(1)}, u32[]{:S(2)}, u32[]{:S(2)}) %collective-permute-start.8) | collective-permute-done | bytes 32800 | tf_op jit(solution)/shard_map/ppermute | solution.py:156
  54.1 0.6 next_block.4.rest_0_
  54.7 0.1 collective-permute-start.11
  54.8 1.5 %collective-permute-start.10 = (bf16[64,256]{1,0:T(8,128)(2,1)S(1)}, bf16[64,256]{1,0:T(8,128)(2,1)S(1)}, u32[]{:S(2)}, u32[]{:S(2)}) collective-permute-start(bf16[64,256]{1,0:T(8,128)(2,1)S(1)} %next_block.4.rest_0_), channel_id=1, source_target_pairs={{2,0},{3,1},{0,2},{1,3},{6,4},{7,5},{4,6},{5,7},{10,8},{11,9},{8,1... | collective-permute-start | bytes 98312 | tf_op jit(solution)/shard_map/ppermute | solution.py:41
  56.3 0.4 collective-permute-start.9
  56.7 1.3 %prep.4 = (bf16[512,128]{1,0:T(8,128)(2,1)S(1)}, f32[8,512]{1,0:T(8,128)S(1)}, bf16[512,100]{1,0:T(8,128)(2,1)S(1)}) custom-call(s32[3,3,1,256]{3,2,1,0:T(1,128)S(1)} %copy-done.10, s32[3,3,1,256]{3,2,1,0:T(1,128)S(1)} %collective-permute-done.refs_1_, s32[3,3,1,256]{3,2,1,0:T(1,128)S(1)} %collective-permute-done.1.refs_2_, ...), custom_call_target="tpu_custom_call" | custom-call | flops 100000000 | bytes 1000000 | tf_op jit(solution)/shard_map/prep/pallas_call | solution.py:260
  58.0 0.5 collective-permute-done.11.rest_3_
  58.5 0.3 collective-permute-done.10.rest_2_
  58.8 2.5 %batch.4 = s16[8,64,256]{2,1,0:T(8,128)(2,1)} custom-call(bf16[512,128]{1,0:T(8,128)(2,1)S(1)} %get-tuple-element.43.cols_ref, f32[8,512]{1,0:T(8,128)S(1)} %get-tuple-element.44.row_ref, bf16[512,100]{1,0:T(8,128)(2,1)S(1)} %get-tuple-element.45.enc_ref, bf16[256,256]{1,0:T(8,128)(2,1)S(1)} %copy-done.3, bf16[256,256]{1,0:T(8,128)(2,1)S(1)} %copy-done.4, ...), custom_call_target="tpu_custom_call" | custom-call | flops 100000000 | bytes 4000000 | tf_op jit(solution)/shard_map/batch/pallas_call | solution.py:326
  61.3 5.6 %all-to-all-start.2 = ((s16[8,64,256]{2,1,0:T(8,128)(2,1)}), s16[8,64,256]{2,1,0:T(8,128)(2,1)S(1)}, u32[]{:S(2)}, u32[]{:S(2)}) async-start(s16[8,64,256]{2,1,0:T(8,128)(2,1)} %batch.4), calls=%async_computation.2 | async-start | bytes 524288 | tf_op jit(solution)/shard_map/all_to_all | solution.py:488
  67.0 2.0 %collective-permute-start.12 = (bf16[4,64,256]{2,1,0:T(8,128)(2,1)S(1)}, bf16[4,64,256]{2,1,0:T(8,128)(2,1)S(1)}, u32[]{:S(2)}, u32[]{:S(2)}) collective-permute-start(bf16[4,64,256]{2,1,0:T(8,128)(2,1)S(1)} %copy-done.14), channel_id=1, source_target_pairs={{0,4},{4,0},{8,12},{12,8},{16,20},{20,16},{24,28},{28,24},{1,5},{5... | collective-permute-start | bytes 393224 | tf_op jit(solution)/shard_map/ppermute | solution.py:156
  69.0 6.0 %collective-permute-done.12.got_ref = bf16[4,64,256]{2,1,0:T(8,128)(2,1)S(1)} collective-permute-done((bf16[4,64,256]{2,1,0:T(8,128)(2,1)S(1)}, bf16[4,64,256]{2,1,0:T(8,128)(2,1)S(1)}, u32[]{:S(2)}, u32[]{:S(2)}) %collective-permute-start.12) | collective-permute-done | bytes 131104 | tf_op jit(solution)/shard_map/ppermute | solution.py:156
  75.0 0.6 merge.6
  75.7 2.8 %collective-permute-start.13 = (bf16[2,64,256]{2,1,0:T(8,128)(2,1)S(1)}, bf16[2,64,256]{2,1,0:T(8,128)(2,1)S(1)}, u32[]{:S(2)}, u32[]{:S(2)}) collective-permute-start(bf16[2,64,256]{2,1,0:T(8,128)(2,1)S(1)} %get-tuple-element.60), channel_id=1, source_target_pairs={{0,16},{4,20},{8,24},{12,28},{16,0},{20,4},{24,8},{28,12},{1,17},{... | collective-permute-start | bytes 196616 | tf_op jit(solution)/shard_map/ppermute | solution.py:156
  78.4 2.6 %collective-permute-done.13.got_ref = bf16[2,64,256]{2,1,0:T(8,128)(2,1)S(1)} collective-permute-done((bf16[2,64,256]{2,1,0:T(8,128)(2,1)S(1)}, bf16[2,64,256]{2,1,0:T(8,128)(2,1)S(1)}, u32[]{:S(2)}, u32[]{:S(2)}) %collective-permute-start.13) | collective-permute-done | bytes 65568 | tf_op jit(solution)/shard_map/ppermute | solution.py:156
  81.0 0.6 merge.7
  81.6 1.6 %collective-permute-start.14 = (bf16[1,64,256]{2,1,0:T(8,128)(2,1)S(1)}, bf16[1,64,256]{2,1,0:T(8,128)(2,1)S(1)}, u32[]{:S(2)}, u32[]{:S(2)}) collective-permute-start(bf16[1,64,256]{2,1,0:T(8,128)(2,1)S(1)} %get-tuple-element.62), channel_id=1, source_target_pairs={{0,8},{4,12},{8,0},{12,4},{16,24},{20,28},{24,16},{28,20},{1,9},{5... | collective-permute-start | bytes 98312 | tf_op jit(solution)/shard_map/ppermute | solution.py:156
  83.2 2.4 %collective-permute-done.14.refs_1_ = bf16[1,64,256]{2,1,0:T(8,128)(2,1)S(1)} collective-permute-done((bf16[1,64,256]{2,1,0:T(8,128)(2,1)S(1)}, bf16[1,64,256]{2,1,0:T(8,128)(2,1)S(1)}, u32[]{:S(2)}, u32[]{:S(2)}) %collective-permute-start.14) | collective-permute-done | bytes 32800 | tf_op jit(solution)/shard_map/ppermute | solution.py:156
  85.6 0.0 all-to-all-done.2.rest_1_.refs_3_
  85.6 0.6 next_block.5.rest_0_
  86.2 0.1 collective-permute-start.17
  86.3 1.2 %collective-permute-start.16 = (bf16[64,256]{1,0:T(8,128)(2,1)S(1)}, bf16[64,256]{1,0:T(8,128)(2,1)S(1)}, u32[]{:S(2)}, u32[]{:S(2)}) collective-permute-start(bf16[64,256]{1,0:T(8,128)(2,1)S(1)} %next_block.5.rest_0_), channel_id=1, source_target_pairs={{2,0},{3,1},{0,2},{1,3},{6,4},{7,5},{4,6},{5,7},{10,8},{11,9},{8,1... | collective-permute-start | bytes 98312 | tf_op jit(solution)/shard_map/ppermute | solution.py:41
  87.5 0.7 collective-permute-start.15
  88.2 1.3 %prep.5 = (bf16[512,128]{1,0:T(8,128)(2,1)S(1)}, f32[8,512]{1,0:T(8,128)S(1)}, bf16[512,100]{1,0:T(8,128)(2,1)S(1)}) custom-call(s32[3,3,1,256]{3,2,1,0:T(1,128)S(1)} %copy-done.10, s32[3,3,1,256]{3,2,1,0:T(1,128)S(1)} %collective-permute-done.refs_1_, s32[3,3,1,256]{3,2,1,0:T(1,128)S(1)} %collective-permute-done.1.refs_2_, ...), custom_call_target="tpu_custom_call" | custom-call | flops 100000000 | bytes 1000000 | tf_op jit(solution)/shard_map/prep/pallas_call | solution.py:260
  89.5 0.2 collective-permute-done.17.rest_3_
  89.7 0.8 collective-permute-done.16.rest_2_
  90.4 0.0 collective-permute-done.15.rest_1_
  90.4 2.5 %batch.5 = s16[8,64,256]{2,1,0:T(8,128)(2,1)} custom-call(bf16[512,128]{1,0:T(8,128)(2,1)S(1)} %get-tuple-element.54.cols_ref, f32[8,512]{1,0:T(8,128)S(1)} %get-tuple-element.55.row_ref, bf16[512,100]{1,0:T(8,128)(2,1)S(1)} %get-tuple-element.56.enc_ref, bf16[256,256]{1,0:T(8,128)(2,1)S(1)} %copy-done.3, bf16[256,256]{1,0:T(8,128)(2,1)S(1)} %copy-done.4, ...), custom_call_target="tpu_custom_call" | custom-call | flops 100000000 | bytes 4000000 | tf_op jit(solution)/shard_map/batch/pallas_call | solution.py:326
  92.9 5.6 %all-to-all-start.3 = ((s16[8,64,256]{2,1,0:T(8,128)(2,1)}), s16[8,64,256]{2,1,0:T(8,128)(2,1)S(1)}, u32[]{:S(2)}, u32[]{:S(2)}) async-start(s16[8,64,256]{2,1,0:T(8,128)(2,1)} %batch.5), calls=%async_computation.3 | async-start | bytes 524288 | tf_op jit(solution)/shard_map/all_to_all | solution.py:488
  98.6 2.4 %settle.1 = (f32[16,64,256]{2,1,0:T(8,128)}, f32[8,64,256]{2,1,0:T(8,128)S(1)}) custom-call(s32[3,1,8]{2,1,0:T(1,128)S(1)} %bitcast.19, f32[16,64,256]{2,1,0:T(8,128)S(1)} %bitcast.10, s16[8,72,256]{2,1,0:T(8,128)(2,1)S(1)} %all-to-all-done.1.refs_2_.rest_0_.counts, s16[8,64,256]{2,1,0:T(8,128)(2,1)S(1)} %all-to-all-done.2.rest_1_.refs_3_), custom_call_target="tpu_custom_call" | custom-call | flops 20000000 | bytes 3000000 | tf_op jit(solution)/shard_map/settle/pallas_call | solution.py:437
  101.0 6.8 %all-to-all-done.3.delta = s16[8,64,256]{2,1,0:T(8,128)(2,1)S(1)} async-done(((s16[8,64,256]{2,1,0:T(8,128)(2,1)}), s16[8,64,256]{2,1,0:T(8,128)(2,1)S(1)}, u32[]{:S(2)}, u32[]{:S(2)}) %all-to-all-start.3) | async-done | bytes 262176 | tf_op jit(solution)/shard_map/all_to_all | solution.py:488
  107.8 0.8 finish.1
  (28 shorter events, 0.1 us)
Async XLA Ops:
  3.3 16.4 %copy-start.6 = (s32[8,3,1]{0,2,1:T(1,128)S(1)}, s32[8,3,1]{0,2,1:T(1,128)}, u32[]{:S(2)}) copy-start(s32[8,3,1]{0,2,1:T(1,128)} %param.18) | copy-start | bytes 292
  3.3 19.0 %copy-start.10 = (s32[3,3,1,256]{3,2,1,0:T(1,128)S(1)}, s32[3,3,1,256]{3,2,1,0:T(1,128)}, u32[]{:S(2)}) copy-start(s32[3,3,1,256]{3,2,1,0:T(1,128)} %get-tuple-element.34.refs_0_) | copy-start | bytes 27652
  3.3 22.3 %copy-start.13 = (f32[768]{0:T(1024)S(1)}, f32[768]{0:T(1024)}, u32[]{:S(2)}) copy-start(f32[768]{0:T(1024)} %param.27) | copy-start | bytes 9220
  3.3 23.7 %copy-start.11 = (f32[1,100]{1,0:T(1,128)S(1)}, f32[1,100]{1,0:T(1,128)}, u32[]{:S(2)}) copy-start(f32[1,100]{1,0:T(1,128)} %get-tuple-element.35.refs_4_) | copy-start | bytes 1204
  3.3 23.7 %copy-start.12 = (f32[1,100]{1,0:T(1,128)S(1)}, f32[1,100]{1,0:T(1,128)}, u32[]{:S(2)}) copy-start(f32[1,100]{1,0:T(1,128)} %get-tuple-element.36.refs_5_) | copy-start | bytes 1204
  3.3 25.5 %copy-start.2 = (bf16[256,768]{1,0:T(8,128)(2,1)S(1)}, bf16[256,768]{1,0:T(8,128)(2,1)}, u32[]{:S(2)}) copy-start(bf16[256,768]{1,0:T(8,128)(2,1)} %wh_ref.5) | copy-start | bytes 1179652
  3.4 25.5 %copy-start.5 = (bf16[100,256]{1,0:T(8,128)(2,1)S(1)}, bf16[100,256]{1,0:T(8,128)(2,1)}, u32[]{:S(2)}) copy-start(bf16[100,256]{1,0:T(8,128)(2,1)} %wt_ref.5) | copy-start | bytes 153604
  19.7 9.1 %copy-start.1 = (bf16[256,768]{1,0:T(8,128)(2,1)S(1)}, bf16[256,768]{1,0:T(8,128)(2,1)}, u32[]{:S(2)}) copy-start(bf16[256,768]{1,0:T(8,128)(2,1)} %wi_ref.5) | copy-start | bytes 1179652
  20.3 8.5 %collective-permute-start.5 = (bf16[64,256]{1,0:T(8,128)(2,1)S(1)}, bf16[64,256]{1,0:T(8,128)(2,1)S(1)}, u32[]{:S(2)}, u32[]{:S(2)}) collective-permute-start(bf16[64,256]{1,0:T(8,128)(2,1)S(1)} %next_block.3.rest_1_), channel_id=1, source_target_pairs={{3,0},{2,1},{1,2},{0,3},{7,4},{6,5},{5,6},{4,7},{11,8},{10,9},{9,1... | collective-permute-start | bytes 98312 | tf_op jit(solution)/shard_map/ppermute | solution.py:41
  20.4 8.4 %collective-permute-start.4 = (bf16[64,256]{1,0:T(8,128)(2,1)S(1)}, bf16[64,256]{1,0:T(8,128)(2,1)S(1)}, u32[]{:S(2)}, u32[]{:S(2)}) collective-permute-start(bf16[64,256]{1,0:T(8,128)(2,1)S(1)} %next_block.3.rest_1_), channel_id=1, source_target_pairs={{2,0},{3,1},{0,2},{1,3},{6,4},{7,5},{4,6},{5,7},{10,8},{11,9},{8,1... | collective-permute-start | bytes 98312 | tf_op jit(solution)/shard_map/ppermute | solution.py:41
  22.0 6.8 %collective-permute-start.3 = (bf16[64,256]{1,0:T(8,128)(2,1)S(1)}, bf16[64,256]{1,0:T(8,128)(2,1)S(1)}, u32[]{:S(2)}, u32[]{:S(2)}) collective-permute-start(bf16[64,256]{1,0:T(8,128)(2,1)S(1)} %next_block.3.rest_1_), channel_id=1, source_target_pairs={{1,0},{0,1},{3,2},{2,3},{5,4},{4,5},{7,6},{6,7},{9,8},{8,9},{11,10... | collective-permute-start | bytes 98312 | tf_op jit(solution)/shard_map/ppermute | solution.py:41
  22.3 3.1 %collective-permute-start.2 = (s32[3,3,1,256]{3,2,1,0:T(1,128)S(1)}, s32[3,3,1,256]{3,2,1,0:T(1,128)S(1)}, u32[]{:S(2)}, u32[]{:S(2)}) collective-permute-start(s32[3,3,1,256]{3,2,1,0:T(1,128)S(1)} %copy-done.10), channel_id=1, source_target_pairs={{3,0},{2,1},{1,2},{0,3},{7,4},{6,5},{5,6},{4,7},{11,8},{10,9},{9,1... | collective-permute-start | bytes 27656 | tf_op jit(solution)/shard_map/ppermute | solution.py:41
  23.4 3.7 %collective-permute-start.1 = (s32[3,3,1,256]{3,2,1,0:T(1,128)S(1)}, s32[3,3,1,256]{3,2,1,0:T(1,128)S(1)}, u32[]{:S(2)}, u32[]{:S(2)}) collective-permute-start(s32[3,3,1,256]{3,2,1,0:T(1,128)S(1)} %copy-done.10), channel_id=1, source_target_pairs={{2,0},{3,1},{0,2},{1,3},{6,4},{7,5},{4,6},{5,7},{10,8},{11,9},{8,1... | collective-permute-start | bytes 27656 | tf_op jit(solution)/shard_map/ppermute | solution.py:41
  25.3 1.7 %collective-permute-start = (s32[3,3,1,256]{3,2,1,0:T(1,128)S(1)}, s32[3,3,1,256]{3,2,1,0:T(1,128)S(1)}, u32[]{:S(2)}, u32[]{:S(2)}) collective-permute-start(s32[3,3,1,256]{3,2,1,0:T(1,128)S(1)} %copy-done.10), channel_id=1, source_target_pairs={{1,0},{0,1},{3,2},{2,3},{5,4},{4,5},{7,6},{6,7},{9,8},{8,9},{11,10... | collective-permute-start | bytes 27656 | tf_op jit(solution)/shard_map/ppermute | solution.py:41
  27.0 1.8 %copy-start.3 = (bf16[256,256]{1,0:T(8,128)(2,1)S(1)}, bf16[256,256]{1,0:T(8,128)(2,1)}, u32[]{:S(2)}) copy-start(bf16[256,256]{1,0:T(8,128)(2,1)} %ws_ref.5) | copy-start | bytes 393220
  27.1 1.8 %copy-start.4 = (bf16[256,256]{1,0:T(8,128)(2,1)S(1)}, bf16[256,256]{1,0:T(8,128)(2,1)}, u32[]{:S(2)}) copy-start(bf16[256,256]{1,0:T(8,128)(2,1)} %wo_ref.5) | copy-start | bytes 393220
  28.8 0.7 copy-start.9
  32.0 3.7 %copy-start.15 = (bf16[4,64,256]{2,1,0:T(8,128)(2,1)S(1)}, bf16[4,64,256]{2,1,0:T(8,128)(2,1)}, u32[]{:S(2)}) copy-start(bf16[4,64,256]{2,1,0:T(8,128)(2,1)} %get-tuple-element.47) | copy-start | bytes 393220
  32.0 11.5 %copy-start.8 = (bf16[4,64,256]{2,1,0:T(8,128)(2,1)S(1)}, bf16[4,64,256]{2,1,0:T(8,128)(2,1)}, u32[]{:S(2)}) copy-start(bf16[4,64,256]{2,1,0:T(8,128)(2,1)} %get-tuple-element.46.keep_in) | copy-start | bytes 393220
  32.0 22.1 %all-to-all-start.1 = ((s16[8,72,256]{2,1,0:T(8,128)(2,1)}), s16[8,72,256]{2,1,0:T(8,128)(2,1)S(1)}, u32[]{:S(2)}, u32[]{:S(2)}) async-start(s16[8,72,256]{2,1,0:T(8,128)(2,1)} %batch.3), calls=%async_computation.1 | async-start | bytes 589824 | tf_op jit(solution)/shard_map/all_to_all | solution.py:488
  35.7 7.8 %collective-permute-start.6 = (bf16[4,64,256]{2,1,0:T(8,128)(2,1)S(1)}, bf16[4,64,256]{2,1,0:T(8,128)(2,1)S(1)}, u32[]{:S(2)}, u32[]{:S(2)}) collective-permute-start(bf16[4,64,256]{2,1,0:T(8,128)(2,1)S(1)} %copy-done.15), channel_id=1, source_target_pairs={{0,4},{4,0},{8,12},{12,8},{16,20},{20,16},{24,28},{28,24},{1,5},{5... | collective-permute-start | bytes 393224 | tf_op jit(solution)/shard_map/ppermute | solution.py:156
  44.2 5.4 %collective-permute-start.7 = (bf16[2,64,256]{2,1,0:T(8,128)(2,1)S(1)}, bf16[2,64,256]{2,1,0:T(8,128)(2,1)S(1)}, u32[]{:S(2)}, u32[]{:S(2)}) collective-permute-start(bf16[2,64,256]{2,1,0:T(8,128)(2,1)S(1)} %get-tuple-element.49), channel_id=1, source_target_pairs={{0,16},{4,20},{8,24},{12,28},{16,0},{20,4},{24,8},{28,12},{1,17},{... | collective-permute-start | bytes 196616 | tf_op jit(solution)/shard_map/ppermute | solution.py:156
  50.1 4.0 %collective-permute-start.8 = (bf16[1,64,256]{2,1,0:T(8,128)(2,1)S(1)}, bf16[1,64,256]{2,1,0:T(8,128)(2,1)S(1)}, u32[]{:S(2)}, u32[]{:S(2)}) collective-permute-start(bf16[1,64,256]{2,1,0:T(8,128)(2,1)S(1)} %get-tuple-element.51), channel_id=1, source_target_pairs={{0,8},{4,12},{8,0},{12,4},{16,24},{20,28},{24,16},{28,20},{1,9},{5... | collective-permute-start | bytes 98312 | tf_op jit(solution)/shard_map/ppermute | solution.py:156
  54.7 3.8 %collective-permute-start.11 = (bf16[64,256]{1,0:T(8,128)(2,1)S(1)}, bf16[64,256]{1,0:T(8,128)(2,1)S(1)}, u32[]{:S(2)}, u32[]{:S(2)}) collective-permute-start(bf16[64,256]{1,0:T(8,128)(2,1)S(1)} %next_block.4.rest_0_), channel_id=1, source_target_pairs={{3,0},{2,1},{1,2},{0,3},{7,4},{6,5},{5,6},{4,7},{11,8},{10,9},{9,1... | collective-permute-start | bytes 98312 | tf_op jit(solution)/shard_map/ppermute | solution.py:41
  54.8 4.0 %collective-permute-start.10 = (bf16[64,256]{1,0:T(8,128)(2,1)S(1)}, bf16[64,256]{1,0:T(8,128)(2,1)S(1)}, u32[]{:S(2)}, u32[]{:S(2)}) collective-permute-start(bf16[64,256]{1,0:T(8,128)(2,1)S(1)} %next_block.4.rest_0_), channel_id=1, source_target_pairs={{2,0},{3,1},{0,2},{1,3},{6,4},{7,5},{4,6},{5,7},{10,8},{11,9},{8,1... | collective-permute-start | bytes 98312 | tf_op jit(solution)/shard_map/ppermute | solution.py:41
  56.3 2.5 %collective-permute-start.9 = (bf16[64,256]{1,0:T(8,128)(2,1)S(1)}, bf16[64,256]{1,0:T(8,128)(2,1)S(1)}, u32[]{:S(2)}, u32[]{:S(2)}) collective-permute-start(bf16[64,256]{1,0:T(8,128)(2,1)S(1)} %next_block.4.rest_0_), channel_id=1, source_target_pairs={{1,0},{0,1},{3,2},{2,3},{5,4},{4,5},{7,6},{6,7},{9,8},{8,9},{11,10... | collective-permute-start | bytes 98312 | tf_op jit(solution)/shard_map/ppermute | solution.py:41
  61.3 5.6 %copy-start.14 = (bf16[4,64,256]{2,1,0:T(8,128)(2,1)S(1)}, bf16[4,64,256]{2,1,0:T(8,128)(2,1)}, u32[]{:S(2)}) copy-start(bf16[4,64,256]{2,1,0:T(8,128)(2,1)} %get-tuple-element.58) | copy-start | bytes 393220
  61.3 13.7 %copy-start.7 = (bf16[4,64,256]{2,1,0:T(8,128)(2,1)S(1)}, bf16[4,64,256]{2,1,0:T(8,128)(2,1)}, u32[]{:S(2)}) copy-start(bf16[4,64,256]{2,1,0:T(8,128)(2,1)} %get-tuple-element.57.keep_in) | copy-start | bytes 393220
  61.3 24.3 %all-to-all-start.2 = ((s16[8,64,256]{2,1,0:T(8,128)(2,1)}), s16[8,64,256]{2,1,0:T(8,128)(2,1)S(1)}, u32[]{:S(2)}, u32[]{:S(2)}) async-start(s16[8,64,256]{2,1,0:T(8,128)(2,1)} %batch.4), calls=%async_computation.2 | async-start | bytes 524288 | tf_op jit(solution)/shard_map/all_to_all | solution.py:488
  67.0 8.1 %collective-permute-start.12 = (bf16[4,64,256]{2,1,0:T(8,128)(2,1)S(1)}, bf16[4,64,256]{2,1,0:T(8,128)(2,1)S(1)}, u32[]{:S(2)}, u32[]{:S(2)}) collective-permute-start(bf16[4,64,256]{2,1,0:T(8,128)(2,1)S(1)} %copy-done.14), channel_id=1, source_target_pairs={{0,4},{4,0},{8,12},{12,8},{16,20},{20,16},{24,28},{28,24},{1,5},{5... | collective-permute-start | bytes 393224 | tf_op jit(solution)/shard_map/ppermute | solution.py:156
  75.7 5.3 %collective-permute-start.13 = (bf16[2,64,256]{2,1,0:T(8,128)(2,1)S(1)}, bf16[2,64,256]{2,1,0:T(8,128)(2,1)S(1)}, u32[]{:S(2)}, u32[]{:S(2)}) collective-permute-start(bf16[2,64,256]{2,1,0:T(8,128)(2,1)S(1)} %get-tuple-element.60), channel_id=1, source_target_pairs={{0,16},{4,20},{8,24},{12,28},{16,0},{20,4},{24,8},{28,12},{1,17},{... | collective-permute-start | bytes 196616 | tf_op jit(solution)/shard_map/ppermute | solution.py:156
  81.6 4.0 %collective-permute-start.14 = (bf16[1,64,256]{2,1,0:T(8,128)(2,1)S(1)}, bf16[1,64,256]{2,1,0:T(8,128)(2,1)S(1)}, u32[]{:S(2)}, u32[]{:S(2)}) collective-permute-start(bf16[1,64,256]{2,1,0:T(8,128)(2,1)S(1)} %get-tuple-element.62), channel_id=1, source_target_pairs={{0,8},{4,12},{8,0},{12,4},{16,24},{20,28},{24,16},{28,20},{1,9},{5... | collective-permute-start | bytes 98312 | tf_op jit(solution)/shard_map/ppermute | solution.py:156
  86.2 3.4 %collective-permute-start.17 = (bf16[64,256]{1,0:T(8,128)(2,1)S(1)}, bf16[64,256]{1,0:T(8,128)(2,1)S(1)}, u32[]{:S(2)}, u32[]{:S(2)}) collective-permute-start(bf16[64,256]{1,0:T(8,128)(2,1)S(1)} %next_block.5.rest_0_), channel_id=1, source_target_pairs={{3,0},{2,1},{1,2},{0,3},{7,4},{6,5},{5,6},{4,7},{11,8},{10,9},{9,1... | collective-permute-start | bytes 98312 | tf_op jit(solution)/shard_map/ppermute | solution.py:41
  86.3 4.1 %collective-permute-start.16 = (bf16[64,256]{1,0:T(8,128)(2,1)S(1)}, bf16[64,256]{1,0:T(8,128)(2,1)S(1)}, u32[]{:S(2)}, u32[]{:S(2)}) collective-permute-start(bf16[64,256]{1,0:T(8,128)(2,1)S(1)} %next_block.5.rest_0_), channel_id=1, source_target_pairs={{2,0},{3,1},{0,2},{1,3},{6,4},{7,5},{4,6},{5,7},{10,8},{11,9},{8,1... | collective-permute-start | bytes 98312 | tf_op jit(solution)/shard_map/ppermute | solution.py:41
  87.5 2.9 %collective-permute-start.15 = (bf16[64,256]{1,0:T(8,128)(2,1)S(1)}, bf16[64,256]{1,0:T(8,128)(2,1)S(1)}, u32[]{:S(2)}, u32[]{:S(2)}) collective-permute-start(bf16[64,256]{1,0:T(8,128)(2,1)S(1)} %next_block.5.rest_0_), channel_id=1, source_target_pairs={{1,0},{0,1},{3,2},{2,3},{5,4},{4,5},{7,6},{6,7},{9,8},{8,9},{11,10... | collective-permute-start | bytes 98312 | tf_op jit(solution)/shard_map/ppermute | solution.py:41
  90.4 8.1 %copy-start = (f32[1024,256]{1,0:T(8,128)S(1)}, f32[1024,256]{1,0:T(8,128)}, u32[]{:S(2)}) copy-start(f32[1024,256]{1,0:T(8,128)} %param.14) | copy-start | bytes 3145732
  92.9 14.8 %all-to-all-start.3 = ((s16[8,64,256]{2,1,0:T(8,128)(2,1)}), s16[8,64,256]{2,1,0:T(8,128)(2,1)S(1)}, u32[]{:S(2)}, u32[]{:S(2)}) async-start(s16[8,64,256]{2,1,0:T(8,128)(2,1)} %batch.5), calls=%async_computation.3 | async-start | bytes 524288 | tf_op jit(solution)/shard_map/all_to_all | solution.py:488
where the time goes:
time: 109 us
  starting transfers between devices  35.6 us (33%)
  waiting for transfers between devices  33 us (30%)
  Pallas kernels  22.6 us (21%)
  blocking collectives  16.4 us (15%)
    ppermute x6, waiting for transfers between devices, cube(): got = lax.ppermute(send, 'rep', [(i, i ^ 1 << bit) for i in range(groups)])  21.8 us
    all_to_all x1, blocking collectives, exchange(): return lax.all_to_all(x, 'rep', split_axis=0, concat_axis=0, tiled=True)  16.4 us
    all_to_all x3, starting transfers between devices, exchange(): return lax.all_to_all(x, 'rep', split_axis=0, concat_axis=0, tiled=True)  15 us
    ppermute x6, starting transfers between devices, cube(): got = lax.ppermute(send, 'rep', [(i, i ^ 1 << bit) for i in range(groups)])  12.7 us
    ppermute x12, starting transfers between devices, share(): lax.ppermute(block, 'shard', [(partner(i, k, n), i) for i in range(n)])  7.86 us
    pallas_call x3, Pallas kernels, batch_step(): pl.pallas_call(functools.partial(batch_kernel, len(blocks), len(counts)),...  7.46 us
    all_to_all x3, waiting for transfers between devices, exchange(): return lax.all_to_all(x, 'rep', split_axis=0, concat_axis=0, tiled=True)  6.77 us
    ppermute x12, waiting for transfers between devices, share(): lax.ppermute(block, 'shard', [(partner(i, k, n), i) for i in range(n)])  4.47 us
  transfers between devices with their start and end apart: 21, of which 13 were waited for; matrix products, arithmetic and copies ran while one was open for 0% of the time, Pallas kernels for 9%

commit v1 on v0

--- a/solution.py
+++ b/solution.py
@@ -17,7 +17,6 @@
 ALL_ROOM = pltpu.CompilerParams(vmem_limit_bytes=60 << 20)
 ROOM = pltpu.CompilerParams(vmem_limit_bytes=12 << 20)
 
-
 NT = (((1,), (1,)), ((), ()))
 
 
@@ -55,13 +54,58 @@
     return steps
 
 
-def pick_kernel(batches, count, n_lists, ids_ref, mem_ref, *refs):
+def plan_rows(batches, groups):
+    rows, steps = {}, cube_lists(groups)
+    for g in range(groups):
+        rows["owner", g] = len(rows)
+    for b in range(1, batches):
+        for step, (_, kept) in enumerate(steps):
+            for j in kept if step < len(steps) - 1 else [0]:
+                rows["other", b, step, j] = len(rows)
+    for g in range(groups):
+        rows["block", g] = len(rows)
+        rows["fresh", g] = len(rows)
+    for b in range(1, batches):
+        for e in range(b):
+            while len(rows) % 8:
+                rows["pad", len(rows)] = len(rows)
+            for g in range(groups):
+                rows["hit", b, e, g] = len(rows)
+    return rows
+
+
+def write_plan(ids_ref, count, batches, groups, plan_ref):
+    me = lax.axis_index("rep")
+    steps = cube_lists(groups)
+    mine = [ids_ref[b, 0, me] for b in range(batches)]
+    for key, r in plan_rows(batches, groups).items():
+        if key[0] == "owner":
+            on = lax.div(mine[0], count) == key[1]
+        elif key[0] == "other":
+            _, b, step, j = key
+            owner = lax.div(ids_ref[b, 0, me ^ j], count)
+            on = (lax.shift_right_logical(owner ^ me, steps[step][0]) & 1) == 1
+        elif key[0] == "block":
+            on = ids_ref[batches - 1, 0, key[1]]
+        elif key[0] == "fresh":
+            on = is_fresh(ids_ref, batches - 1, key[1], count, me)[1]
+        elif key[0] == "hit":
+            _, b, e, g = key
+            on = ids_ref[e, 0, g] == mine[b]
+        else:
+            continue
+        plan_ref[r : r + 1, :] = jnp.full((1, LANES), on.astype(jnp.float32))
+
+
+def flag(plan_ref, row, width):
+    return jnp.concatenate([plan_ref[row : row + 1, :]] * (width // LANES), 1)
+
+
+def pick_kernel(batches, count, n_lists, places, ids_ref, mem_ref, *refs):
     lists, refs = refs[:n_lists], refs[n_lists:]
-    n_small = (len(refs) - 2 * batches - 3) // 2
-    small, refs = refs[:n_small], refs[n_small:]
-    first_ref, idx_ref, refs = refs[0], refs[1], refs[2:]
-    halves, small_out, refs = refs[: 2 * batches - 2], refs[2 * batches - 2 : 2 * batches - 2 + n_small], refs[-3:]
-    bufs, sems, list_sems = refs
+    small, refs = refs[: len(places)], refs[len(places) :]
+    first_ref, idx_ref, small_ref, plan_ref, *halves, bufs, sems, list_sems = refs[: 4 + 2 * batches - 2 + 3]
+    parts = refs[4 + 2 * batches - 2 + 3 :]
     groups = ids_ref.shape[2]
     bit, kept = cube_lists(groups)[0]
     me = lax.axis_index("rep")
@@ -75,87 +119,84 @@
         cp = pltpu.make_async_copy(mem_ref.at[lax.rem(ids_ref[b, 0, g], count)], bufs.at[k], sems.at[k])
         cp.start()
         copies.append(cp)
-    moves = [(ref, idx_ref.at[k]) for k, ref in enumerate(lists)] + list(zip(small, small_out))
+    moves = [(ref, idx_ref.at[k]) for k, ref in enumerate(lists)] + list(zip(small, parts))
     rest = [pltpu.make_async_copy(src, dst, list_sems.at[k]) for k, (src, dst) in enumerate(moves)]
     for cp in rest:
         cp.start()
+    write_plan(ids_ref, count, batches, groups, plan_ref)
     for k, (_, _, out_ref, at) in enumerate(plan):
         copies[k].wait()
         out_ref[at] = bufs[k].astype(jnp.bfloat16)
     for cp in rest:
         cp.wait()
+    for at, part in zip(places, parts):
+        small_ref[:, at : at + part.shape[1]] = part[...]
 
 
 def pick(ids, mem, lists, small):
     count, rows, width = mem.shape
     batches, _, groups = ids.shape
     half = jax.ShapeDtypeStruct((groups // 2, rows, width), jnp.bfloat16)
-    first, idx, *out = pl.pallas_call(
-        functools.partial(pick_kernel, batches, count, len(lists)),
+    places, size = [], 0
+    for x in small:
+        places.append(size)
+        size += pl.cdiv(x.shape[1], LANES) * LANES
+    n_plan = pl.cdiv(len(plan_rows(batches, groups)), 8) * 8
+    first, idx, small_out, plan, *out = pl.pallas_call(
+        functools.partial(pick_kernel, batches, count, len(lists), places),
         out_shape=[
             jax.ShapeDtypeStruct((groups, rows, width), jnp.bfloat16),
             jax.ShapeDtypeStruct((len(lists), *lists[0].shape), jnp.int32),
+            jax.ShapeDtypeStruct((1, size), jnp.float32),
+            jax.ShapeDtypeStruct((n_plan, LANES), jnp.float32),
         ]
-        + [half] * (2 * batches - 2)
-        + [jax.ShapeDtypeStruct(x.shape, x.dtype) for x in small],
+        + [half] * (2 * batches - 2),
         in_specs=[SMEM] + [HBM] * (1 + len(lists) + len(small)),
-        out_specs=[VMEM] * (2 + 2 * batches - 2 + len(small)),
+        out_specs=[VMEM] * (4 + 2 * batches - 2),
         scratch_shapes=[
             pltpu.VMEM((batches * groups, rows, width), mem.dtype),
             pltpu.SemaphoreType.DMA((batches * groups,)),
             pltpu.SemaphoreType.DMA((len(lists) + len(small),)),
-        ],
+        ]
+        + [pltpu.VMEM(x.shape, x.dtype) for x in small],
         compiler_params=ALL_ROOM,
         cost_estimate=pl.CostEstimate(flops=20_000_000, bytes_accessed=1_000_000, transcendentals=0),
         name="pick",
     )(ids, mem, *lists, *small)
     halves = [out[2 * b : 2 * b + 2] for b in range(batches - 1)]
-    return first, idx, halves, out[2 * batches - 2 :]
-
-
-def from_partner(ids_ref, b, count, j, bit, me):
-    owner = lax.div(ids_ref[b, 0, me ^ j], count)
-    return (lax.shift_right_logical(owner ^ me, bit) & 1) == 1
-
-
-def merge_kernel(b, step, count, ids_ref, keep_in, got_ref, keep_ref, send_ref):
-    steps = cube_lists(ids_ref.shape[2])
-    me = lax.axis_index("rep")
-    (bit, kept), (_, after) = steps[step], steps[step + 1]
+    return first, idx, small_out, plan, halves
+
+
+def merge_kernel(b, step, groups, rows, plan_ref, keep_in, got_ref, keep_ref, send_ref):
+    steps = cube_lists(groups)
+    kept, (next_bit, after) = steps[step][1], steps[step + 1]
     for i, j in enumerate(kept):
         out_ref = keep_ref if j in after else send_ref
-        k = after.index(j if j in after else j ^ (1 << steps[step + 1][0]))
-        other = from_partner(ids_ref, b, count, j, bit, me)
-
-        @pl.when(other)
-        def _():
-            out_ref[k] = got_ref[i]
-
-        @pl.when(jnp.logical_not(other))
-        def _():
-            out_ref[k] = keep_in[i]
-
-
-def merge(b, step, ids, count, keep, got):
-    half, rows, width = keep.shape
+        k = after.index(j if j in after else j ^ (1 << next_bit))
+        other = flag(plan_ref, rows["other", b, step, j], keep_in.shape[2]) > 0.5
+        chosen = jnp.where(other, got_ref[i].astype(jnp.float32), keep_in[i].astype(jnp.float32))
+        out_ref[k] = chosen.astype(jnp.bfloat16)
+
+
+def merge(b, step, groups, rows, plan, keep, got):
+    half, height, width = keep.shape
     return pl.pallas_call(
-        functools.partial(merge_kernel, b, step, count),
-        out_shape=[jax.ShapeDtypeStruct((half // 2, rows, width), keep.dtype)] * 2,
-        in_specs=[SMEM, VMEM, VMEM],
+        functools.partial(merge_kernel, b, step, groups, rows),
+        out_shape=[jax.ShapeDtypeStruct((half // 2, height, width), keep.dtype)] * 2,
+        in_specs=[VMEM] * 3,
         out_specs=[VMEM] * 2,
         compiler_params=ROOM,
         cost_estimate=pl.CostEstimate(flops=1_000_000, bytes_accessed=300_000, transcendentals=0),
         name="merge",
-    )(ids, keep, got)
-
-
-def cube(b, ids, keep, send, count):
-    groups = ids.shape[2]
+    )(plan, keep, got)
+
+
+def cube(b, groups, rows, plan, keep, send):
     bits = bit_order(groups)
     for step, bit in enumerate(bits):
         got = lax.ppermute(send, "rep", [(i, i ^ 1 << bit) for i in range(groups)])
         if step < len(bits) - 1:
-            keep, send = merge(b, step, ids, count, keep, got)
+            keep, send = merge(b, step, groups, rows, plan, keep, got)
     return keep, got
 
 
@@ -186,7 +227,7 @@
 
 def prep_kernel(b, shards, *refs):
     idx, refs = refs[:shards], refs[shards:]
-    freq_ref, phase_ref, cols_ref, row_ref, enc_ref, *tally_ref, pack = refs
+    small_ref, cols_ref, row_ref, enc_ref, *tally_ref, pack = refs
     me = lax.axis_index("shard")
     entries = cols_ref.shape[0]
     lines = pack.shape[0]
@@ -230,7 +271,8 @@
     ).astype(jnp.float32).astype(jnp.bfloat16)
     row_ref[...] = bdot(eye, wide, NT)
     time = cols[:, 3:4] + 256.0 * cols[:, 4:5]
-    enc_ref[...] = cosine(time * freq_ref[...] + phase_ref[...]).astype(jnp.bfloat16)
+    width = enc_ref.shape[1]
+    enc_ref[...] = cosine(time * small_ref[:, :width] + small_ref[:, LANES : LANES + width]).astype(jnp.bfloat16)
     if tally_ref:
         width = tally_ref[0].shape[1]
         line = lax.broadcasted_iota(jnp.int32, (COUNT_ROWS, LANES), 0)
@@ -248,34 +290,34 @@
         tally_ref[0][...] = tally.astype(jnp.int32).astype(jnp.int16)
 
 
-def prep(b, idx, freq, phase, entries, width):
+def prep(b, idx, small, encoded, entries, width):
     lines = 2 * len(idx) * idx[0].shape[3] // LANES
     out = [
         jax.ShapeDtypeStruct((entries, LANES), jnp.bfloat16),
         jax.ShapeDtypeStruct((8, entries), jnp.float32),
-        jax.ShapeDtypeStruct((entries, freq.shape[1]), jnp.bfloat16),
+        jax.ShapeDtypeStruct((entries, encoded), jnp.bfloat16),
     ]
     if b == 0:
         out.append(jax.ShapeDtypeStruct((COUNT_ROWS, width), jnp.int16))
     return pl.pallas_call(
         functools.partial(prep_kernel, b, len(idx)),
         out_shape=out,
-        in_specs=[VMEM] * (len(idx) + 2),
+        in_specs=[VMEM] * (len(idx) + 1),
         out_specs=[VMEM] * len(out),
         scratch_shapes=[pltpu.VMEM((lines, 8, LANES), jnp.float32)],
         compiler_params=ROOM,
         cost_estimate=pl.CostEstimate(flops=100_000_000, bytes_accessed=1_000_000, transcendentals=0),
         name="prep",
-    )(*idx, freq, phase)
-
-
-def batch_kernel(n, tallies, cols_ref, row_ref, enc_ref, ws_ref, wo_ref, wt_ref, bm_ref, wi_ref, wh_ref, bg_ref, *rest):
+    )(*idx, small)
+
+
+def batch_kernel(n, tallies, cols_ref, row_ref, enc_ref, ws_ref, wo_ref, wt_ref, small_ref, wi_ref, wh_ref, bg_ref, *rest):
     counts, blocks, out_ref = rest[:tallies], rest[tallies : tallies + n], rest[-1]
     width = out_ref.shape[2]
     entries = cols_ref.shape[0]
     table = jnp.concatenate([blk[...] for blk in blocks], 0)
     mine = blocks[0][...]
-    chunk = min(entries, 256)
+    chunk = min(entries, 512)
     total = jnp.zeros((BLK, width), jnp.float32)
     tally = jnp.zeros((BLK, LANES), jnp.float32)
     for c in range(entries // chunk):
@@ -291,7 +333,7 @@
         own = bdot(own_hot, mine).astype(jnp.bfloat16)
         other = bdot(other_hot, table).astype(jnp.bfloat16)
         message = bdot(own, ws_ref[...]) + bdot(other, wo_ref[...])
-        message = message + (bdot(enc_ref[at, :], wt_ref[...]) + bm_ref[...])
+        message = message + (bdot(enc_ref[at, :], wt_ref[...]) + small_ref[:, 2 * LANES : 2 * LANES + width])
         message = jnp.maximum(message, 0.0).astype(jnp.bfloat16)
 
         def gate(part):
@@ -340,6 +382,10 @@
     return jnp.sum(jnp.where(up == across, row[:, :LANES], 0.0), axis=1, keepdims=True)
 
 
+def counts_of(first, g, b):
+    return first[g, BLK : BLK + COUNT_ROWS, :].astype(jnp.int32).astype(jnp.float32)[b : b + 1]
+
+
 def gather_hits(ids_ref, delta, counts, b, block, first, total, tally):
     total[...] = jnp.zeros_like(total)
     tally[...] = jnp.zeros_like(tally)
@@ -347,7 +393,7 @@
 
         @pl.when(ids_ref[b, 0, g] == block)
         def _():
-            count = column(counts[g, BLK : BLK + COUNT_ROWS, :].astype(jnp.int32).astype(jnp.float32)[b : b + 1])
+            count = column(counts_of(counts, g, b))
             tally[...] += jnp.broadcast_to(count, tally.shape)
             total[...] += delta[g, :BLK, :].astype(jnp.int32).astype(jnp.float32) * (count * (1.0 / STEPS))
 
@@ -357,30 +403,32 @@
     return total[...] * jnp.concatenate([scale] * (total.shape[1] // LANES), 1)
 
 
-def next_kernel(b, count, ids_ref, *refs):
+def next_kernel(b, groups, rows, plan_ref, *refs):
     (*rest, out_ref, value, total, tally) = refs
     starts, deltas = rest[: len(rest) - b], rest[len(rest) - b :]
-    groups = ids_ref.shape[2]
-    me = lax.axis_index("rep")
-    mine = ids_ref[b, 0, me]
-    if len(starts) == 1:
-        value[...] = starts[0][lax.div(mine, count)].astype(jnp.float32)
-    else:
-        other = from_partner(ids_ref, b, count, 0, bit_order(groups)[-1], me)
-        value[...] = starts[0][0].astype(jnp.float32)
-
-        @pl.when(other)
+    width = out_ref.shape[1]
+    if b == 0:
+        block = jnp.zeros(out_ref.shape, jnp.float32)
+        for g in range(groups):
+            block = jnp.where(flag(plan_ref, rows["owner", g], width) > 0.5, starts[0][g].astype(jnp.float32), block)
+        out_ref[...] = block.astype(jnp.bfloat16)
+        return
+    last = len(bit_order(groups)) - 1
+    other = flag(plan_ref, rows["other", b, last, 0], width) > 0.5
+    value[...] = jnp.where(other, starts[1][0].astype(jnp.float32), starts[0][0].astype(jnp.float32))
+    for e in range(b):
+        at = rows["hit", b, e, 0]
+
+        @pl.when(jnp.max(plan_ref[at : at + groups, :]) > 0.5)
         def _():
-            value[...] = starts[1][0].astype(jnp.float32)
-
-    for e in range(b):
-        hit = ids_ref[e, 0, 0] == mine
-        for g in range(1, groups):
-            hit = jnp.logical_or(hit, ids_ref[e, 0, g] == mine)
-
-        @pl.when(hit)
-        def _():
-            gather_hits(ids_ref, deltas[e], deltas[0], e, mine, 0, total, tally)
+            total[...] = jnp.zeros_like(total)
+            tally[...] = jnp.zeros_like(tally)
+            for g in range(groups):
+                weight = jnp.broadcast_to(plan_ref[at + g : at + g + 1, :], tally.shape)
+                weight = weight * column(counts_of(deltas[0], g, e))
+                tally[...] += weight
+                weight = jnp.concatenate([weight * (1.0 / STEPS)] * (width // LANES), 1)
+                total[...] += weight * deltas[e][g, :BLK, :].astype(jnp.int32).astype(jnp.float32)
             value[...] += gain(total, tally)
 
     out_ref[...] = value[...].astype(jnp.bfloat16)
@@ -390,17 +438,17 @@
     return [pltpu.VMEM((rows, width), jnp.float32), pltpu.VMEM((rows, LANES), jnp.float32)]
 
 
-def next_block(b, count, ids, starts, deltas):
-    rows, width = BLK, starts[0].shape[2]
+def next_block(b, groups, rows, plan, starts, deltas):
+    width = starts[0].shape[2]
     return pl.pallas_call(
-        functools.partial(next_kernel, b, count),
-        out_shape=jax.ShapeDtypeStruct((rows, width), jnp.bfloat16),
-        in_specs=[SMEM] + [VMEM] * (len(starts) + len(deltas)),
+        functools.partial(next_kernel, b, groups, rows),
+        out_shape=jax.ShapeDtypeStruct((BLK, width), jnp.bfloat16),
+        in_specs=[VMEM] * (1 + len(starts) + len(deltas)),
         out_specs=VMEM,
-        scratch_shapes=[pltpu.VMEM((rows, width), jnp.float32)] + scratch(rows, width),
+        scratch_shapes=[pltpu.VMEM((BLK, width), jnp.float32)] + scratch(BLK, width),
         compiler_params=ROOM,
         name="next_block",
-    )(ids, *starts, *deltas)
+    )(plan, *starts, *deltas)
 
 
 def is_fresh(ids_ref, b, g, count, me):
@@ -449,39 +497,52 @@
     )(ids, mem, *deltas)
 
 
-def finish_kernel(b, count, ids_ref, mem_ref, last_ref, counts, delta, out_ref, bufs, total, tally, sems):
-    me = lax.axis_index("rep")
-    for g in range(delta.shape[0]):
-        block, fresh = is_fresh(ids_ref, b, g, count, me)
-
-        @pl.when(fresh)
+def finish_kernel(b, count, rows, plan_ref, mem_ref, last_ref, counts, delta, out_ref, bufs, total, tally, sems):
+    groups, _, width = last_ref.shape
+
+    def line(key, g):
+        return plan_ref[rows[key, g] : rows[key, g] + 1, :]
+
+    def copy(g):
+        place = lax.rem(jnp.max(line("block", g)).astype(jnp.int32), count)
+        return pltpu.make_async_copy(bufs.at[g], out_ref.at[place], sems.at[g])
+
+    fresh = [jnp.max(line("fresh", g)) > 0.5 for g in range(groups)]
+    for g in range(groups):
+
+        @pl.when(fresh[g])
         def _():
-            gather_hits(ids_ref, delta, counts, b, block, g, total, tally)
+            total[...] = jnp.zeros_like(total)
+            tally[...] = jnp.zeros_like(tally)
+            for e in range(g, groups):
+                weight = jnp.where(line("block", e) == line("block", g), 1.0, 0.0) * column(counts_of(counts, e, b))
+                tally[...] += weight
+                weight = jnp.concatenate([weight * (1.0 / STEPS)] * (width // LANES), 1)
+                total[...] += weight * delta[e, :BLK, :].astype(jnp.int32).astype(jnp.float32)
             bufs[g] = last_ref[g] + gain(total, tally)
-            pltpu.make_async_copy(bufs.at[g], out_ref.at[lax.rem(block, count)], sems.at[g]).start()
-
-    for g in range(delta.shape[0]):
-        block, fresh = is_fresh(ids_ref, b, g, count, me)
-
-        @pl.when(fresh)
+            copy(g).start()
+
+    for g in range(groups):
+
+        @pl.when(fresh[g])
         def _():
-            pltpu.make_async_copy(bufs.at[g], out_ref.at[lax.rem(block, count)], sems.at[g]).wait()
-
-
-def finish(b, count, ids, mem, last, counts, delta):
-    groups, rows, width = last.shape
+            copy(g).wait()
+
+
+def finish(b, count, rows, plan, mem, last, counts, delta):
+    groups, height, width = last.shape
     return pl.pallas_call(
-        functools.partial(finish_kernel, b, count),
+        functools.partial(finish_kernel, b, count, rows),
         out_shape=jax.ShapeDtypeStruct(mem.shape, mem.dtype),
-        in_specs=[SMEM, HBM, VMEM, VMEM, VMEM],
+        in_specs=[VMEM, HBM, VMEM, VMEM, VMEM],
         out_specs=HBM,
         input_output_aliases={1: 0},
         scratch_shapes=[pltpu.VMEM(last.shape, jnp.float32)]
-        + scratch(rows, width)
+        + scratch(height, width)
         + [pltpu.SemaphoreType.DMA((groups,))],
         compiler_params=ROOM,
         name="finish",
-    )(ids, mem, last, counts, delta)
+    )(plan, mem, last, counts, delta)
 
 
 def exchange(x):
@@ -513,24 +574,25 @@
     mem = memory.reshape(count, BLK, width)
     raw = [jnp.swapaxes(x, 0, 1) for x in (anchor_rows, target_rows, event_times)]
     small = (frequency.reshape(1, -1), phase.reshape(1, -1), b_message.reshape(1, -1))
-    sent, idx, halves, (freq, shift, bm) = pick(ids, mem, raw, small)
-    weights = (w_source, w_other, w_time, bm, w_input, w_hidden, b_gates.reshape(1, -1))
+    sent, idx, small, plan, halves = pick(ids, mem, raw, small)
+    rows = plan_rows(batches, groups)
+    weights = (w_source, w_other, w_time, small, w_input, w_hidden, b_gates.reshape(1, -1))
     starts = [(exchange(sent),)]
-    starts += [cube(b, ids, *halves[b - 1], count) for b in range(1, batches)]
+    starts += [cube(b, groups, rows, plan, *halves[b - 1]) for b in range(1, batches)]
     idx = share(idx, shards)
     entry, counts = [], ()
     for b in range(batches):
-        out = prep(b, idx, freq, shift, entries, width)
+        out = prep(b, idx, small, frequency.shape[0], entries, width)
         entry.append(out[:3])
         counts = counts or out[3:]
     deltas = []
     for b in range(batches):
-        block = next_block(b, count, ids, starts[b], deltas)
+        block = next_block(b, groups, rows, plan, starts[b], deltas)
         blocks = share(block, shards)
         sent = batch_step(blocks, entry[b], counts if b == 0 else (), weights, groups)
         deltas.append(exchange(sent))
     mem, last = settle(count, ids, mem, deltas[:-1])
-    mem = finish(batches - 1, count, ids, mem, last, deltas[0], deltas[-1])
+    mem = finish(batches - 1, count, rows, plan, mem, last, deltas[0], deltas[-1])
     return mem.reshape(memory.shape)
 
 

time: 109 us -> 104 us (0.954)
  Pallas kernels: 22.6 us -> 18 us
    pallas_call x9, Pallas kernels: 8.39 us -> 4.06 us  [the longest x1 3.3 us: pick(): pl.pallas_call(functools.partial(pick_kernel, batches, count, len(lists),...]
  transfers between devices with their start and end apart: 21 -> 21, of which waited for: 13 -> 13; matrix products, arithmetic and copies ran while one was open for 0% -> 0% of each run, Pallas kernels for 9% -> 7%
where the time goes in v1:
time: 104 us; the launch traced here: 103 us
  starting transfers between devices  35.4 us (34%)
  waiting for transfers between devices  33 us (32%)
  Pallas kernels  18 us (17%)
  blocking collectives  16.6 us (16%)
    ppermute x6, waiting for transfers between devices, cube(): got = lax.ppermute(send, 'rep', [(i, i ^ 1 << bit) for i in range(groups)])  21.8 us
    all_to_all x1, blocking collectives, exchange(): return lax.all_to_all(x, 'rep', split_axis=0, concat_axis=0, tiled=True)  16.6 us
    all_to_all x3, starting transfers between devices, exchange(): return lax.all_to_all(x, 'rep', split_axis=0, concat_axis=0, tiled=True)  15.1 us
    ppermute x6, starting transfers between devices, cube(): got = lax.ppermute(send, 'rep', [(i, i ^ 1 << bit) for i in range(groups)])  12.7 us
    ppermute x12, starting transfers between devices, share(): lax.ppermute(block, 'shard', [(partner(i, k, n), i) for i in range(n)])  7.54 us
    pallas_call x3, Pallas kernels, batch_step(): pl.pallas_call(functools.partial(batch_kernel, len(blocks), len(counts)),...  7.15 us
    all_to_all x3, waiting for transfers between devices, exchange(): return lax.all_to_all(x, 'rep', split_axis=0, concat_axis=0, tiled=True)  6.76 us
    ppermute x12, waiting for transfers between devices, share(): lax.ppermute(block, 'shard', [(partner(i, k, n), i) for i in range(n)])  4.42 us
  transfers between devices with their start and end apart: 21, of which 13 were waited for; matrix products, arithmetic and copies ran while one was open for 0% of the time, Pallas kernels for 7%

profile of v1, /device:TPU:0, one launch (start us, length us, event | category | flops | bytes accessed | tf_op | source)
XLA Modules:
  0.0 103.3 jit_solution(8847187242878350427)
XLA Ops:
  0.0 3.3 %pick.1 = (bf16[8,64,256]{2,1,0:T(8,128)(2,1)}, s32[3,3,1,256]{3,2,1,0:T(1,128)}, f32[1,512]{1,0:T(1,128)}, f32[64,128]{1,0:T(8,128)}, bf16[4,64,256]{2,1,0:T(8,...) custom-call(s32[3,1,8]{2,1,0:T(1,128)} %bitcast.11, ...), custom_call_target="tpu_custom_call" | custom-call | flops 20000000 | bytes 1000000 | tf_op jit(solution)/shard_map/pick/pallas_call | solution.py:145
  3.3 0.0 copy-start.12
  3.3 0.0 copy-start.9
  3.4 0.0 copy-start.2
  3.4 16.6 %all_to_all.20.refs_0_ = bf16[8,64,256]{2,1,0:T(8,128)(2,1)S(1)} all-to-all(bf16[8,64,256]{2,1,0:T(8,128)(2,1)} %get-tuple-element.40), channel_id=1, replica_groups=mesh['rep'=8,'shard'=4] {'rep'}, dimensions={0} | all-to-all | bytes 524288 | tf_op jit(solution)/shard_map/all_to_all | solution.py:549
  20.0 0.1 collective-permute-start.5
  20.1 1.4 %collective-permute-start.4 = (bf16[64,256]{1,0:T(8,128)(2,1)S(1)}, bf16[64,256]{1,0:T(8,128)(2,1)S(1)}, u32[]{:S(2)}, u32[]{:S(2)}) collective-permute-start(bf16[64,256]{1,0:T(8,128)(2,1)S(1)} %next_block.3.rest_1_), channel_id=1, source_target_pairs={{2,0},{3,1},{0,2},{1,3},{6,4},{7,5},{4,6},{5,7},{10,8},{11,9},{8,1... | collective-permute-start | bytes 98312 | tf_op jit(solution)/shard_map/ppermute | solution.py:40
  21.5 0.5 collective-permute-start.3
  21.9 0.9 collective-permute-start.2
  22.9 0.8 collective-permute-start.1
  23.6 1.4 %collective-permute-done.2.refs_3_ = s32[3,3,1,256]{3,2,1,0:T(1,128)S(1)} collective-permute-done((s32[3,3,1,256]{3,2,1,0:T(1,128)S(1)}, s32[3,3,1,256]{3,2,1,0:T(1,128)S(1)}, u32[]{:S(2)}, u32[]{:S(2)}) %collective-permute-start.2) | collective-permute-done | bytes 9248 | tf_op jit(solution)/shard_map/ppermute | solution.py:40
  25.0 0.1 collective-permute-start
  25.1 0.0 copy-done.12
  25.1 1.4 %collective-permute-done.1.refs_2_ = s32[3,3,1,256]{3,2,1,0:T(1,128)S(1)} collective-permute-done((s32[3,3,1,256]{3,2,1,0:T(1,128)S(1)}, s32[3,3,1,256]{3,2,1,0:T(1,128)S(1)}, u32[]{:S(2)}, u32[]{:S(2)}) %collective-permute-start.1) | collective-permute-done | bytes 9248 | tf_op jit(solution)/shard_map/ppermute | solution.py:40
  26.5 0.0 collective-permute-done.refs_1_
  26.5 0.0 copy-start.5
  26.5 0.0 copy-start.6
  26.6 1.7 %prep.3 = (bf16[512,128]{1,0:T(8,128)(2,1)S(1)}, f32[8,512]{1,0:T(8,128)S(1)}, bf16[512,100]{1,0:T(8,128)(2,1)S(1)}, s16[8,256]{1,0:T(8,128)(2,1)S(1)}) custom-call(s32[3,3,1,256]{3,2,1,0:T(1,128)S(1)} %copy-done.11, s32[3,3,1,256]{3,2,1,0:T(1,128)S(1)} %collective-permute-done.refs_1_, s32[3,3,1,256]{3,2,1,0:T(1,128)S(1)} %collective-permute-done.1.refs_2_, ...), custom_call_target="tpu_custom_call" | custom-call | flops 100000000 | bytes 1000000 | tf_op jit(solution)/shard_map/prep/pallas_call | solution.py:302
  28.3 0.0 collective-permute-done.5.rest_4_
  28.3 0.0 collective-permute-done.4.rest_3_
  28.3 0.0 collective-permute-done.3.rest_2_
  28.4 2.4 %batch.3 = s16[8,72,256]{2,1,0:T(8,128)(2,1)} custom-call(bf16[512,128]{1,0:T(8,128)(2,1)S(1)} %get-tuple-element.36.cols_ref, f32[8,512]{1,0:T(8,128)S(1)} %get-tuple-element.37.row_ref, bf16[512,100]{1,0:T(8,128)(2,1)S(1)} %get-tuple-element.38.enc_ref, bf16[256,256]{1,0:T(8,128)(2,1)S(1)} %copy-done.4, bf16[256,256]{1,0:T(8,128)(2,1)S(1)} %copy-done.5, ...), custom_call_target="tpu_custom_call" | custom-call | flops 100000000 | bytes 4000000 | tf_op jit(solution)/shard_map/batch/pallas_call | solution.py:368
  30.8 3.7 %all-to-all-start.1 = ((s16[8,72,256]{2,1,0:T(8,128)(2,1)}), s16[8,72,256]{2,1,0:T(8,128)(2,1)S(1)}, u32[]{:S(2)}, u32[]{:S(2)}) async-start(s16[8,72,256]{2,1,0:T(8,128)(2,1)} %batch.3), calls=%async_computation.1 | async-start | bytes 589824 | tf_op jit(solution)/shard_map/all_to_all | solution.py:549
  34.5 0.0 copy-done.14
  34.5 2.0 %collective-permute-start.6 = (bf16[4,64,256]{2,1,0:T(8,128)(2,1)S(1)}, bf16[4,64,256]{2,1,0:T(8,128)(2,1)S(1)}, u32[]{:S(2)}, u32[]{:S(2)}) collective-permute-start(bf16[4,64,256]{2,1,0:T(8,128)(2,1)S(1)} %copy-done.14), channel_id=1, source_target_pairs={{0,4},{4,0},{8,12},{12,8},{16,20},{20,16},{24,28},{28,24},{1,5},{5... | collective-permute-start | bytes 393224 | tf_op jit(solution)/shard_map/ppermute | solution.py:197
  36.5 5.9 %collective-permute-done.6.got_ref = bf16[4,64,256]{2,1,0:T(8,128)(2,1)S(1)} collective-permute-done((bf16[4,64,256]{2,1,0:T(8,128)(2,1)S(1)}, bf16[4,64,256]{2,1,0:T(8,128)(2,1)S(1)}, u32[]{:S(2)}, u32[]{:S(2)}) %collective-permute-start.6) | collective-permute-done | bytes 131104 | tf_op jit(solution)/shard_map/ppermute | solution.py:197
  42.4 0.0 copy-done.8
  42.4 2.8 %collective-permute-start.7 = (bf16[2,64,256]{2,1,0:T(8,128)(2,1)S(1)}, bf16[2,64,256]{2,1,0:T(8,128)(2,1)S(1)}, u32[]{:S(2)}, u32[]{:S(2)}) collective-permute-start(bf16[2,64,256]{2,1,0:T(8,128)(2,1)S(1)} %get-tuple-element.47), channel_id=1, source_target_pairs={{0,16},{4,20},{8,24},{12,28},{16,0},{20,4},{24,8},{28,12},{1,17},{... | collective-permute-start | bytes 196616 | tf_op jit(solution)/shard_map/ppermute | solution.py:197
  45.3 2.5 %collective-permute-done.7.got_ref = bf16[2,64,256]{2,1,0:T(8,128)(2,1)S(1)} collective-permute-done((bf16[2,64,256]{2,1,0:T(8,128)(2,1)S(1)}, bf16[2,64,256]{2,1,0:T(8,128)(2,1)S(1)}, u32[]{:S(2)}, u32[]{:S(2)}) %collective-permute-start.7) | collective-permute-done | bytes 65568 | tf_op jit(solution)/shard_map/ppermute | solution.py:197
  47.8 1.5 %collective-permute-start.8 = (bf16[1,64,256]{2,1,0:T(8,128)(2,1)S(1)}, bf16[1,64,256]{2,1,0:T(8,128)(2,1)S(1)}, u32[]{:S(2)}, u32[]{:S(2)}) collective-permute-start(bf16[1,64,256]{2,1,0:T(8,128)(2,1)S(1)} %get-tuple-element.49), channel_id=1, source_target_pairs={{0,8},{4,12},{8,0},{12,4},{16,24},{20,28},{24,16},{28,20},{1,9},{5... | collective-permute-start | bytes 98312 | tf_op jit(solution)/shard_map/ppermute | solution.py:197
  49.3 2.5 %collective-permute-done.8.refs_1_ = bf16[1,64,256]{2,1,0:T(8,128)(2,1)S(1)} collective-permute-done((bf16[1,64,256]{2,1,0:T(8,128)(2,1)S(1)}, bf16[1,64,256]{2,1,0:T(8,128)(2,1)S(1)}, u32[]{:S(2)}, u32[]{:S(2)}) %collective-permute-start.8) | collective-permute-done | bytes 32800 | tf_op jit(solution)/shard_map/ppermute | solution.py:197
  51.8 0.0 all-to-all-done.1.refs_2_.rest_0_.counts
  51.8 0.1 next_block.4.rest_0_
  51.9 0.1 collective-permute-start.11
  52.0 1.4 %collective-permute-start.10 = (bf16[64,256]{1,0:T(8,128)(2,1)S(1)}, bf16[64,256]{1,0:T(8,128)(2,1)S(1)}, u32[]{:S(2)}, u32[]{:S(2)}) collective-permute-start(bf16[64,256]{1,0:T(8,128)(2,1)S(1)} %next_block.4.rest_0_), channel_id=1, source_target_pairs={{2,0},{3,1},{0,2},{1,3},{6,4},{7,5},{4,6},{5,7},{10,8},{11,9},{8,1... | collective-permute-start | bytes 98312 | tf_op jit(solution)/shard_map/ppermute | solution.py:40
  53.4 0.5 collective-permute-start.9
  53.9 1.3 %prep.4 = (bf16[512,128]{1,0:T(8,128)(2,1)S(1)}, f32[8,512]{1,0:T(8,128)S(1)}, bf16[512,100]{1,0:T(8,128)(2,1)S(1)}) custom-call(s32[3,3,1,256]{3,2,1,0:T(1,128)S(1)} %copy-done.11, s32[3,3,1,256]{3,2,1,0:T(1,128)S(1)} %collective-permute-done.refs_1_, s32[3,3,1,256]{3,2,1,0:T(1,128)S(1)} %collective-permute-done.1.refs_2_, ...), custom_call_target="tpu_custom_call" | custom-call | flops 100000000 | bytes 1000000 | tf_op jit(solution)/shard_map/prep/pallas_call | solution.py:302
  55.2 0.4 collective-permute-done.11.rest_3_
  55.6 0.4 collective-permute-done.10.rest_2_
  56.0 0.0 collective-permute-done.9.rest_1_
  56.0 2.4 %batch.4 = s16[8,64,256]{2,1,0:T(8,128)(2,1)} custom-call(bf16[512,128]{1,0:T(8,128)(2,1)S(1)} %get-tuple-element.41.cols_ref, f32[8,512]{1,0:T(8,128)S(1)} %get-tuple-element.42.row_ref, bf16[512,100]{1,0:T(8,128)(2,1)S(1)} %get-tuple-element.43.enc_ref, bf16[256,256]{1,0:T(8,128)(2,1)S(1)} %copy-done.4, bf16[256,256]{1,0:T(8,128)(2,1)S(1)} %copy-done.5, ...), custom_call_target="tpu_custom_call" | custom-call | flops 100000000 | bytes 4000000 | tf_op jit(solution)/shard_map/batch/pallas_call | solution.py:368
  58.4 5.6 %all-to-all-start.2 = ((s16[8,64,256]{2,1,0:T(8,128)(2,1)}), s16[8,64,256]{2,1,0:T(8,128)(2,1)S(1)}, u32[]{:S(2)}, u32[]{:S(2)}) async-start(s16[8,64,256]{2,1,0:T(8,128)(2,1)} %batch.4), calls=%async_computation.2 | async-start | bytes 524288 | tf_op jit(solution)/shard_map/all_to_all | solution.py:549
  64.0 2.0 %collective-permute-start.12 = (bf16[4,64,256]{2,1,0:T(8,128)(2,1)S(1)}, bf16[4,64,256]{2,1,0:T(8,128)(2,1)S(1)}, u32[]{:S(2)}, u32[]{:S(2)}) collective-permute-start(bf16[4,64,256]{2,1,0:T(8,128)(2,1)S(1)} %copy-done.13), channel_id=1, source_target_pairs={{0,4},{4,0},{8,12},{12,8},{16,20},{20,16},{24,28},{28,24},{1,5},{5... | collective-permute-start | bytes 393224 | tf_op jit(solution)/shard_map/ppermute | solution.py:197
  66.0 6.0 %collective-permute-done.12.got_ref = bf16[4,64,256]{2,1,0:T(8,128)(2,1)S(1)} collective-permute-done((bf16[4,64,256]{2,1,0:T(8,128)(2,1)S(1)}, bf16[4,64,256]{2,1,0:T(8,128)(2,1)S(1)}, u32[]{:S(2)}, u32[]{:S(2)}) %collective-permute-start.12) | collective-permute-done | bytes 131104 | tf_op jit(solution)/shard_map/ppermute | solution.py:197
  72.1 2.8 %collective-permute-start.13 = (bf16[2,64,256]{2,1,0:T(8,128)(2,1)S(1)}, bf16[2,64,256]{2,1,0:T(8,128)(2,1)S(1)}, u32[]{:S(2)}, u32[]{:S(2)}) collective-permute-start(bf16[2,64,256]{2,1,0:T(8,128)(2,1)S(1)} %get-tuple-element.58), channel_id=1, source_target_pairs={{0,16},{4,20},{8,24},{12,28},{16,0},{20,4},{24,8},{28,12},{1,17},{... | collective-permute-start | bytes 196616 | tf_op jit(solution)/shard_map/ppermute | solution.py:197
  74.8 2.6 %collective-permute-done.13.got_ref = bf16[2,64,256]{2,1,0:T(8,128)(2,1)S(1)} collective-permute-done((bf16[2,64,256]{2,1,0:T(8,128)(2,1)S(1)}, bf16[2,64,256]{2,1,0:T(8,128)(2,1)S(1)}, u32[]{:S(2)}, u32[]{:S(2)}) %collective-permute-start.13) | collective-permute-done | bytes 65568 | tf_op jit(solution)/shard_map/ppermute | solution.py:197
  77.4 1.6 %collective-permute-start.14 = (bf16[1,64,256]{2,1,0:T(8,128)(2,1)S(1)}, bf16[1,64,256]{2,1,0:T(8,128)(2,1)S(1)}, u32[]{:S(2)}, u32[]{:S(2)}) collective-permute-start(bf16[1,64,256]{2,1,0:T(8,128)(2,1)S(1)} %get-tuple-element.60), channel_id=1, source_target_pairs={{0,8},{4,12},{8,0},{12,4},{16,24},{20,28},{24,16},{28,20},{1,9},{5... | collective-permute-start | bytes 98312 | tf_op jit(solution)/shard_map/ppermute | solution.py:197
  79.0 2.4 %collective-permute-done.14.refs_1_ = bf16[1,64,256]{2,1,0:T(8,128)(2,1)S(1)} collective-permute-done((bf16[1,64,256]{2,1,0:T(8,128)(2,1)S(1)}, bf16[1,64,256]{2,1,0:T(8,128)(2,1)S(1)}, u32[]{:S(2)}, u32[]{:S(2)}) %collective-permute-start.14) | collective-permute-done | bytes 32800 | tf_op jit(solution)/shard_map/ppermute | solution.py:197
  81.4 0.0 all-to-all-done.2.rest_1_.refs_3_
  81.4 0.2 next_block.5.rest_0_
  81.7 0.1 collective-permute-start.17
  81.7 1.3 %collective-permute-start.16 = (bf16[64,256]{1,0:T(8,128)(2,1)S(1)}, bf16[64,256]{1,0:T(8,128)(2,1)S(1)}, u32[]{:S(2)}, u32[]{:S(2)}) collective-permute-start(bf16[64,256]{1,0:T(8,128)(2,1)S(1)} %next_block.5.rest_0_), channel_id=1, source_target_pairs={{2,0},{3,1},{0,2},{1,3},{6,4},{7,5},{4,6},{5,7},{10,8},{11,9},{8,1... | collective-permute-start | bytes 98312 | tf_op jit(solution)/shard_map/ppermute | solution.py:40
  83.1 0.5 collective-permute-start.15
  83.6 1.3 %prep.5 = (bf16[512,128]{1,0:T(8,128)(2,1)S(1)}, f32[8,512]{1,0:T(8,128)S(1)}, bf16[512,100]{1,0:T(8,128)(2,1)S(1)}) custom-call(s32[3,3,1,256]{3,2,1,0:T(1,128)S(1)} %copy-done.11, s32[3,3,1,256]{3,2,1,0:T(1,128)S(1)} %collective-permute-done.refs_1_, s32[3,3,1,256]{3,2,1,0:T(1,128)S(1)} %collective-permute-done.1.refs_2_, ...), custom_call_target="tpu_custom_call" | custom-call | flops 100000000 | bytes 1000000 | tf_op jit(solution)/shard_map/prep/pallas_call | solution.py:302
  84.9 0.3 collective-permute-done.17.rest_3_
  85.2 0.5 collective-permute-done.16.rest_2_
  85.7 0.0 collective-permute-done.15.rest_1_
  85.7 2.4 %batch.5 = s16[8,64,256]{2,1,0:T(8,128)(2,1)} custom-call(bf16[512,128]{1,0:T(8,128)(2,1)S(1)} %get-tuple-element.52.cols_ref, f32[8,512]{1,0:T(8,128)S(1)} %get-tuple-element.53.row_ref, bf16[512,100]{1,0:T(8,128)(2,1)S(1)} %get-tuple-element.54.enc_ref, bf16[256,256]{1,0:T(8,128)(2,1)S(1)} %copy-done.4, bf16[256,256]{1,0:T(8,128)(2,1)S(1)} %copy-done.5, ...), custom_call_target="tpu_custom_call" | custom-call | flops 100000000 | bytes 4000000 | tf_op jit(solution)/shard_map/batch/pallas_call | solution.py:368
  88.1 5.8 %all-to-all-start.3 = ((s16[8,64,256]{2,1,0:T(8,128)(2,1)}), s16[8,64,256]{2,1,0:T(8,128)(2,1)S(1)}, u32[]{:S(2)}, u32[]{:S(2)}) async-start(s16[8,64,256]{2,1,0:T(8,128)(2,1)} %batch.5), calls=%async_computation.3 | async-start | bytes 524288 | tf_op jit(solution)/shard_map/all_to_all | solution.py:549
  93.9 0.0 copy-done
  93.9 0.0 copy-done.10
  93.9 2.4 %settle.1 = (f32[16,64,256]{2,1,0:T(8,128)}, f32[8,64,256]{2,1,0:T(8,128)S(1)}) custom-call(s32[3,1,8]{2,1,0:T(1,128)S(1)} %bitcast.12, f32[16,64,256]{2,1,0:T(8,128)S(1)} %bitcast.10, s16[8,72,256]{2,1,0:T(8,128)(2,1)S(1)} %all-to-all-done.1.refs_2_.rest_0_.counts, s16[8,64,256]{2,1,0:T(8,128)(2,1)S(1)} %all-to-all-done.2.rest_1_.refs_3_), custom_call_target="tpu_custom_call" | custom-call | flops 20000000 | bytes 3000000 | tf_op jit(solution)/shard_map/settle/pallas_call | solution.py:485
  96.3 6.8 %all-to-all-done.3.delta = s16[8,64,256]{2,1,0:T(8,128)(2,1)S(1)} async-done(((s16[8,64,256]{2,1,0:T(8,128)(2,1)}), s16[8,64,256]{2,1,0:T(8,128)(2,1)S(1)}, u32[]{:S(2)}, u32[]{:S(2)}) %all-to-all-start.3) | async-done | bytes 262176 | tf_op jit(solution)/shard_map/all_to_all | solution.py:549
  103.1 0.2 finish.1
  (26 shorter events, 0.2 us)
Async XLA Ops:
  3.3 16.6 %copy-start.3 = (f32[64,128]{1,0:T(8,128)S(1)}, f32[64,128]{1,0:T(8,128)}, u32[]{:S(2)}) copy-start(f32[64,128]{1,0:T(8,128)} %get-tuple-element.33.plan_ref) | copy-start | bytes 98308
  3.3 18.6 %copy-start.11 = (s32[3,3,1,256]{3,2,1,0:T(1,128)S(1)}, s32[3,3,1,256]{3,2,1,0:T(1,128)}, u32[]{:S(2)}) copy-start(s32[3,3,1,256]{3,2,1,0:T(1,128)} %get-tuple-element.34.refs_0_) | copy-start | bytes 27652
  3.3 21.8 %copy-start.12 = (f32[768]{0:T(1024)S(1)}, f32[768]{0:T(1024)}, u32[]{:S(2)}) copy-start(f32[768]{0:T(1024)} %param.27) | copy-start | bytes 9220
  3.3 23.2 %copy-start.9 = (f32[1,512]{1,0:T(1,128)S(1)}, f32[1,512]{1,0:T(1,128)}, u32[]{:S(2)}) copy-start(f32[1,512]{1,0:T(1,128)} %get-tuple-element.35.refs_4_.small_ref) | copy-start | bytes 6148
  3.4 25.0 %copy-start.2 = (bf16[256,768]{1,0:T(8,128)(2,1)S(1)}, bf16[256,768]{1,0:T(8,128)(2,1)}, u32[]{:S(2)}) copy-start(bf16[256,768]{1,0:T(8,128)(2,1)} %wh_ref.5) | copy-start | bytes 1179652
  20.0 8.4 %copy-start.1 = (bf16[256,768]{1,0:T(8,128)(2,1)S(1)}, bf16[256,768]{1,0:T(8,128)(2,1)}, u32[]{:S(2)}) copy-start(bf16[256,768]{1,0:T(8,128)(2,1)} %wi_ref.5) | copy-start | bytes 1179652
  20.0 8.3 %collective-permute-start.5 = (bf16[64,256]{1,0:T(8,128)(2,1)S(1)}, bf16[64,256]{1,0:T(8,128)(2,1)S(1)}, u32[]{:S(2)}, u32[]{:S(2)}) collective-permute-start(bf16[64,256]{1,0:T(8,128)(2,1)S(1)} %next_block.3.rest_1_), channel_id=1, source_target_pairs={{3,0},{2,1},{1,2},{0,3},{7,4},{6,5},{5,6},{4,7},{11,8},{10,9},{9,1... | collective-permute-start | bytes 98312 | tf_op jit(solution)/shard_map/ppermute | solution.py:40
  20.1 8.2 %collective-permute-start.4 = (bf16[64,256]{1,0:T(8,128)(2,1)S(1)}, bf16[64,256]{1,0:T(8,128)(2,1)S(1)}, u32[]{:S(2)}, u32[]{:S(2)}) collective-permute-start(bf16[64,256]{1,0:T(8,128)(2,1)S(1)} %next_block.3.rest_1_), channel_id=1, source_target_pairs={{2,0},{3,1},{0,2},{1,3},{6,4},{7,5},{4,6},{5,7},{10,8},{11,9},{8,1... | collective-permute-start | bytes 98312 | tf_op jit(solution)/shard_map/ppermute | solution.py:40
  21.5 6.8 %collective-permute-start.3 = (bf16[64,256]{1,0:T(8,128)(2,1)S(1)}, bf16[64,256]{1,0:T(8,128)(2,1)S(1)}, u32[]{:S(2)}, u32[]{:S(2)}) collective-permute-start(bf16[64,256]{1,0:T(8,128)(2,1)S(1)} %next_block.3.rest_1_), channel_id=1, source_target_pairs={{1,0},{0,1},{3,2},{2,3},{5,4},{4,5},{7,6},{6,7},{9,8},{8,9},{11,10... | collective-permute-start | bytes 98312 | tf_op jit(solution)/shard_map/ppermute | solution.py:40
  21.9 3.1 %collective-permute-start.2 = (s32[3,3,1,256]{3,2,1,0:T(1,128)S(1)}, s32[3,3,1,256]{3,2,1,0:T(1,128)S(1)}, u32[]{:S(2)}, u32[]{:S(2)}) collective-permute-start(s32[3,3,1,256]{3,2,1,0:T(1,128)S(1)} %copy-done.11), channel_id=1, source_target_pairs={{3,0},{2,1},{1,2},{0,3},{7,4},{6,5},{5,6},{4,7},{11,8},{10,9},{9,1... | collective-permute-start | bytes 27656 | tf_op jit(solution)/shard_map/ppermute | solution.py:40
  22.9 3.7 %collective-permute-start.1 = (s32[3,3,1,256]{3,2,1,0:T(1,128)S(1)}, s32[3,3,1,256]{3,2,1,0:T(1,128)S(1)}, u32[]{:S(2)}, u32[]{:S(2)}) collective-permute-start(s32[3,3,1,256]{3,2,1,0:T(1,128)S(1)} %copy-done.11), channel_id=1, source_target_pairs={{2,0},{3,1},{0,2},{1,3},{6,4},{7,5},{4,6},{5,7},{10,8},{11,9},{8,1... | collective-permute-start | bytes 27656 | tf_op jit(solution)/shard_map/ppermute | solution.py:40
  25.0 1.5 %collective-permute-start = (s32[3,3,1,256]{3,2,1,0:T(1,128)S(1)}, s32[3,3,1,256]{3,2,1,0:T(1,128)S(1)}, u32[]{:S(2)}, u32[]{:S(2)}) collective-permute-start(s32[3,3,1,256]{3,2,1,0:T(1,128)S(1)} %copy-done.11), channel_id=1, source_target_pairs={{1,0},{0,1},{3,2},{2,3},{5,4},{4,5},{7,6},{6,7},{9,8},{8,9},{11,10... | collective-permute-start | bytes 27656 | tf_op jit(solution)/shard_map/ppermute | solution.py:40
  26.5 1.8 %copy-start.4 = (bf16[256,256]{1,0:T(8,128)(2,1)S(1)}, bf16[256,256]{1,0:T(8,128)(2,1)}, u32[]{:S(2)}) copy-start(bf16[256,256]{1,0:T(8,128)(2,1)} %ws_ref.5) | copy-start | bytes 393220
  26.5 1.8 %copy-start.5 = (bf16[256,256]{1,0:T(8,128)(2,1)S(1)}, bf16[256,256]{1,0:T(8,128)(2,1)}, u32[]{:S(2)}) copy-start(bf16[256,256]{1,0:T(8,128)(2,1)} %wo_ref.5) | copy-start | bytes 393220
  26.5 1.8 %copy-start.6 = (bf16[100,256]{1,0:T(8,128)(2,1)S(1)}, bf16[100,256]{1,0:T(8,128)(2,1)}, u32[]{:S(2)}) copy-start(bf16[100,256]{1,0:T(8,128)(2,1)} %wt_ref.5) | copy-start | bytes 153604
  30.7 3.7 %copy-start.14 = (bf16[4,64,256]{2,1,0:T(8,128)(2,1)S(1)}, bf16[4,64,256]{2,1,0:T(8,128)(2,1)}, u32[]{:S(2)}) copy-start(bf16[4,64,256]{2,1,0:T(8,128)(2,1)} %get-tuple-element.45) | copy-start | bytes 393220
  30.8 11.7 %copy-start.8 = (bf16[4,64,256]{2,1,0:T(8,128)(2,1)S(1)}, bf16[4,64,256]{2,1,0:T(8,128)(2,1)}, u32[]{:S(2)}) copy-start(bf16[4,64,256]{2,1,0:T(8,128)(2,1)} %get-tuple-element.44.keep_in) | copy-start | bytes 393220
  30.8 21.1 %all-to-all-start.1 = ((s16[8,72,256]{2,1,0:T(8,128)(2,1)}), s16[8,72,256]{2,1,0:T(8,128)(2,1)S(1)}, u32[]{:S(2)}, u32[]{:S(2)}) async-start(s16[8,72,256]{2,1,0:T(8,128)(2,1)} %batch.3), calls=%async_computation.1 | async-start | bytes 589824 | tf_op jit(solution)/shard_map/all_to_all | solution.py:549
  34.5 7.9 %collective-permute-start.6 = (bf16[4,64,256]{2,1,0:T(8,128)(2,1)S(1)}, bf16[4,64,256]{2,1,0:T(8,128)(2,1)S(1)}, u32[]{:S(2)}, u32[]{:S(2)}) collective-permute-start(bf16[4,64,256]{2,1,0:T(8,128)(2,1)S(1)} %copy-done.14), channel_id=1, source_target_pairs={{0,4},{4,0},{8,12},{12,8},{16,20},{20,16},{24,28},{28,24},{1,5},{5... | collective-permute-start | bytes 393224 | tf_op jit(solution)/shard_map/ppermute | solution.py:197
  42.4 5.4 %collective-permute-start.7 = (bf16[2,64,256]{2,1,0:T(8,128)(2,1)S(1)}, bf16[2,64,256]{2,1,0:T(8,128)(2,1)S(1)}, u32[]{:S(2)}, u32[]{:S(2)}) collective-permute-start(bf16[2,64,256]{2,1,0:T(8,128)(2,1)S(1)} %get-tuple-element.47), channel_id=1, source_target_pairs={{0,16},{4,20},{8,24},{12,28},{16,0},{20,4},{24,8},{28,12},{1,17},{... | collective-permute-start | bytes 196616 | tf_op jit(solution)/shard_map/ppermute | solution.py:197
  47.8 4.0 %collective-permute-start.8 = (bf16[1,64,256]{2,1,0:T(8,128)(2,1)S(1)}, bf16[1,64,256]{2,1,0:T(8,128)(2,1)S(1)}, u32[]{:S(2)}, u32[]{:S(2)}) collective-permute-start(bf16[1,64,256]{2,1,0:T(8,128)(2,1)S(1)} %get-tuple-element.49), channel_id=1, source_target_pairs={{0,8},{4,12},{8,0},{12,4},{16,24},{20,28},{24,16},{28,20},{1,9},{5... | collective-permute-start | bytes 98312 | tf_op jit(solution)/shard_map/ppermute | solution.py:197
  51.9 3.6 %collective-permute-start.11 = (bf16[64,256]{1,0:T(8,128)(2,1)S(1)}, bf16[64,256]{1,0:T(8,128)(2,1)S(1)}, u32[]{:S(2)}, u32[]{:S(2)}) collective-permute-start(bf16[64,256]{1,0:T(8,128)(2,1)S(1)} %next_block.4.rest_0_), channel_id=1, source_target_pairs={{3,0},{2,1},{1,2},{0,3},{7,4},{6,5},{5,6},{4,7},{11,8},{10,9},{9,1... | collective-permute-start | bytes 98312 | tf_op jit(solution)/shard_map/ppermute | solution.py:40
  52.0 4.0 %collective-permute-start.10 = (bf16[64,256]{1,0:T(8,128)(2,1)S(1)}, bf16[64,256]{1,0:T(8,128)(2,1)S(1)}, u32[]{:S(2)}, u32[]{:S(2)}) collective-permute-start(bf16[64,256]{1,0:T(8,128)(2,1)S(1)} %next_block.4.rest_0_), channel_id=1, source_target_pairs={{2,0},{3,1},{0,2},{1,3},{6,4},{7,5},{4,6},{5,7},{10,8},{11,9},{8,1... | collective-permute-start | bytes 98312 | tf_op jit(solution)/shard_map/ppermute | solution.py:40
  53.4 2.6 %collective-permute-start.9 = (bf16[64,256]{1,0:T(8,128)(2,1)S(1)}, bf16[64,256]{1,0:T(8,128)(2,1)S(1)}, u32[]{:S(2)}, u32[]{:S(2)}) collective-permute-start(bf16[64,256]{1,0:T(8,128)(2,1)S(1)} %next_block.4.rest_0_), channel_id=1, source_target_pairs={{1,0},{0,1},{3,2},{2,3},{5,4},{4,5},{7,6},{6,7},{9,8},{8,9},{11,10... | collective-permute-start | bytes 98312 | tf_op jit(solution)/shard_map/ppermute | solution.py:40
  58.4 5.6 %copy-start.13 = (bf16[4,64,256]{2,1,0:T(8,128)(2,1)S(1)}, bf16[4,64,256]{2,1,0:T(8,128)(2,1)}, u32[]{:S(2)}) copy-start(bf16[4,64,256]{2,1,0:T(8,128)(2,1)} %get-tuple-element.56) | copy-start | bytes 393220
  58.4 13.6 %copy-start.7 = (bf16[4,64,256]{2,1,0:T(8,128)(2,1)S(1)}, bf16[4,64,256]{2,1,0:T(8,128)(2,1)}, u32[]{:S(2)}) copy-start(bf16[4,64,256]{2,1,0:T(8,128)(2,1)} %get-tuple-element.55.keep_in) | copy-start | bytes 393220
  58.4 23.0 %all-to-all-start.2 = ((s16[8,64,256]{2,1,0:T(8,128)(2,1)}), s16[8,64,256]{2,1,0:T(8,128)(2,1)S(1)}, u32[]{:S(2)}, u32[]{:S(2)}) async-start(s16[8,64,256]{2,1,0:T(8,128)(2,1)} %batch.4), calls=%async_computation.2 | async-start | bytes 524288 | tf_op jit(solution)/shard_map/all_to_all | solution.py:549
  64.0 8.0 %collective-permute-start.12 = (bf16[4,64,256]{2,1,0:T(8,128)(2,1)S(1)}, bf16[4,64,256]{2,1,0:T(8,128)(2,1)S(1)}, u32[]{:S(2)}, u32[]{:S(2)}) collective-permute-start(bf16[4,64,256]{2,1,0:T(8,128)(2,1)S(1)} %copy-done.13), channel_id=1, source_target_pairs={{0,4},{4,0},{8,12},{12,8},{16,20},{20,16},{24,28},{28,24},{1,5},{5... | collective-permute-start | bytes 393224 | tf_op jit(solution)/shard_map/ppermute | solution.py:197
  72.1 5.3 %collective-permute-start.13 = (bf16[2,64,256]{2,1,0:T(8,128)(2,1)S(1)}, bf16[2,64,256]{2,1,0:T(8,128)(2,1)S(1)}, u32[]{:S(2)}, u32[]{:S(2)}) collective-permute-start(bf16[2,64,256]{2,1,0:T(8,128)(2,1)S(1)} %get-tuple-element.58), channel_id=1, source_target_pairs={{0,16},{4,20},{8,24},{12,28},{16,0},{20,4},{24,8},{28,12},{1,17},{... | collective-permute-start | bytes 196616 | tf_op jit(solution)/shard_map/ppermute | solution.py:197
  77.4 4.0 %collective-permute-start.14 = (bf16[1,64,256]{2,1,0:T(8,128)(2,1)S(1)}, bf16[1,64,256]{2,1,0:T(8,128)(2,1)S(1)}, u32[]{:S(2)}, u32[]{:S(2)}) collective-permute-start(bf16[1,64,256]{2,1,0:T(8,128)(2,1)S(1)} %get-tuple-element.60), channel_id=1, source_target_pairs={{0,8},{4,12},{8,0},{12,4},{16,24},{20,28},{24,16},{28,20},{1,9},{5... | collective-permute-start | bytes 98312 | tf_op jit(solution)/shard_map/ppermute | solution.py:197
  81.7 3.6 %collective-permute-start.17 = (bf16[64,256]{1,0:T(8,128)(2,1)S(1)}, bf16[64,256]{1,0:T(8,128)(2,1)S(1)}, u32[]{:S(2)}, u32[]{:S(2)}) collective-permute-start(bf16[64,256]{1,0:T(8,128)(2,1)S(1)} %next_block.5.rest_0_), channel_id=1, source_target_pairs={{3,0},{2,1},{1,2},{0,3},{7,4},{6,5},{5,6},{4,7},{11,8},{10,9},{9,1... | collective-permute-start | bytes 98312 | tf_op jit(solution)/shard_map/ppermute | solution.py:40
  81.7 4.0 %collective-permute-start.16 = (bf16[64,256]{1,0:T(8,128)(2,1)S(1)}, bf16[64,256]{1,0:T(8,128)(2,1)S(1)}, u32[]{:S(2)}, u32[]{:S(2)}) collective-permute-start(bf16[64,256]{1,0:T(8,128)(2,1)S(1)} %next_block.5.rest_0_), channel_id=1, source_target_pairs={{2,0},{3,1},{0,2},{1,3},{6,4},{7,5},{4,6},{5,7},{10,8},{11,9},{8,1... | collective-permute-start | bytes 98312 | tf_op jit(solution)/shard_map/ppermute | solution.py:40
  83.1 2.7 %collective-permute-start.15 = (bf16[64,256]{1,0:T(8,128)(2,1)S(1)}, bf16[64,256]{1,0:T(8,128)(2,1)S(1)}, u32[]{:S(2)}, u32[]{:S(2)}) collective-permute-start(bf16[64,256]{1,0:T(8,128)(2,1)S(1)} %next_block.5.rest_0_), channel_id=1, source_target_pairs={{1,0},{0,1},{3,2},{2,3},{5,4},{4,5},{7,6},{6,7},{9,8},{8,9},{11,10... | collective-permute-start | bytes 98312 | tf_op jit(solution)/shard_map/ppermute | solution.py:40
  85.7 8.1 %copy-start = (f32[1024,256]{1,0:T(8,128)S(1)}, f32[1024,256]{1,0:T(8,128)}, u32[]{:S(2)}) copy-start(f32[1024,256]{1,0:T(8,128)} %param.14) | copy-start | bytes 3145732
  88.1 5.8 %copy-start.10 = (s32[8,3,1]{0,2,1:T(1,128)S(1)}, s32[8,3,1]{0,2,1:T(1,128)}, u32[]{:S(2)}) copy-start(s32[8,3,1]{0,2,1:T(1,128)} %param.18) | copy-start | bytes 292
  88.1 15.0 %all-to-all-start.3 = ((s16[8,64,256]{2,1,0:T(8,128)(2,1)}), s16[8,64,256]{2,1,0:T(8,128)(2,1)S(1)}, u32[]{:S(2)}, u32[]{:S(2)}) async-start(s16[8,64,256]{2,1,0:T(8,128)(2,1)} %batch.5), calls=%async_computation.3 | async-start | bytes 524288 | tf_op jit(solution)/shard_map/all_to_all | solution.py:549

commit v2 on v1

--- a/solution.py
+++ b/solution.py
@@ -17,6 +17,7 @@
 ALL_ROOM = pltpu.CompilerParams(vmem_limit_bytes=60 << 20)
 ROOM = pltpu.CompilerParams(vmem_limit_bytes=12 << 20)
 
+
 NT = (((1,), (1,)), ((), ()))
 
 
@@ -24,6 +25,16 @@
     if dims is None:
         return jnp.dot(a, b, preferred_element_type=jnp.float32)
     return lax.dot_general(a, b, dims, preferred_element_type=jnp.float32)
+
+
+def place_of(block, count):
+    return block & (count - 1) if count & (count - 1) == 0 else lax.rem(block, count)
+
+
+def owner_of(block, count):
+    if count & (count - 1) == 0:
+        return lax.shift_right_logical(block, count.bit_length() - 1)
+    return lax.div(block, count)
 
 
 def partner(i, k, n):
@@ -80,10 +91,10 @@
     mine = [ids_ref[b, 0, me] for b in range(batches)]
     for key, r in plan_rows(batches, groups).items():
         if key[0] == "owner":
-            on = lax.div(mine[0], count) == key[1]
+            on = owner_of(mine[0], count) == key[1]
         elif key[0] == "other":
             _, b, step, j = key
-            owner = lax.div(ids_ref[b, 0, me ^ j], count)
+            owner = owner_of(ids_ref[b, 0, me ^ j], count)
             on = (lax.shift_right_logical(owner ^ me, steps[step][0]) & 1) == 1
         elif key[0] == "block":
             on = ids_ref[batches - 1, 0, key[1]]
@@ -116,7 +127,7 @@
         plan += [(b, me ^ j, keep_ref, k) for k, j in enumerate(kept)]
     copies = []
     for k, (b, g, _, _) in enumerate(plan):
-        cp = pltpu.make_async_copy(mem_ref.at[lax.rem(ids_ref[b, 0, g], count)], bufs.at[k], sems.at[k])
+        cp = pltpu.make_async_copy(mem_ref.at[place_of(ids_ref[b, 0, g], count)], bufs.at[k], sems.at[k])
         cp.start()
         copies.append(cp)
     moves = [(ref, idx_ref.at[k]) for k, ref in enumerate(lists)] + list(zip(small, parts))
@@ -453,7 +464,7 @@
 
 def is_fresh(ids_ref, b, g, count, me):
     block = ids_ref[b, 0, g]
-    fresh = lax.div(block, count) == me
+    fresh = owner_of(block, count) == me
     for e in range(g):
         fresh = jnp.logical_and(fresh, ids_ref[b, 0, e] != block)
     return block, fresh
@@ -473,11 +484,11 @@
             @pl.when(fresh)
             def _():
                 gather_hits(ids_ref, delta, deltas[0], b, block, g, total, tally)
-                place = lax.rem(block, count)
+                place = place_of(block, count)
                 out_ref[place] += gain(total, tally)
 
     for g in range(groups):
-        last_ref[g] = out_ref[lax.rem(ids_ref[len(deltas), 0, g], count)]
+        last_ref[g] = out_ref[place_of(ids_ref[len(deltas), 0, g], count)]
 
 
 def settle(count, ids, mem, deltas):
@@ -504,7 +515,7 @@
         return plan_ref[rows[key, g] : rows[key, g] + 1, :]
 
     def copy(g):
-        place = lax.rem(jnp.max(line("block", g)).astype(jnp.int32), count)
+        place = place_of(jnp.max(line("block", g)).astype(jnp.int32), count)
         return pltpu.make_async_copy(bufs.at[g], out_ref.at[place], sems.at[g])
 
     fresh = [jnp.max(line("fresh", g)) > 0.5 for g in range(groups)]

time: 104 us -> 104 us (level)
  no operation moved by 1% of the time
where the time goes in v2:
time: 104 us; the launch traced here: 103 us
  starting transfers between devices  35.4 us (34%)
  waiting for transfers between devices  33 us (32%)
  Pallas kernels  18 us (17%)
  blocking collectives  16.6 us (16%)
    ppermute x6, waiting for transfers between devices, cube(): got = lax.ppermute(send, 'rep', [(i, i ^ 1 << bit) for i in range(groups)])  21.8 us
    all_to_all x1, blocking collectives, exchange(): return lax.all_to_all(x, 'rep', split_axis=0, concat_axis=0, tiled=True)  16.6 us
    all_to_all x3, starting transfers between devices, exchange(): return lax.all_to_all(x, 'rep', split_axis=0, concat_axis=0, tiled=True)  15.1 us
    ppermute x6, starting transfers between devices, cube(): got = lax.ppermute(send, 'rep', [(i, i ^ 1 << bit) for i in range(groups)])  12.7 us
    ppermute x12, starting transfers between devices, share(): lax.ppermute(block, 'shard', [(partner(i, k, n), i) for i in range(n)])  7.54 us
    pallas_call x3, Pallas kernels, batch_step(): pl.pallas_call(functools.partial(batch_kernel, len(blocks), len(counts)),...  7.15 us
    all_to_all x3, waiting for transfers between devices, exchange(): return lax.all_to_all(x, 'rep', split_axis=0, concat_axis=0, tiled=True)  6.79 us
    ppermute x12, waiting for transfers between devices, share(): lax.ppermute(block, 'shard', [(partner(i, k, n), i) for i in range(n)])  4.4 us
  transfers between devices with their start and end apart: 21, of which 13 were waited for; matrix products, arithmetic and copies ran while one was open for 0% of the time, Pallas kernels for 7%

profile of v2, /device:TPU:0, one launch (start us, length us, event | category | flops | bytes accessed | tf_op | source)
XLA Modules:
  0.0 103.3 jit_solution(3932544437310886645)
XLA Ops:
  0.0 3.3 %pick.1 = (bf16[8,64,256]{2,1,0:T(8,128)(2,1)}, s32[3,3,1,256]{3,2,1,0:T(1,128)}, f32[1,512]{1,0:T(1,128)}, f32[64,128]{1,0:T(8,128)}, bf16[4,64,256]{2,1,0:T(8,...) custom-call(s32[3,1,8]{2,1,0:T(1,128)} %bitcast.11, ...), custom_call_target="tpu_custom_call" | custom-call | flops 20000000 | bytes 1000000 | tf_op jit(solution)/shard_map/pick/pallas_call | solution.py:156
  3.3 0.0 copy-start.12
  3.4 0.0 copy-start.2
  3.4 16.6 %all_to_all.20.refs_0_ = bf16[8,64,256]{2,1,0:T(8,128)(2,1)S(1)} all-to-all(bf16[8,64,256]{2,1,0:T(8,128)(2,1)} %get-tuple-element.40), channel_id=1, replica_groups=mesh['rep'=8,'shard'=4] {'rep'}, dimensions={0} | all-to-all | bytes 524288 | tf_op jit(solution)/shard_map/all_to_all | solution.py:560
  20.0 0.1 collective-permute-start.5
  20.1 1.4 %collective-permute-start.4 = (bf16[64,256]{1,0:T(8,128)(2,1)S(1)}, bf16[64,256]{1,0:T(8,128)(2,1)S(1)}, u32[]{:S(2)}, u32[]{:S(2)}) collective-permute-start(bf16[64,256]{1,0:T(8,128)(2,1)S(1)} %next_block.3.rest_1_), channel_id=1, source_target_pairs={{2,0},{3,1},{0,2},{1,3},{6,4},{7,5},{4,6},{5,7},{10,8},{11,9},{8,1... | collective-permute-start | bytes 98312 | tf_op jit(solution)/shard_map/ppermute | solution.py:51
  21.5 0.5 collective-permute-start.3
  21.9 0.9 collective-permute-start.2
  22.9 0.8 collective-permute-start.1
  23.6 1.4 %collective-permute-done.2.refs_3_ = s32[3,3,1,256]{3,2,1,0:T(1,128)S(1)} collective-permute-done((s32[3,3,1,256]{3,2,1,0:T(1,128)S(1)}, s32[3,3,1,256]{3,2,1,0:T(1,128)S(1)}, u32[]{:S(2)}, u32[]{:S(2)}) %collective-permute-start.2) | collective-permute-done | bytes 9248 | tf_op jit(solution)/shard_map/ppermute | solution.py:51
  25.0 0.1 collective-permute-start
  25.1 1.4 %collective-permute-done.1.refs_2_ = s32[3,3,1,256]{3,2,1,0:T(1,128)S(1)} collective-permute-done((s32[3,3,1,256]{3,2,1,0:T(1,128)S(1)}, s32[3,3,1,256]{3,2,1,0:T(1,128)S(1)}, u32[]{:S(2)}, u32[]{:S(2)}) %collective-permute-start.1) | collective-permute-done | bytes 9248 | tf_op jit(solution)/shard_map/ppermute | solution.py:51
  26.5 0.0 collective-permute-done.refs_1_
  26.5 0.0 copy-start.5
  26.5 0.0 copy-start.6
  26.6 1.7 %prep.3 = (bf16[512,128]{1,0:T(8,128)(2,1)S(1)}, f32[8,512]{1,0:T(8,128)S(1)}, bf16[512,100]{1,0:T(8,128)(2,1)S(1)}, s16[8,256]{1,0:T(8,128)(2,1)S(1)}) custom-call(s32[3,3,1,256]{3,2,1,0:T(1,128)S(1)} %copy-done.11, s32[3,3,1,256]{3,2,1,0:T(1,128)S(1)} %collective-permute-done.refs_1_, s32[3,3,1,256]{3,2,1,0:T(1,128)S(1)} %collective-permute-done.1.refs_2_, ...), custom_call_target="tpu_custom_call" | custom-call | flops 100000000 | bytes 1000000 | tf_op jit(solution)/shard_map/prep/pallas_call | solution.py:313
  28.3 0.0 collective-permute-done.5.rest_4_
  28.3 0.0 collective-permute-done.4.rest_3_
  28.3 0.0 collective-permute-done.3.rest_2_
  28.3 0.0 copy-done.2
  28.3 0.0 copy-done.1
  28.3 0.0 copy-done.4
  28.3 0.0 copy-done.5
  28.3 0.0 copy-done.6
  28.4 2.4 %batch.3 = s16[8,72,256]{2,1,0:T(8,128)(2,1)} custom-call(bf16[512,128]{1,0:T(8,128)(2,1)S(1)} %get-tuple-element.36.cols_ref, f32[8,512]{1,0:T(8,128)S(1)} %get-tuple-element.37.row_ref, bf16[512,100]{1,0:T(8,128)(2,1)S(1)} %get-tuple-element.38.enc_ref, bf16[256,256]{1,0:T(8,128)(2,1)S(1)} %copy-done.4, bf16[256,256]{1,0:T(8,128)(2,1)S(1)} %copy-done.5, ...), custom_call_target="tpu_custom_call" | custom-call | flops 100000000 | bytes 4000000 | tf_op jit(solution)/shard_map/batch/pallas_call | solution.py:379
  30.8 3.7 %all-to-all-start.1 = ((s16[8,72,256]{2,1,0:T(8,128)(2,1)}), s16[8,72,256]{2,1,0:T(8,128)(2,1)S(1)}, u32[]{:S(2)}, u32[]{:S(2)}) async-start(s16[8,72,256]{2,1,0:T(8,128)(2,1)} %batch.3), calls=%async_computation.1 | async-start | bytes 589824 | tf_op jit(solution)/shard_map/all_to_all | solution.py:560
  34.5 2.0 %collective-permute-start.6 = (bf16[4,64,256]{2,1,0:T(8,128)(2,1)S(1)}, bf16[4,64,256]{2,1,0:T(8,128)(2,1)S(1)}, u32[]{:S(2)}, u32[]{:S(2)}) collective-permute-start(bf16[4,64,256]{2,1,0:T(8,128)(2,1)S(1)} %copy-done.14), channel_id=1, source_target_pairs={{0,4},{4,0},{8,12},{12,8},{16,20},{20,16},{24,28},{28,24},{1,5},{5... | collective-permute-start | bytes 393224 | tf_op jit(solution)/shard_map/ppermute | solution.py:208
  36.5 5.9 %collective-permute-done.6.got_ref = bf16[4,64,256]{2,1,0:T(8,128)(2,1)S(1)} collective-permute-done((bf16[4,64,256]{2,1,0:T(8,128)(2,1)S(1)}, bf16[4,64,256]{2,1,0:T(8,128)(2,1)S(1)}, u32[]{:S(2)}, u32[]{:S(2)}) %collective-permute-start.6) | collective-permute-done | bytes 131104 | tf_op jit(solution)/shard_map/ppermute | solution.py:208
  42.4 2.8 %collective-permute-start.7 = (bf16[2,64,256]{2,1,0:T(8,128)(2,1)S(1)}, bf16[2,64,256]{2,1,0:T(8,128)(2,1)S(1)}, u32[]{:S(2)}, u32[]{:S(2)}) collective-permute-start(bf16[2,64,256]{2,1,0:T(8,128)(2,1)S(1)} %get-tuple-element.47), channel_id=1, source_target_pairs={{0,16},{4,20},{8,24},{12,28},{16,0},{20,4},{24,8},{28,12},{1,17},{... | collective-permute-start | bytes 196616 | tf_op jit(solution)/shard_map/ppermute | solution.py:208
  45.3 2.5 %collective-permute-done.7.got_ref = bf16[2,64,256]{2,1,0:T(8,128)(2,1)S(1)} collective-permute-done((bf16[2,64,256]{2,1,0:T(8,128)(2,1)S(1)}, bf16[2,64,256]{2,1,0:T(8,128)(2,1)S(1)}, u32[]{:S(2)}, u32[]{:S(2)}) %collective-permute-start.7) | collective-permute-done | bytes 65568 | tf_op jit(solution)/shard_map/ppermute | solution.py:208
  47.8 1.5 %collective-permute-start.8 = (bf16[1,64,256]{2,1,0:T(8,128)(2,1)S(1)}, bf16[1,64,256]{2,1,0:T(8,128)(2,1)S(1)}, u32[]{:S(2)}, u32[]{:S(2)}) collective-permute-start(bf16[1,64,256]{2,1,0:T(8,128)(2,1)S(1)} %get-tuple-element.49), channel_id=1, source_target_pairs={{0,8},{4,12},{8,0},{12,4},{16,24},{20,28},{24,16},{28,20},{1,9},{5... | collective-permute-start | bytes 98312 | tf_op jit(solution)/shard_map/ppermute | solution.py:208
  49.3 2.5 %collective-permute-done.8.refs_1_ = bf16[1,64,256]{2,1,0:T(8,128)(2,1)S(1)} collective-permute-done((bf16[1,64,256]{2,1,0:T(8,128)(2,1)S(1)}, bf16[1,64,256]{2,1,0:T(8,128)(2,1)S(1)}, u32[]{:S(2)}, u32[]{:S(2)}) %collective-permute-start.8) | collective-permute-done | bytes 32800 | tf_op jit(solution)/shard_map/ppermute | solution.py:208
  51.8 0.0 all-to-all-done.1.refs_2_.rest_0_.counts
  51.8 0.1 next_block.4.rest_0_
  51.9 0.1 collective-permute-start.11
  52.0 1.4 %collective-permute-start.10 = (bf16[64,256]{1,0:T(8,128)(2,1)S(1)}, bf16[64,256]{1,0:T(8,128)(2,1)S(1)}, u32[]{:S(2)}, u32[]{:S(2)}) collective-permute-start(bf16[64,256]{1,0:T(8,128)(2,1)S(1)} %next_block.4.rest_0_), channel_id=1, source_target_pairs={{2,0},{3,1},{0,2},{1,3},{6,4},{7,5},{4,6},{5,7},{10,8},{11,9},{8,1... | collective-permute-start | bytes 98312 | tf_op jit(solution)/shard_map/ppermute | solution.py:51
  53.4 0.5 collective-permute-start.9
  53.9 1.3 %prep.4 = (bf16[512,128]{1,0:T(8,128)(2,1)S(1)}, f32[8,512]{1,0:T(8,128)S(1)}, bf16[512,100]{1,0:T(8,128)(2,1)S(1)}) custom-call(s32[3,3,1,256]{3,2,1,0:T(1,128)S(1)} %copy-done.11, s32[3,3,1,256]{3,2,1,0:T(1,128)S(1)} %collective-permute-done.refs_1_, s32[3,3,1,256]{3,2,1,0:T(1,128)S(1)} %collective-permute-done.1.refs_2_, ...), custom_call_target="tpu_custom_call" | custom-call | flops 100000000 | bytes 1000000 | tf_op jit(solution)/shard_map/prep/pallas_call | solution.py:313
  55.2 0.4 collective-permute-done.11.rest_3_
  55.6 0.4 collective-permute-done.10.rest_2_
  56.0 0.0 collective-permute-done.9.rest_1_
  56.0 2.4 %batch.4 = s16[8,64,256]{2,1,0:T(8,128)(2,1)} custom-call(bf16[512,128]{1,0:T(8,128)(2,1)S(1)} %get-tuple-element.41.cols_ref, f32[8,512]{1,0:T(8,128)S(1)} %get-tuple-element.42.row_ref, bf16[512,100]{1,0:T(8,128)(2,1)S(1)} %get-tuple-element.43.enc_ref, bf16[256,256]{1,0:T(8,128)(2,1)S(1)} %copy-done.4, bf16[256,256]{1,0:T(8,128)(2,1)S(1)} %copy-done.5, ...), custom_call_target="tpu_custom_call" | custom-call | flops 100000000 | bytes 4000000 | tf_op jit(solution)/shard_map/batch/pallas_call | solution.py:379
  58.4 5.6 %all-to-all-start.2 = ((s16[8,64,256]{2,1,0:T(8,128)(2,1)}), s16[8,64,256]{2,1,0:T(8,128)(2,1)S(1)}, u32[]{:S(2)}, u32[]{:S(2)}) async-start(s16[8,64,256]{2,1,0:T(8,128)(2,1)} %batch.4), calls=%async_computation.2 | async-start | bytes 524288 | tf_op jit(solution)/shard_map/all_to_all | solution.py:560
  64.0 2.0 %collective-permute-start.12 = (bf16[4,64,256]{2,1,0:T(8,128)(2,1)S(1)}, bf16[4,64,256]{2,1,0:T(8,128)(2,1)S(1)}, u32[]{:S(2)}, u32[]{:S(2)}) collective-permute-start(bf16[4,64,256]{2,1,0:T(8,128)(2,1)S(1)} %copy-done.13), channel_id=1, source_target_pairs={{0,4},{4,0},{8,12},{12,8},{16,20},{20,16},{24,28},{28,24},{1,5},{5... | collective-permute-start | bytes 393224 | tf_op jit(solution)/shard_map/ppermute | solution.py:208
  66.0 6.0 %collective-permute-done.12.got_ref = bf16[4,64,256]{2,1,0:T(8,128)(2,1)S(1)} collective-permute-done((bf16[4,64,256]{2,1,0:T(8,128)(2,1)S(1)}, bf16[4,64,256]{2,1,0:T(8,128)(2,1)S(1)}, u32[]{:S(2)}, u32[]{:S(2)}) %collective-permute-start.12) | collective-permute-done | bytes 131104 | tf_op jit(solution)/shard_map/ppermute | solution.py:208
  72.1 2.8 %collective-permute-start.13 = (bf16[2,64,256]{2,1,0:T(8,128)(2,1)S(1)}, bf16[2,64,256]{2,1,0:T(8,128)(2,1)S(1)}, u32[]{:S(2)}, u32[]{:S(2)}) collective-permute-start(bf16[2,64,256]{2,1,0:T(8,128)(2,1)S(1)} %get-tuple-element.58), channel_id=1, source_target_pairs={{0,16},{4,20},{8,24},{12,28},{16,0},{20,4},{24,8},{28,12},{1,17},{... | collective-permute-start | bytes 196616 | tf_op jit(solution)/shard_map/ppermute | solution.py:208
  74.8 2.6 %collective-permute-done.13.got_ref = bf16[2,64,256]{2,1,0:T(8,128)(2,1)S(1)} collective-permute-done((bf16[2,64,256]{2,1,0:T(8,128)(2,1)S(1)}, bf16[2,64,256]{2,1,0:T(8,128)(2,1)S(1)}, u32[]{:S(2)}, u32[]{:S(2)}) %collective-permute-start.13) | collective-permute-done | bytes 65568 | tf_op jit(solution)/shard_map/ppermute | solution.py:208
  77.4 1.6 %collective-permute-start.14 = (bf16[1,64,256]{2,1,0:T(8,128)(2,1)S(1)}, bf16[1,64,256]{2,1,0:T(8,128)(2,1)S(1)}, u32[]{:S(2)}, u32[]{:S(2)}) collective-permute-start(bf16[1,64,256]{2,1,0:T(8,128)(2,1)S(1)} %get-tuple-element.60), channel_id=1, source_target_pairs={{0,8},{4,12},{8,0},{12,4},{16,24},{20,28},{24,16},{28,20},{1,9},{5... | collective-permute-start | bytes 98312 | tf_op jit(solution)/shard_map/ppermute | solution.py:208
  79.0 2.4 %collective-permute-done.14.refs_1_ = bf16[1,64,256]{2,1,0:T(8,128)(2,1)S(1)} collective-permute-done((bf16[1,64,256]{2,1,0:T(8,128)(2,1)S(1)}, bf16[1,64,256]{2,1,0:T(8,128)(2,1)S(1)}, u32[]{:S(2)}, u32[]{:S(2)}) %collective-permute-start.14) | collective-permute-done | bytes 32800 | tf_op jit(solution)/shard_map/ppermute | solution.py:208
  81.4 0.0 all-to-all-done.2.rest_1_.refs_3_
  81.4 0.2 next_block.5.rest_0_
  81.7 0.1 collective-permute-start.17
  81.7 1.3 %collective-permute-start.16 = (bf16[64,256]{1,0:T(8,128)(2,1)S(1)}, bf16[64,256]{1,0:T(8,128)(2,1)S(1)}, u32[]{:S(2)}, u32[]{:S(2)}) collective-permute-start(bf16[64,256]{1,0:T(8,128)(2,1)S(1)} %next_block.5.rest_0_), channel_id=1, source_target_pairs={{2,0},{3,1},{0,2},{1,3},{6,4},{7,5},{4,6},{5,7},{10,8},{11,9},{8,1... | collective-permute-start | bytes 98312 | tf_op jit(solution)/shard_map/ppermute | solution.py:51
  83.1 0.5 collective-permute-start.15
  83.6 1.3 %prep.5 = (bf16[512,128]{1,0:T(8,128)(2,1)S(1)}, f32[8,512]{1,0:T(8,128)S(1)}, bf16[512,100]{1,0:T(8,128)(2,1)S(1)}) custom-call(s32[3,3,1,256]{3,2,1,0:T(1,128)S(1)} %copy-done.11, s32[3,3,1,256]{3,2,1,0:T(1,128)S(1)} %collective-permute-done.refs_1_, s32[3,3,1,256]{3,2,1,0:T(1,128)S(1)} %collective-permute-done.1.refs_2_, ...), custom_call_target="tpu_custom_call" | custom-call | flops 100000000 | bytes 1000000 | tf_op jit(solution)/shard_map/prep/pallas_call | solution.py:313
  84.9 0.3 collective-permute-done.17.rest_3_
  85.3 0.5 collective-permute-done.16.rest_2_
  85.7 0.0 collective-permute-done.15.rest_1_
  85.7 2.4 %batch.5 = s16[8,64,256]{2,1,0:T(8,128)(2,1)} custom-call(bf16[512,128]{1,0:T(8,128)(2,1)S(1)} %get-tuple-element.52.cols_ref, f32[8,512]{1,0:T(8,128)S(1)} %get-tuple-element.53.row_ref, bf16[512,100]{1,0:T(8,128)(2,1)S(1)} %get-tuple-element.54.enc_ref, bf16[256,256]{1,0:T(8,128)(2,1)S(1)} %copy-done.4, bf16[256,256]{1,0:T(8,128)(2,1)S(1)} %copy-done.5, ...), custom_call_target="tpu_custom_call" | custom-call | flops 100000000 | bytes 4000000 | tf_op jit(solution)/shard_map/batch/pallas_call | solution.py:379
  88.1 5.8 %all-to-all-start.3 = ((s16[8,64,256]{2,1,0:T(8,128)(2,1)}), s16[8,64,256]{2,1,0:T(8,128)(2,1)S(1)}, u32[]{:S(2)}, u32[]{:S(2)}) async-start(s16[8,64,256]{2,1,0:T(8,128)(2,1)} %batch.5), calls=%async_computation.3 | async-start | bytes 524288 | tf_op jit(solution)/shard_map/all_to_all | solution.py:560
  93.9 0.0 copy-done
  93.9 2.4 %settle.1 = (f32[16,64,256]{2,1,0:T(8,128)}, f32[8,64,256]{2,1,0:T(8,128)S(1)}) custom-call(s32[3,1,8]{2,1,0:T(1,128)S(1)} %bitcast.12, f32[16,64,256]{2,1,0:T(8,128)S(1)} %bitcast.10, s16[8,72,256]{2,1,0:T(8,128)(2,1)S(1)} %all-to-all-done.1.refs_2_.rest_0_.counts, s16[8,64,256]{2,1,0:T(8,128)(2,1)S(1)} %all-to-all-done.2.rest_1_.refs_3_), custom_call_target="tpu_custom_call" | custom-call | flops 20000000 | bytes 3000000 | tf_op jit(solution)/shard_map/settle/pallas_call | solution.py:496
  96.3 6.8 %all-to-all-done.3.delta = s16[8,64,256]{2,1,0:T(8,128)(2,1)S(1)} async-done(((s16[8,64,256]{2,1,0:T(8,128)(2,1)}), s16[8,64,256]{2,1,0:T(8,128)(2,1)S(1)}, u32[]{:S(2)}, u32[]{:S(2)}) %all-to-all-start.3) | async-done | bytes 262176 | tf_op jit(solution)/shard_map/all_to_all | solution.py:560
  103.1 0.2 finish.1
  (26 shorter events, 0.2 us)
Async XLA Ops:
  3.3 16.6 %copy-start.3 = (f32[64,128]{1,0:T(8,128)S(1)}, f32[64,128]{1,0:T(8,128)}, u32[]{:S(2)}) copy-start(f32[64,128]{1,0:T(8,128)} %get-tuple-element.33.plan_ref) | copy-start | bytes 98308
  3.3 18.6 %copy-start.11 = (s32[3,3,1,256]{3,2,1,0:T(1,128)S(1)}, s32[3,3,1,256]{3,2,1,0:T(1,128)}, u32[]{:S(2)}) copy-start(s32[3,3,1,256]{3,2,1,0:T(1,128)} %get-tuple-element.34.refs_0_) | copy-start | bytes 27652
  3.3 21.8 %copy-start.12 = (f32[768]{0:T(1024)S(1)}, f32[768]{0:T(1024)}, u32[]{:S(2)}) copy-start(f32[768]{0:T(1024)} %param.27) | copy-start | bytes 9220
  3.3 23.2 %copy-start.9 = (f32[1,512]{1,0:T(1,128)S(1)}, f32[1,512]{1,0:T(1,128)}, u32[]{:S(2)}) copy-start(f32[1,512]{1,0:T(1,128)} %get-tuple-element.35.refs_4_.small_ref) | copy-start | bytes 6148
  3.4 24.9 %copy-start.2 = (bf16[256,768]{1,0:T(8,128)(2,1)S(1)}, bf16[256,768]{1,0:T(8,128)(2,1)}, u32[]{:S(2)}) copy-start(bf16[256,768]{1,0:T(8,128)(2,1)} %wh_ref.5) | copy-start | bytes 1179652
  20.0 8.4 %copy-start.1 = (bf16[256,768]{1,0:T(8,128)(2,1)S(1)}, bf16[256,768]{1,0:T(8,128)(2,1)}, u32[]{:S(2)}) copy-start(bf16[256,768]{1,0:T(8,128)(2,1)} %wi_ref.5) | copy-start | bytes 1179652
  20.0 8.3 %collective-permute-start.5 = (bf16[64,256]{1,0:T(8,128)(2,1)S(1)}, bf16[64,256]{1,0:T(8,128)(2,1)S(1)}, u32[]{:S(2)}, u32[]{:S(2)}) collective-permute-start(bf16[64,256]{1,0:T(8,128)(2,1)S(1)} %next_block.3.rest_1_), channel_id=1, source_target_pairs={{3,0},{2,1},{1,2},{0,3},{7,4},{6,5},{5,6},{4,7},{11,8},{10,9},{9,1... | collective-permute-start | bytes 98312 | tf_op jit(solution)/shard_map/ppermute | solution.py:51
  20.1 8.2 %collective-permute-start.4 = (bf16[64,256]{1,0:T(8,128)(2,1)S(1)}, bf16[64,256]{1,0:T(8,128)(2,1)S(1)}, u32[]{:S(2)}, u32[]{:S(2)}) collective-permute-start(bf16[64,256]{1,0:T(8,128)(2,1)S(1)} %next_block.3.rest_1_), channel_id=1, source_target_pairs={{2,0},{3,1},{0,2},{1,3},{6,4},{7,5},{4,6},{5,7},{10,8},{11,9},{8,1... | collective-permute-start | bytes 98312 | tf_op jit(solution)/shard_map/ppermute | solution.py:51
  21.5 6.8 %collective-permute-start.3 = (bf16[64,256]{1,0:T(8,128)(2,1)S(1)}, bf16[64,256]{1,0:T(8,128)(2,1)S(1)}, u32[]{:S(2)}, u32[]{:S(2)}) collective-permute-start(bf16[64,256]{1,0:T(8,128)(2,1)S(1)} %next_block.3.rest_1_), channel_id=1, source_target_pairs={{1,0},{0,1},{3,2},{2,3},{5,4},{4,5},{7,6},{6,7},{9,8},{8,9},{11,10... | collective-permute-start | bytes 98312 | tf_op jit(solution)/shard_map/ppermute | solution.py:51
  21.9 3.1 %collective-permute-start.2 = (s32[3,3,1,256]{3,2,1,0:T(1,128)S(1)}, s32[3,3,1,256]{3,2,1,0:T(1,128)S(1)}, u32[]{:S(2)}, u32[]{:S(2)}) collective-permute-start(s32[3,3,1,256]{3,2,1,0:T(1,128)S(1)} %copy-done.11), channel_id=1, source_target_pairs={{3,0},{2,1},{1,2},{0,3},{7,4},{6,5},{5,6},{4,7},{11,8},{10,9},{9,1... | collective-permute-start | bytes 27656 | tf_op jit(solution)/shard_map/ppermute | solution.py:51
  22.9 3.7 %collective-permute-start.1 = (s32[3,3,1,256]{3,2,1,0:T(1,128)S(1)}, s32[3,3,1,256]{3,2,1,0:T(1,128)S(1)}, u32[]{:S(2)}, u32[]{:S(2)}) collective-permute-start(s32[3,3,1,256]{3,2,1,0:T(1,128)S(1)} %copy-done.11), channel_id=1, source_target_pairs={{2,0},{3,1},{0,2},{1,3},{6,4},{7,5},{4,6},{5,7},{10,8},{11,9},{8,1... | collective-permute-start | bytes 27656 | tf_op jit(solution)/shard_map/ppermute | solution.py:51
  25.0 1.5 %collective-permute-start = (s32[3,3,1,256]{3,2,1,0:T(1,128)S(1)}, s32[3,3,1,256]{3,2,1,0:T(1,128)S(1)}, u32[]{:S(2)}, u32[]{:S(2)}) collective-permute-start(s32[3,3,1,256]{3,2,1,0:T(1,128)S(1)} %copy-done.11), channel_id=1, source_target_pairs={{1,0},{0,1},{3,2},{2,3},{5,4},{4,5},{7,6},{6,7},{9,8},{8,9},{11,10... | collective-permute-start | bytes 27656 | tf_op jit(solution)/shard_map/ppermute | solution.py:51
  26.5 1.8 %copy-start.4 = (bf16[256,256]{1,0:T(8,128)(2,1)S(1)}, bf16[256,256]{1,0:T(8,128)(2,1)}, u32[]{:S(2)}) copy-start(bf16[256,256]{1,0:T(8,128)(2,1)} %ws_ref.5) | copy-start | bytes 393220
  26.5 1.8 %copy-start.5 = (bf16[256,256]{1,0:T(8,128)(2,1)S(1)}, bf16[256,256]{1,0:T(8,128)(2,1)}, u32[]{:S(2)}) copy-start(bf16[256,256]{1,0:T(8,128)(2,1)} %wo_ref.5) | copy-start | bytes 393220
  26.5 1.8 %copy-start.6 = (bf16[100,256]{1,0:T(8,128)(2,1)S(1)}, bf16[100,256]{1,0:T(8,128)(2,1)}, u32[]{:S(2)}) copy-start(bf16[100,256]{1,0:T(8,128)(2,1)} %wt_ref.5) | copy-start | bytes 153604
  30.7 3.7 %copy-start.14 = (bf16[4,64,256]{2,1,0:T(8,128)(2,1)S(1)}, bf16[4,64,256]{2,1,0:T(8,128)(2,1)}, u32[]{:S(2)}) copy-start(bf16[4,64,256]{2,1,0:T(8,128)(2,1)} %get-tuple-element.45) | copy-start | bytes 393220
  30.7 11.7 %copy-start.8 = (bf16[4,64,256]{2,1,0:T(8,128)(2,1)S(1)}, bf16[4,64,256]{2,1,0:T(8,128)(2,1)}, u32[]{:S(2)}) copy-start(bf16[4,64,256]{2,1,0:T(8,128)(2,1)} %get-tuple-element.44.keep_in) | copy-start | bytes 393220
  30.8 21.1 %all-to-all-start.1 = ((s16[8,72,256]{2,1,0:T(8,128)(2,1)}), s16[8,72,256]{2,1,0:T(8,128)(2,1)S(1)}, u32[]{:S(2)}, u32[]{:S(2)}) async-start(s16[8,72,256]{2,1,0:T(8,128)(2,1)} %batch.3), calls=%async_computation.1 | async-start | bytes 589824 | tf_op jit(solution)/shard_map/all_to_all | solution.py:560
  34.5 7.9 %collective-permute-start.6 = (bf16[4,64,256]{2,1,0:T(8,128)(2,1)S(1)}, bf16[4,64,256]{2,1,0:T(8,128)(2,1)S(1)}, u32[]{:S(2)}, u32[]{:S(2)}) collective-permute-start(bf16[4,64,256]{2,1,0:T(8,128)(2,1)S(1)} %copy-done.14), channel_id=1, source_target_pairs={{0,4},{4,0},{8,12},{12,8},{16,20},{20,16},{24,28},{28,24},{1,5},{5... | collective-permute-start | bytes 393224 | tf_op jit(solution)/shard_map/ppermute | solution.py:208
  42.4 5.4 %collective-permute-start.7 = (bf16[2,64,256]{2,1,0:T(8,128)(2,1)S(1)}, bf16[2,64,256]{2,1,0:T(8,128)(2,1)S(1)}, u32[]{:S(2)}, u32[]{:S(2)}) collective-permute-start(bf16[2,64,256]{2,1,0:T(8,128)(2,1)S(1)} %get-tuple-element.47), channel_id=1, source_target_pairs={{0,16},{4,20},{8,24},{12,28},{16,0},{20,4},{24,8},{28,12},{1,17},{... | collective-permute-start | bytes 196616 | tf_op jit(solution)/shard_map/ppermute | solution.py:208
  47.8 4.0 %collective-permute-start.8 = (bf16[1,64,256]{2,1,0:T(8,128)(2,1)S(1)}, bf16[1,64,256]{2,1,0:T(8,128)(2,1)S(1)}, u32[]{:S(2)}, u32[]{:S(2)}) collective-permute-start(bf16[1,64,256]{2,1,0:T(8,128)(2,1)S(1)} %get-tuple-element.49), channel_id=1, source_target_pairs={{0,8},{4,12},{8,0},{12,4},{16,24},{20,28},{24,16},{28,20},{1,9},{5... | collective-permute-start | bytes 98312 | tf_op jit(solution)/shard_map/ppermute | solution.py:208
  51.9 3.6 %collective-permute-start.11 = (bf16[64,256]{1,0:T(8,128)(2,1)S(1)}, bf16[64,256]{1,0:T(8,128)(2,1)S(1)}, u32[]{:S(2)}, u32[]{:S(2)}) collective-permute-start(bf16[64,256]{1,0:T(8,128)(2,1)S(1)} %next_block.4.rest_0_), channel_id=1, source_target_pairs={{3,0},{2,1},{1,2},{0,3},{7,4},{6,5},{5,6},{4,7},{11,8},{10,9},{9,1... | collective-permute-start | bytes 98312 | tf_op jit(solution)/shard_map/ppermute | solution.py:51
  52.0 4.0 %collective-permute-start.10 = (bf16[64,256]{1,0:T(8,128)(2,1)S(1)}, bf16[64,256]{1,0:T(8,128)(2,1)S(1)}, u32[]{:S(2)}, u32[]{:S(2)}) collective-permute-start(bf16[64,256]{1,0:T(8,128)(2,1)S(1)} %next_block.4.rest_0_), channel_id=1, source_target_pairs={{2,0},{3,1},{0,2},{1,3},{6,4},{7,5},{4,6},{5,7},{10,8},{11,9},{8,1... | collective-permute-start | bytes 98312 | tf_op jit(solution)/shard_map/ppermute | solution.py:51
  53.4 2.6 %collective-permute-start.9 = (bf16[64,256]{1,0:T(8,128)(2,1)S(1)}, bf16[64,256]{1,0:T(8,128)(2,1)S(1)}, u32[]{:S(2)}, u32[]{:S(2)}) collective-permute-start(bf16[64,256]{1,0:T(8,128)(2,1)S(1)} %next_block.4.rest_0_), channel_id=1, source_target_pairs={{1,0},{0,1},{3,2},{2,3},{5,4},{4,5},{7,6},{6,7},{9,8},{8,9},{11,10... | collective-permute-start | bytes 98312 | tf_op jit(solution)/shard_map/ppermute | solution.py:51
  58.4 5.6 %copy-start.13 = (bf16[4,64,256]{2,1,0:T(8,128)(2,1)S(1)}, bf16[4,64,256]{2,1,0:T(8,128)(2,1)}, u32[]{:S(2)}) copy-start(bf16[4,64,256]{2,1,0:T(8,128)(2,1)} %get-tuple-element.56) | copy-start | bytes 393220
  58.4 13.6 %copy-start.7 = (bf16[4,64,256]{2,1,0:T(8,128)(2,1)S(1)}, bf16[4,64,256]{2,1,0:T(8,128)(2,1)}, u32[]{:S(2)}) copy-start(bf16[4,64,256]{2,1,0:T(8,128)(2,1)} %get-tuple-element.55.keep_in) | copy-start | bytes 393220
  58.4 23.0 %all-to-all-start.2 = ((s16[8,64,256]{2,1,0:T(8,128)(2,1)}), s16[8,64,256]{2,1,0:T(8,128)(2,1)S(1)}, u32[]{:S(2)}, u32[]{:S(2)}) async-start(s16[8,64,256]{2,1,0:T(8,128)(2,1)} %batch.4), calls=%async_computation.2 | async-start | bytes 524288 | tf_op jit(solution)/shard_map/all_to_all | solution.py:560
  64.0 8.0 %collective-permute-start.12 = (bf16[4,64,256]{2,1,0:T(8,128)(2,1)S(1)}, bf16[4,64,256]{2,1,0:T(8,128)(2,1)S(1)}, u32[]{:S(2)}, u32[]{:S(2)}) collective-permute-start(bf16[4,64,256]{2,1,0:T(8,128)(2,1)S(1)} %copy-done.13), channel_id=1, source_target_pairs={{0,4},{4,0},{8,12},{12,8},{16,20},{20,16},{24,28},{28,24},{1,5},{5... | collective-permute-start | bytes 393224 | tf_op jit(solution)/shard_map/ppermute | solution.py:208
  72.1 5.3 %collective-permute-start.13 = (bf16[2,64,256]{2,1,0:T(8,128)(2,1)S(1)}, bf16[2,64,256]{2,1,0:T(8,128)(2,1)S(1)}, u32[]{:S(2)}, u32[]{:S(2)}) collective-permute-start(bf16[2,64,256]{2,1,0:T(8,128)(2,1)S(1)} %get-tuple-element.58), channel_id=1, source_target_pairs={{0,16},{4,20},{8,24},{12,28},{16,0},{20,4},{24,8},{28,12},{1,17},{... | collective-permute-start | bytes 196616 | tf_op jit(solution)/shard_map/ppermute | solution.py:208
  77.4 4.0 %collective-permute-start.14 = (bf16[1,64,256]{2,1,0:T(8,128)(2,1)S(1)}, bf16[1,64,256]{2,1,0:T(8,128)(2,1)S(1)}, u32[]{:S(2)}, u32[]{:S(2)}) collective-permute-start(bf16[1,64,256]{2,1,0:T(8,128)(2,1)S(1)} %get-tuple-element.60), channel_id=1, source_target_pairs={{0,8},{4,12},{8,0},{12,4},{16,24},{20,28},{24,16},{28,20},{1,9},{5... | collective-permute-start | bytes 98312 | tf_op jit(solution)/shard_map/ppermute | solution.py:208
  81.7 3.6 %collective-permute-start.17 = (bf16[64,256]{1,0:T(8,128)(2,1)S(1)}, bf16[64,256]{1,0:T(8,128)(2,1)S(1)}, u32[]{:S(2)}, u32[]{:S(2)}) collective-permute-start(bf16[64,256]{1,0:T(8,128)(2,1)S(1)} %next_block.5.rest_0_), channel_id=1, source_target_pairs={{3,0},{2,1},{1,2},{0,3},{7,4},{6,5},{5,6},{4,7},{11,8},{10,9},{9,1... | collective-permute-start | bytes 98312 | tf_op jit(solution)/shard_map/ppermute | solution.py:51
  81.7 4.0 %collective-permute-start.16 = (bf16[64,256]{1,0:T(8,128)(2,1)S(1)}, bf16[64,256]{1,0:T(8,128)(2,1)S(1)}, u32[]{:S(2)}, u32[]{:S(2)}) collective-permute-start(bf16[64,256]{1,0:T(8,128)(2,1)S(1)} %next_block.5.rest_0_), channel_id=1, source_target_pairs={{2,0},{3,1},{0,2},{1,3},{6,4},{7,5},{4,6},{5,7},{10,8},{11,9},{8,1... | collective-permute-start | bytes 98312 | tf_op jit(solution)/shard_map/ppermute | solution.py:51
  83.1 2.6 %collective-permute-start.15 = (bf16[64,256]{1,0:T(8,128)(2,1)S(1)}, bf16[64,256]{1,0:T(8,128)(2,1)S(1)}, u32[]{:S(2)}, u32[]{:S(2)}) collective-permute-start(bf16[64,256]{1,0:T(8,128)(2,1)S(1)} %next_block.5.rest_0_), channel_id=1, source_target_pairs={{1,0},{0,1},{3,2},{2,3},{5,4},{4,5},{7,6},{6,7},{9,8},{8,9},{11,10... | collective-permute-start | bytes 98312 | tf_op jit(solution)/shard_map/ppermute | solution.py:51
  85.7 8.1 %copy-start = (f32[1024,256]{1,0:T(8,128)S(1)}, f32[1024,256]{1,0:T(8,128)}, u32[]{:S(2)}) copy-start(f32[1024,256]{1,0:T(8,128)} %param.14) | copy-start | bytes 3145732
  88.1 5.8 %copy-start.10 = (s32[8,3,1]{0,2,1:T(1,128)S(1)}, s32[8,3,1]{0,2,1:T(1,128)}, u32[]{:S(2)}) copy-start(s32[8,3,1]{0,2,1:T(1,128)} %param.18) | copy-start | bytes 292
  88.1 15.0 %all-to-all-start.3 = ((s16[8,64,256]{2,1,0:T(8,128)(2,1)}), s16[8,64,256]{2,1,0:T(8,128)(2,1)S(1)}, u32[]{:S(2)}, u32[]{:S(2)}) async-start(s16[8,64,256]{2,1,0:T(8,128)(2,1)} %batch.5), calls=%async_computation.3 | async-start | bytes 524288 | tf_op jit(solution)/shard_map/all_to_all | solution.py:560

commit v3 on v1

--- a/solution.py
+++ b/solution.py
@@ -227,7 +227,7 @@
 
 def prep_kernel(b, shards, *refs):
     idx, refs = refs[:shards], refs[shards:]
-    small_ref, cols_ref, row_ref, enc_ref, *tally_ref, pack = refs
+    small_ref, cols_ref, row_ref, enc_ref, pack = refs
     me = lax.axis_index("shard")
     entries = cols_ref.shape[0]
     lines = pack.shape[0]
@@ -273,32 +273,47 @@
     time = cols[:, 3:4] + 256.0 * cols[:, 4:5]
     width = enc_ref.shape[1]
     enc_ref[...] = cosine(time * small_ref[:, :width] + small_ref[:, LANES : LANES + width]).astype(jnp.bfloat16)
-    if tally_ref:
-        width = tally_ref[0].shape[1]
-        line = lax.broadcasted_iota(jnp.int32, (COUNT_ROWS, LANES), 0)
-        local = lax.broadcasted_iota(jnp.int32, (LANES, LANES), 0)
-        tally = jnp.zeros((COUNT_ROWS, LANES), jnp.float32)
-        for e in range(idx[0].shape[1]):
-            rows, _, _ = own_and_other(idx, e)
-            rows = rows - me * BLK
-            hits = jnp.zeros((LANES, LANES), jnp.float32)
-            for r in range(lines):
-                hits = hits + jnp.where(rows[r : r + 1, :] == local, 1.0, 0.0)
-            count = bdot(jnp.ones((COUNT_ROWS, LANES), jnp.bfloat16), hits.astype(jnp.bfloat16), NT)
-            tally = jnp.where(line == e, count, tally)
-        tally = jnp.concatenate([tally] * (width // LANES), 1)
-        tally_ref[0][...] = tally.astype(jnp.int32).astype(jnp.int16)
-
-
-def prep(b, idx, small, encoded, entries, width):
+
+
+def tally_kernel(shards, *refs):
+    idx, tally_ref = refs[:shards], refs[shards]
+    me = lax.axis_index("shard")
+    width = tally_ref.shape[1]
+    lines = 2 * shards * idx[0].shape[3] // LANES
+    line = lax.broadcasted_iota(jnp.int32, (COUNT_ROWS, LANES), 0)
+    local = lax.broadcasted_iota(jnp.int32, (LANES, LANES), 0)
+    tally = jnp.zeros((COUNT_ROWS, LANES), jnp.float32)
+    for e in range(idx[0].shape[1]):
+        rows, _, _ = own_and_other(idx, e)
+        rows = rows - me * BLK
+        hits = jnp.zeros((LANES, LANES), jnp.float32)
+        for r in range(lines):
+            hits = hits + jnp.where(rows[r : r + 1, :] == local, 1.0, 0.0)
+        count = bdot(jnp.ones((COUNT_ROWS, LANES), jnp.bfloat16), hits.astype(jnp.bfloat16), NT)
+        tally = jnp.where(line == e, count, tally)
+    tally = jnp.concatenate([tally] * (width // LANES), 1)
+    tally_ref[...] = tally.astype(jnp.int32).astype(jnp.int16)
+
+
+def tallies(idx, width):
+    return pl.pallas_call(
+        functools.partial(tally_kernel, len(idx)),
+        out_shape=jax.ShapeDtypeStruct((COUNT_ROWS, width), jnp.int16),
+        in_specs=[VMEM] * len(idx),
+        out_specs=VMEM,
+        compiler_params=ROOM,
+        cost_estimate=pl.CostEstimate(flops=10_000_000, bytes_accessed=100_000, transcendentals=0),
+        name="tallies",
+    )(*idx)
+
+
+def prep(b, idx, small, encoded, entries):
     lines = 2 * len(idx) * idx[0].shape[3] // LANES
     out = [
         jax.ShapeDtypeStruct((entries, LANES), jnp.bfloat16),
         jax.ShapeDtypeStruct((8, entries), jnp.float32),
         jax.ShapeDtypeStruct((entries, encoded), jnp.bfloat16),
     ]
-    if b == 0:
-        out.append(jax.ShapeDtypeStruct((COUNT_ROWS, width), jnp.int16))
     return pl.pallas_call(
         functools.partial(prep_kernel, b, len(idx)),
         out_shape=out,
@@ -580,11 +595,11 @@
     starts = [(exchange(sent),)]
     starts += [cube(b, groups, rows, plan, *halves[b - 1]) for b in range(1, batches)]
     idx = share(idx, shards)
-    entry, counts = [], ()
+    entry = []
+    counts = (tallies(idx, width),)
     for b in range(batches):
-        out = prep(b, idx, small, frequency.shape[0], entries, width)
-        entry.append(out[:3])
-        counts = counts or out[3:]
+        out = prep(b, idx, small, frequency.shape[0], entries)
+        entry.append(out)
     deltas = []
     for b in range(batches):
         block = next_block(b, groups, rows, plan, starts[b], deltas)

time: 104 us -> 104 us (level)
  no operation moved by 1% of the time
where the time goes in v3:
time: 104 us; the launch traced here: 103 us
  starting transfers between devices  35.4 us (34%)
  waiting for transfers between devices  33 us (32%)
  Pallas kernels  18.1 us (17%)
  blocking collectives  16.6 us (16%)
    ppermute x6, waiting for transfers between devices, cube(): got = lax.ppermute(send, 'rep', [(i, i ^ 1 << bit) for i in range(groups)])  21.8 us
    all_to_all x1, blocking collectives, exchange(): return lax.all_to_all(x, 'rep', split_axis=0, concat_axis=0, tiled=True)  16.6 us
    all_to_all x3, starting transfers between devices, exchange(): return lax.all_to_all(x, 'rep', split_axis=0, concat_axis=0, tiled=True)  15.1 us
    ppermute x6, starting transfers between devices, cube(): got = lax.ppermute(send, 'rep', [(i, i ^ 1 << bit) for i in range(groups)])  12.7 us
    ppermute x12, starting transfers between devices, share(): lax.ppermute(block, 'shard', [(partner(i, k, n), i) for i in range(n)])  7.54 us
    pallas_call x3, Pallas kernels, batch_step(): pl.pallas_call(functools.partial(batch_kernel, len(blocks), len(counts)),...  7.15 us
    all_to_all x3, waiting for transfers between devices, exchange(): return lax.all_to_all(x, 'rep', split_axis=0, concat_axis=0, tiled=True)  6.76 us
    ppermute x12, waiting for transfers between devices, share(): lax.ppermute(block, 'shard', [(partner(i, k, n), i) for i in range(n)])  4.41 us
  transfers between devices with their start and end apart: 21, of which 13 were waited for; matrix products, arithmetic and copies ran while one was open for 0% of the time, Pallas kernels for 7%

profile of v3, /device:TPU:0, one launch (start us, length us, event | category | flops | bytes accessed | tf_op | source)
XLA Modules:
  0.0 103.4 jit_solution(3701506354006589447)
XLA Ops:
  0.0 3.3 %pick.1 = (bf16[8,64,256]{2,1,0:T(8,128)(2,1)}, s32[3,3,1,256]{3,2,1,0:T(1,128)}, f32[1,512]{1,0:T(1,128)}, f32[64,128]{1,0:T(8,128)}, bf16[4,64,256]{2,1,0:T(8,...) custom-call(s32[3,1,8]{2,1,0:T(1,128)} %bitcast.11, ...), custom_call_target="tpu_custom_call" | custom-call | flops 20000000 | bytes 1000000 | tf_op jit(solution)/shard_map/pick/pallas_call | solution.py:145
  3.3 0.0 copy-start.3
  3.3 0.0 copy-start.12
  3.3 0.0 copy-start.9
  3.4 0.0 copy-start.2
  3.4 16.6 %all_to_all.20.refs_0_ = bf16[8,64,256]{2,1,0:T(8,128)(2,1)S(1)} all-to-all(bf16[8,64,256]{2,1,0:T(8,128)(2,1)} %get-tuple-element.38), channel_id=1, replica_groups=mesh['rep'=8,'shard'=4] {'rep'}, dimensions={0} | all-to-all | bytes 524288 | tf_op jit(solution)/shard_map/all_to_all | solution.py:564
  20.0 0.1 collective-permute-start.5
  20.1 1.4 %collective-permute-start.4 = (bf16[64,256]{1,0:T(8,128)(2,1)S(1)}, bf16[64,256]{1,0:T(8,128)(2,1)S(1)}, u32[]{:S(2)}, u32[]{:S(2)}) collective-permute-start(bf16[64,256]{1,0:T(8,128)(2,1)S(1)} %next_block.3.rest_1_), channel_id=1, source_target_pairs={{2,0},{3,1},{0,2},{1,3},{6,4},{7,5},{4,6},{5,7},{10,8},{11,9},{8,1... | collective-permute-start | bytes 98312 | tf_op jit(solution)/shard_map/ppermute | solution.py:40
  21.5 0.5 collective-permute-start.3
  21.9 0.9 collective-permute-start.2
  22.9 0.8 collective-permute-start.1
  23.6 1.4 %collective-permute-done.2.refs_3_ = s32[3,3,1,256]{3,2,1,0:T(1,128)S(1)} collective-permute-done((s32[3,3,1,256]{3,2,1,0:T(1,128)S(1)}, s32[3,3,1,256]{3,2,1,0:T(1,128)S(1)}, u32[]{:S(2)}, u32[]{:S(2)}) %collective-permute-start.2) | collective-permute-done | bytes 9248 | tf_op jit(solution)/shard_map/ppermute | solution.py:40
  25.0 0.1 collective-permute-start
  25.1 0.0 copy-done.12
  25.1 1.4 %collective-permute-done.1.refs_2_ = s32[3,3,1,256]{3,2,1,0:T(1,128)S(1)} collective-permute-done((s32[3,3,1,256]{3,2,1,0:T(1,128)S(1)}, s32[3,3,1,256]{3,2,1,0:T(1,128)S(1)}, u32[]{:S(2)}, u32[]{:S(2)}) %collective-permute-start.1) | collective-permute-done | bytes 9248 | tf_op jit(solution)/shard_map/ppermute | solution.py:40
  26.5 0.0 collective-permute-done.refs_1_
  26.5 0.5 tallies.1.rest_0_
  27.0 0.0 copy-start.6
  27.0 1.3 %prep.3 = (bf16[512,128]{1,0:T(8,128)(2,1)S(1)}, f32[8,512]{1,0:T(8,128)S(1)}, bf16[512,100]{1,0:T(8,128)(2,1)S(1)}) custom-call(s32[3,3,1,256]{3,2,1,0:T(1,128)S(1)} %copy-done.10, s32[3,3,1,256]{3,2,1,0:T(1,128)S(1)} %collective-permute-done.refs_1_, s32[3,3,1,256]{3,2,1,0:T(1,128)S(1)} %collective-permute-done.1.refs_2_, ...), custom_call_target="tpu_custom_call" | custom-call | flops 100000000 | bytes 1000000 | tf_op jit(solution)/shard_map/prep/pallas_call | solution.py:317
  28.3 0.0 collective-permute-done.5.rest_4_
  28.4 0.0 collective-permute-done.4.rest_3_
  28.4 0.0 collective-permute-done.3.rest_2_
  28.4 2.4 %batch.3 = s16[8,72,256]{2,1,0:T(8,128)(2,1)} custom-call(bf16[512,128]{1,0:T(8,128)(2,1)S(1)} %get-tuple-element.35.cols_ref, f32[8,512]{1,0:T(8,128)S(1)} %get-tuple-element.36.row_ref, bf16[512,100]{1,0:T(8,128)(2,1)S(1)} %get-tuple-element.37.enc_ref, bf16[256,256]{1,0:T(8,128)(2,1)S(1)} %copy-done.4, bf16[256,256]{1,0:T(8,128)(2,1)S(1)} %copy-done.5, ...), custom_call_target="tpu_custom_call" | custom-call | flops 100000000 | bytes 4000000 | tf_op jit(solution)/shard_map/batch/pallas_call | solution.py:383
  30.8 3.7 %all-to-all-start.1 = ((s16[8,72,256]{2,1,0:T(8,128)(2,1)}), s16[8,72,256]{2,1,0:T(8,128)(2,1)S(1)}, u32[]{:S(2)}, u32[]{:S(2)}) async-start(s16[8,72,256]{2,1,0:T(8,128)(2,1)} %batch.3), calls=%async_computation.1 | async-start | bytes 589824 | tf_op jit(solution)/shard_map/all_to_all | solution.py:564
  34.5 0.0 copy-done.14
  34.6 2.0 %collective-permute-start.6 = (bf16[4,64,256]{2,1,0:T(8,128)(2,1)S(1)}, bf16[4,64,256]{2,1,0:T(8,128)(2,1)S(1)}, u32[]{:S(2)}, u32[]{:S(2)}) collective-permute-start(bf16[4,64,256]{2,1,0:T(8,128)(2,1)S(1)} %copy-done.14), channel_id=1, source_target_pairs={{0,4},{4,0},{8,12},{12,8},{16,20},{20,16},{24,28},{28,24},{1,5},{5... | collective-permute-start | bytes 393224 | tf_op jit(solution)/shard_map/ppermute | solution.py:197
  36.6 5.9 %collective-permute-done.6.got_ref = bf16[4,64,256]{2,1,0:T(8,128)(2,1)S(1)} collective-permute-done((bf16[4,64,256]{2,1,0:T(8,128)(2,1)S(1)}, bf16[4,64,256]{2,1,0:T(8,128)(2,1)S(1)}, u32[]{:S(2)}, u32[]{:S(2)}) %collective-permute-start.6) | collective-permute-done | bytes 131104 | tf_op jit(solution)/shard_map/ppermute | solution.py:197
  42.5 0.0 copy-done.8
  42.5 2.8 %collective-permute-start.7 = (bf16[2,64,256]{2,1,0:T(8,128)(2,1)S(1)}, bf16[2,64,256]{2,1,0:T(8,128)(2,1)S(1)}, u32[]{:S(2)}, u32[]{:S(2)}) collective-permute-start(bf16[2,64,256]{2,1,0:T(8,128)(2,1)S(1)} %get-tuple-element.45), channel_id=1, source_target_pairs={{0,16},{4,20},{8,24},{12,28},{16,0},{20,4},{24,8},{28,12},{1,17},{... | collective-permute-start | bytes 196616 | tf_op jit(solution)/shard_map/ppermute | solution.py:197
  45.4 2.5 %collective-permute-done.7.got_ref = bf16[2,64,256]{2,1,0:T(8,128)(2,1)S(1)} collective-permute-done((bf16[2,64,256]{2,1,0:T(8,128)(2,1)S(1)}, bf16[2,64,256]{2,1,0:T(8,128)(2,1)S(1)}, u32[]{:S(2)}, u32[]{:S(2)}) %collective-permute-start.7) | collective-permute-done | bytes 65568 | tf_op jit(solution)/shard_map/ppermute | solution.py:197
  47.9 1.5 %collective-permute-start.8 = (bf16[1,64,256]{2,1,0:T(8,128)(2,1)S(1)}, bf16[1,64,256]{2,1,0:T(8,128)(2,1)S(1)}, u32[]{:S(2)}, u32[]{:S(2)}) collective-permute-start(bf16[1,64,256]{2,1,0:T(8,128)(2,1)S(1)} %get-tuple-element.47), channel_id=1, source_target_pairs={{0,8},{4,12},{8,0},{12,4},{16,24},{20,28},{24,16},{28,20},{1,9},{5... | collective-permute-start | bytes 98312 | tf_op jit(solution)/shard_map/ppermute | solution.py:197
  49.4 2.5 %collective-permute-done.8.refs_1_ = bf16[1,64,256]{2,1,0:T(8,128)(2,1)S(1)} collective-permute-done((bf16[1,64,256]{2,1,0:T(8,128)(2,1)S(1)}, bf16[1,64,256]{2,1,0:T(8,128)(2,1)S(1)}, u32[]{:S(2)}, u32[]{:S(2)}) %collective-permute-start.8) | collective-permute-done | bytes 32800 | tf_op jit(solution)/shard_map/ppermute | solution.py:197
  51.9 0.0 all-to-all-done.1.refs_2_.rest_0_.counts
  51.9 0.1 next_block.4.rest_0_
  52.0 0.1 collective-permute-start.11
  52.1 1.4 %collective-permute-start.10 = (bf16[64,256]{1,0:T(8,128)(2,1)S(1)}, bf16[64,256]{1,0:T(8,128)(2,1)S(1)}, u32[]{:S(2)}, u32[]{:S(2)}) collective-permute-start(bf16[64,256]{1,0:T(8,128)(2,1)S(1)} %next_block.4.rest_0_), channel_id=1, source_target_pairs={{2,0},{3,1},{0,2},{1,3},{6,4},{7,5},{4,6},{5,7},{10,8},{11,9},{8,1... | collective-permute-start | bytes 98312 | tf_op jit(solution)/shard_map/ppermute | solution.py:40
  53.5 0.5 collective-permute-start.9
  54.0 1.3 %prep.4 = (bf16[512,128]{1,0:T(8,128)(2,1)S(1)}, f32[8,512]{1,0:T(8,128)S(1)}, bf16[512,100]{1,0:T(8,128)(2,1)S(1)}) custom-call(s32[3,3,1,256]{3,2,1,0:T(1,128)S(1)} %copy-done.10, s32[3,3,1,256]{3,2,1,0:T(1,128)S(1)} %collective-permute-done.refs_1_, s32[3,3,1,256]{3,2,1,0:T(1,128)S(1)} %collective-permute-done.1.refs_2_, ...), custom_call_target="tpu_custom_call" | custom-call | flops 100000000 | bytes 1000000 | tf_op jit(solution)/shard_map/prep/pallas_call | solution.py:317
  55.3 0.4 collective-permute-done.11.rest_3_
  55.7 0.4 collective-permute-done.10.rest_2_
  56.1 0.0 collective-permute-done.9.rest_1_
  56.1 2.4 %batch.4 = s16[8,64,256]{2,1,0:T(8,128)(2,1)} custom-call(bf16[512,128]{1,0:T(8,128)(2,1)S(1)} %get-tuple-element.39.cols_ref, f32[8,512]{1,0:T(8,128)S(1)} %get-tuple-element.40.row_ref, bf16[512,100]{1,0:T(8,128)(2,1)S(1)} %get-tuple-element.41.enc_ref, bf16[256,256]{1,0:T(8,128)(2,1)S(1)} %copy-done.4, bf16[256,256]{1,0:T(8,128)(2,1)S(1)} %copy-done.5, ...), custom_call_target="tpu_custom_call" | custom-call | flops 100000000 | bytes 4000000 | tf_op jit(solution)/shard_map/batch/pallas_call | solution.py:383
  58.5 5.6 %all-to-all-start.2 = ((s16[8,64,256]{2,1,0:T(8,128)(2,1)}), s16[8,64,256]{2,1,0:T(8,128)(2,1)S(1)}, u32[]{:S(2)}, u32[]{:S(2)}) async-start(s16[8,64,256]{2,1,0:T(8,128)(2,1)} %batch.4), calls=%async_computation.2 | async-start | bytes 524288 | tf_op jit(solution)/shard_map/all_to_all | solution.py:564
  64.1 2.0 %collective-permute-start.12 = (bf16[4,64,256]{2,1,0:T(8,128)(2,1)S(1)}, bf16[4,64,256]{2,1,0:T(8,128)(2,1)S(1)}, u32[]{:S(2)}, u32[]{:S(2)}) collective-permute-start(bf16[4,64,256]{2,1,0:T(8,128)(2,1)S(1)} %copy-done.13), channel_id=1, source_target_pairs={{0,4},{4,0},{8,12},{12,8},{16,20},{20,16},{24,28},{28,24},{1,5},{5... | collective-permute-start | bytes 393224 | tf_op jit(solution)/shard_map/ppermute | solution.py:197
  66.1 6.0 %collective-permute-done.12.got_ref = bf16[4,64,256]{2,1,0:T(8,128)(2,1)S(1)} collective-permute-done((bf16[4,64,256]{2,1,0:T(8,128)(2,1)S(1)}, bf16[4,64,256]{2,1,0:T(8,128)(2,1)S(1)}, u32[]{:S(2)}, u32[]{:S(2)}) %collective-permute-start.12) | collective-permute-done | bytes 131104 | tf_op jit(solution)/shard_map/ppermute | solution.py:197
  72.1 0.0 copy-done.7
  72.1 2.8 %collective-permute-start.13 = (bf16[2,64,256]{2,1,0:T(8,128)(2,1)S(1)}, bf16[2,64,256]{2,1,0:T(8,128)(2,1)S(1)}, u32[]{:S(2)}, u32[]{:S(2)}) collective-permute-start(bf16[2,64,256]{2,1,0:T(8,128)(2,1)S(1)} %get-tuple-element.56), channel_id=1, source_target_pairs={{0,16},{4,20},{8,24},{12,28},{16,0},{20,4},{24,8},{28,12},{1,17},{... | collective-permute-start | bytes 196616 | tf_op jit(solution)/shard_map/ppermute | solution.py:197
  74.9 2.6 %collective-permute-done.13.got_ref = bf16[2,64,256]{2,1,0:T(8,128)(2,1)S(1)} collective-permute-done((bf16[2,64,256]{2,1,0:T(8,128)(2,1)S(1)}, bf16[2,64,256]{2,1,0:T(8,128)(2,1)S(1)}, u32[]{:S(2)}, u32[]{:S(2)}) %collective-permute-start.13) | collective-permute-done | bytes 65568 | tf_op jit(solution)/shard_map/ppermute | solution.py:197
  77.5 1.6 %collective-permute-start.14 = (bf16[1,64,256]{2,1,0:T(8,128)(2,1)S(1)}, bf16[1,64,256]{2,1,0:T(8,128)(2,1)S(1)}, u32[]{:S(2)}, u32[]{:S(2)}) collective-permute-start(bf16[1,64,256]{2,1,0:T(8,128)(2,1)S(1)} %get-tuple-element.58), channel_id=1, source_target_pairs={{0,8},{4,12},{8,0},{12,4},{16,24},{20,28},{24,16},{28,20},{1,9},{5... | collective-permute-start | bytes 98312 | tf_op jit(solution)/shard_map/ppermute | solution.py:197
  79.1 2.4 %collective-permute-done.14.refs_1_ = bf16[1,64,256]{2,1,0:T(8,128)(2,1)S(1)} collective-permute-done((bf16[1,64,256]{2,1,0:T(8,128)(2,1)S(1)}, bf16[1,64,256]{2,1,0:T(8,128)(2,1)S(1)}, u32[]{:S(2)}, u32[]{:S(2)}) %collective-permute-start.14) | collective-permute-done | bytes 32800 | tf_op jit(solution)/shard_map/ppermute | solution.py:197
  81.5 0.0 all-to-all-done.2.rest_1_.refs_3_
  81.5 0.2 next_block.5.rest_0_
  81.8 0.1 collective-permute-start.17
  81.8 1.3 %collective-permute-start.16 = (bf16[64,256]{1,0:T(8,128)(2,1)S(1)}, bf16[64,256]{1,0:T(8,128)(2,1)S(1)}, u32[]{:S(2)}, u32[]{:S(2)}) collective-permute-start(bf16[64,256]{1,0:T(8,128)(2,1)S(1)} %next_block.5.rest_0_), channel_id=1, source_target_pairs={{2,0},{3,1},{0,2},{1,3},{6,4},{7,5},{4,6},{5,7},{10,8},{11,9},{8,1... | collective-permute-start | bytes 98312 | tf_op jit(solution)/shard_map/ppermute | solution.py:40
  83.2 0.5 collective-permute-start.15
  83.7 1.3 %prep.5 = (bf16[512,128]{1,0:T(8,128)(2,1)S(1)}, f32[8,512]{1,0:T(8,128)S(1)}, bf16[512,100]{1,0:T(8,128)(2,1)S(1)}) custom-call(s32[3,3,1,256]{3,2,1,0:T(1,128)S(1)} %copy-done.10, s32[3,3,1,256]{3,2,1,0:T(1,128)S(1)} %collective-permute-done.refs_1_, s32[3,3,1,256]{3,2,1,0:T(1,128)S(1)} %collective-permute-done.1.refs_2_, ...), custom_call_target="tpu_custom_call" | custom-call | flops 100000000 | bytes 1000000 | tf_op jit(solution)/shard_map/prep/pallas_call | solution.py:317
  85.0 0.3 collective-permute-done.17.rest_3_
  85.3 0.5 collective-permute-done.16.rest_2_
  85.8 0.0 collective-permute-done.15.rest_1_
  85.8 2.4 %batch.5 = s16[8,64,256]{2,1,0:T(8,128)(2,1)} custom-call(bf16[512,128]{1,0:T(8,128)(2,1)S(1)} %get-tuple-element.50.cols_ref, f32[8,512]{1,0:T(8,128)S(1)} %get-tuple-element.51.row_ref, bf16[512,100]{1,0:T(8,128)(2,1)S(1)} %get-tuple-element.52.enc_ref, bf16[256,256]{1,0:T(8,128)(2,1)S(1)} %copy-done.4, bf16[256,256]{1,0:T(8,128)(2,1)S(1)} %copy-done.5, ...), custom_call_target="tpu_custom_call" | custom-call | flops 100000000 | bytes 4000000 | tf_op jit(solution)/shard_map/batch/pallas_call | solution.py:383
  88.2 5.8 %all-to-all-start.3 = ((s16[8,64,256]{2,1,0:T(8,128)(2,1)}), s16[8,64,256]{2,1,0:T(8,128)(2,1)S(1)}, u32[]{:S(2)}, u32[]{:S(2)}) async-start(s16[8,64,256]{2,1,0:T(8,128)(2,1)} %batch.5), calls=%async_computation.3 | async-start | bytes 524288 | tf_op jit(solution)/shard_map/all_to_all | solution.py:564
  94.0 2.4 %settle.1 = (f32[16,64,256]{2,1,0:T(8,128)}, f32[8,64,256]{2,1,0:T(8,128)S(1)}) custom-call(s32[3,1,8]{2,1,0:T(1,128)S(1)} %bitcast.12, f32[16,64,256]{2,1,0:T(8,128)S(1)} %bitcast.10, s16[8,72,256]{2,1,0:T(8,128)(2,1)S(1)} %all-to-all-done.1.refs_2_.rest_0_.counts, s16[8,64,256]{2,1,0:T(8,128)(2,1)S(1)} %all-to-all-done.2.rest_1_.refs_3_), custom_call_target="tpu_custom_call" | custom-call | flops 20000000 | bytes 3000000 | tf_op jit(solution)/shard_map/settle/pallas_call | solution.py:500
  96.4 6.8 %all-to-all-done.3.delta = s16[8,64,256]{2,1,0:T(8,128)(2,1)S(1)} async-done(((s16[8,64,256]{2,1,0:T(8,128)(2,1)}), s16[8,64,256]{2,1,0:T(8,128)(2,1)S(1)}, u32[]{:S(2)}, u32[]{:S(2)}) %all-to-all-start.3) | async-done | bytes 262176 | tf_op jit(solution)/shard_map/all_to_all | solution.py:564
  103.2 0.2 finish.1
  (27 shorter events, 0.2 us)
Async XLA Ops:
  3.3 16.6 %copy-start.3 = (f32[64,128]{1,0:T(8,128)S(1)}, f32[64,128]{1,0:T(8,128)}, u32[]{:S(2)}) copy-start(f32[64,128]{1,0:T(8,128)} %get-tuple-element.32.plan_ref) | copy-start | bytes 98308
  3.3 18.6 %copy-start.10 = (s32[3,3,1,256]{3,2,1,0:T(1,128)S(1)}, s32[3,3,1,256]{3,2,1,0:T(1,128)}, u32[]{:S(2)}) copy-start(s32[3,3,1,256]{3,2,1,0:T(1,128)} %get-tuple-element.33.refs_0_) | copy-start | bytes 27652
  3.3 21.8 %copy-start.12 = (f32[768]{0:T(1024)S(1)}, f32[768]{0:T(1024)}, u32[]{:S(2)}) copy-start(f32[768]{0:T(1024)} %param.27) | copy-start | bytes 9220
  3.3 23.6 %copy-start.9 = (f32[1,512]{1,0:T(1,128)S(1)}, f32[1,512]{1,0:T(1,128)}, u32[]{:S(2)}) copy-start(f32[1,512]{1,0:T(1,128)} %get-tuple-element.34.refs_4_.small_ref) | copy-start | bytes 6148
  3.4 25.0 %copy-start.2 = (bf16[256,768]{1,0:T(8,128)(2,1)S(1)}, bf16[256,768]{1,0:T(8,128)(2,1)}, u32[]{:S(2)}) copy-start(bf16[256,768]{1,0:T(8,128)(2,1)} %wh_ref.5) | copy-start | bytes 1179652
  20.0 8.4 %copy-start.1 = (bf16[256,768]{1,0:T(8,128)(2,1)S(1)}, bf16[256,768]{1,0:T(8,128)(2,1)}, u32[]{:S(2)}) copy-start(bf16[256,768]{1,0:T(8,128)(2,1)} %wi_ref.5) | copy-start | bytes 1179652
  20.0 8.3 %collective-permute-start.5 = (bf16[64,256]{1,0:T(8,128)(2,1)S(1)}, bf16[64,256]{1,0:T(8,128)(2,1)S(1)}, u32[]{:S(2)}, u32[]{:S(2)}) collective-permute-start(bf16[64,256]{1,0:T(8,128)(2,1)S(1)} %next_block.3.rest_1_), channel_id=1, source_target_pairs={{3,0},{2,1},{1,2},{0,3},{7,4},{6,5},{5,6},{4,7},{11,8},{10,9},{9,1... | collective-permute-start | bytes 98312 | tf_op jit(solution)/shard_map/ppermute | solution.py:40
  20.1 8.3 %collective-permute-start.4 = (bf16[64,256]{1,0:T(8,128)(2,1)S(1)}, bf16[64,256]{1,0:T(8,128)(2,1)S(1)}, u32[]{:S(2)}, u32[]{:S(2)}) collective-permute-start(bf16[64,256]{1,0:T(8,128)(2,1)S(1)} %next_block.3.rest_1_), channel_id=1, source_target_pairs={{2,0},{3,1},{0,2},{1,3},{6,4},{7,5},{4,6},{5,7},{10,8},{11,9},{8,1... | collective-permute-start | bytes 98312 | tf_op jit(solution)/shard_map/ppermute | solution.py:40
  21.5 6.9 %collective-permute-start.3 = (bf16[64,256]{1,0:T(8,128)(2,1)S(1)}, bf16[64,256]{1,0:T(8,128)(2,1)S(1)}, u32[]{:S(2)}, u32[]{:S(2)}) collective-permute-start(bf16[64,256]{1,0:T(8,128)(2,1)S(1)} %next_block.3.rest_1_), channel_id=1, source_target_pairs={{1,0},{0,1},{3,2},{2,3},{5,4},{4,5},{7,6},{6,7},{9,8},{8,9},{11,10... | collective-permute-start | bytes 98312 | tf_op jit(solution)/shard_map/ppermute | solution.py:40
  21.9 3.1 %collective-permute-start.2 = (s32[3,3,1,256]{3,2,1,0:T(1,128)S(1)}, s32[3,3,1,256]{3,2,1,0:T(1,128)S(1)}, u32[]{:S(2)}, u32[]{:S(2)}) collective-permute-start(s32[3,3,1,256]{3,2,1,0:T(1,128)S(1)} %copy-done.10), channel_id=1, source_target_pairs={{3,0},{2,1},{1,2},{0,3},{7,4},{6,5},{5,6},{4,7},{11,8},{10,9},{9,1... | collective-permute-start | bytes 27656 | tf_op jit(solution)/shard_map/ppermute | solution.py:40
  22.9 3.7 %collective-permute-start.1 = (s32[3,3,1,256]{3,2,1,0:T(1,128)S(1)}, s32[3,3,1,256]{3,2,1,0:T(1,128)S(1)}, u32[]{:S(2)}, u32[]{:S(2)}) collective-permute-start(s32[3,3,1,256]{3,2,1,0:T(1,128)S(1)} %copy-done.10), channel_id=1, source_target_pairs={{2,0},{3,1},{0,2},{1,3},{6,4},{7,5},{4,6},{5,7},{10,8},{11,9},{8,1... | collective-permute-start | bytes 27656 | tf_op jit(solution)/shard_map/ppermute | solution.py:40
  25.0 1.5 %collective-permute-start = (s32[3,3,1,256]{3,2,1,0:T(1,128)S(1)}, s32[3,3,1,256]{3,2,1,0:T(1,128)S(1)}, u32[]{:S(2)}, u32[]{:S(2)}) collective-permute-start(s32[3,3,1,256]{3,2,1,0:T(1,128)S(1)} %copy-done.10), channel_id=1, source_target_pairs={{1,0},{0,1},{3,2},{2,3},{5,4},{4,5},{7,6},{6,7},{9,8},{8,9},{11,10... | collective-permute-start | bytes 27656 | tf_op jit(solution)/shard_map/ppermute | solution.py:40
  27.0 1.4 %copy-start.4 = (bf16[256,256]{1,0:T(8,128)(2,1)S(1)}, bf16[256,256]{1,0:T(8,128)(2,1)}, u32[]{:S(2)}) copy-start(bf16[256,256]{1,0:T(8,128)(2,1)} %ws_ref.5) | copy-start | bytes 393220
  27.0 1.4 %copy-start.5 = (bf16[256,256]{1,0:T(8,128)(2,1)S(1)}, bf16[256,256]{1,0:T(8,128)(2,1)}, u32[]{:S(2)}) copy-start(bf16[256,256]{1,0:T(8,128)(2,1)} %wo_ref.5) | copy-start | bytes 393220
  27.0 1.4 %copy-start.6 = (bf16[100,256]{1,0:T(8,128)(2,1)S(1)}, bf16[100,256]{1,0:T(8,128)(2,1)}, u32[]{:S(2)}) copy-start(bf16[100,256]{1,0:T(8,128)(2,1)} %wt_ref.5) | copy-start | bytes 153604
  30.8 3.7 %copy-start.14 = (bf16[4,64,256]{2,1,0:T(8,128)(2,1)S(1)}, bf16[4,64,256]{2,1,0:T(8,128)(2,1)}, u32[]{:S(2)}) copy-start(bf16[4,64,256]{2,1,0:T(8,128)(2,1)} %get-tuple-element.43) | copy-start | bytes 393220
  30.8 11.7 %copy-start.8 = (bf16[4,64,256]{2,1,0:T(8,128)(2,1)S(1)}, bf16[4,64,256]{2,1,0:T(8,128)(2,1)}, u32[]{:S(2)}) copy-start(bf16[4,64,256]{2,1,0:T(8,128)(2,1)} %get-tuple-element.42.keep_in) | copy-start | bytes 393220
  30.8 21.1 %all-to-all-start.1 = ((s16[8,72,256]{2,1,0:T(8,128)(2,1)}), s16[8,72,256]{2,1,0:T(8,128)(2,1)S(1)}, u32[]{:S(2)}, u32[]{:S(2)}) async-start(s16[8,72,256]{2,1,0:T(8,128)(2,1)} %batch.3), calls=%async_computation.1 | async-start | bytes 589824 | tf_op jit(solution)/shard_map/all_to_all | solution.py:564
  34.6 7.9 %collective-permute-start.6 = (bf16[4,64,256]{2,1,0:T(8,128)(2,1)S(1)}, bf16[4,64,256]{2,1,0:T(8,128)(2,1)S(1)}, u32[]{:S(2)}, u32[]{:S(2)}) collective-permute-start(bf16[4,64,256]{2,1,0:T(8,128)(2,1)S(1)} %copy-done.14), channel_id=1, source_target_pairs={{0,4},{4,0},{8,12},{12,8},{16,20},{20,16},{24,28},{28,24},{1,5},{5... | collective-permute-start | bytes 393224 | tf_op jit(solution)/shard_map/ppermute | solution.py:197
  42.5 5.4 %collective-permute-start.7 = (bf16[2,64,256]{2,1,0:T(8,128)(2,1)S(1)}, bf16[2,64,256]{2,1,0:T(8,128)(2,1)S(1)}, u32[]{:S(2)}, u32[]{:S(2)}) collective-permute-start(bf16[2,64,256]{2,1,0:T(8,128)(2,1)S(1)} %get-tuple-element.45), channel_id=1, source_target_pairs={{0,16},{4,20},{8,24},{12,28},{16,0},{20,4},{24,8},{28,12},{1,17},{... | collective-permute-start | bytes 196616 | tf_op jit(solution)/shard_map/ppermute | solution.py:197
  47.9 4.0 %collective-permute-start.8 = (bf16[1,64,256]{2,1,0:T(8,128)(2,1)S(1)}, bf16[1,64,256]{2,1,0:T(8,128)(2,1)S(1)}, u32[]{:S(2)}, u32[]{:S(2)}) collective-permute-start(bf16[1,64,256]{2,1,0:T(8,128)(2,1)S(1)} %get-tuple-element.47), channel_id=1, source_target_pairs={{0,8},{4,12},{8,0},{12,4},{16,24},{20,28},{24,16},{28,20},{1,9},{5... | collective-permute-start | bytes 98312 | tf_op jit(solution)/shard_map/ppermute | solution.py:197
  52.0 3.6 %collective-permute-start.11 = (bf16[64,256]{1,0:T(8,128)(2,1)S(1)}, bf16[64,256]{1,0:T(8,128)(2,1)S(1)}, u32[]{:S(2)}, u32[]{:S(2)}) collective-permute-start(bf16[64,256]{1,0:T(8,128)(2,1)S(1)} %next_block.4.rest_0_), channel_id=1, source_target_pairs={{3,0},{2,1},{1,2},{0,3},{7,4},{6,5},{5,6},{4,7},{11,8},{10,9},{9,1... | collective-permute-start | bytes 98312 | tf_op jit(solution)/shard_map/ppermute | solution.py:40
  52.1 4.0 %collective-permute-start.10 = (bf16[64,256]{1,0:T(8,128)(2,1)S(1)}, bf16[64,256]{1,0:T(8,128)(2,1)S(1)}, u32[]{:S(2)}, u32[]{:S(2)}) collective-permute-start(bf16[64,256]{1,0:T(8,128)(2,1)S(1)} %next_block.4.rest_0_), channel_id=1, source_target_pairs={{2,0},{3,1},{0,2},{1,3},{6,4},{7,5},{4,6},{5,7},{10,8},{11,9},{8,1... | collective-permute-start | bytes 98312 | tf_op jit(solution)/shard_map/ppermute | solution.py:40
  53.5 2.6 %collective-permute-start.9 = (bf16[64,256]{1,0:T(8,128)(2,1)S(1)}, bf16[64,256]{1,0:T(8,128)(2,1)S(1)}, u32[]{:S(2)}, u32[]{:S(2)}) collective-permute-start(bf16[64,256]{1,0:T(8,128)(2,1)S(1)} %next_block.4.rest_0_), channel_id=1, source_target_pairs={{1,0},{0,1},{3,2},{2,3},{5,4},{4,5},{7,6},{6,7},{9,8},{8,9},{11,10... | collective-permute-start | bytes 98312 | tf_op jit(solution)/shard_map/ppermute | solution.py:40
  58.5 5.6 %copy-start.13 = (bf16[4,64,256]{2,1,0:T(8,128)(2,1)S(1)}, bf16[4,64,256]{2,1,0:T(8,128)(2,1)}, u32[]{:S(2)}) copy-start(bf16[4,64,256]{2,1,0:T(8,128)(2,1)} %get-tuple-element.54) | copy-start | bytes 393220
  58.5 13.6 %copy-start.7 = (bf16[4,64,256]{2,1,0:T(8,128)(2,1)S(1)}, bf16[4,64,256]{2,1,0:T(8,128)(2,1)}, u32[]{:S(2)}) copy-start(bf16[4,64,256]{2,1,0:T(8,128)(2,1)} %get-tuple-element.53.keep_in) | copy-start | bytes 393220
  58.5 23.0 %all-to-all-start.2 = ((s16[8,64,256]{2,1,0:T(8,128)(2,1)}), s16[8,64,256]{2,1,0:T(8,128)(2,1)S(1)}, u32[]{:S(2)}, u32[]{:S(2)}) async-start(s16[8,64,256]{2,1,0:T(8,128)(2,1)} %batch.4), calls=%async_computation.2 | async-start | bytes 524288 | tf_op jit(solution)/shard_map/all_to_all | solution.py:564
  64.1 8.0 %collective-permute-start.12 = (bf16[4,64,256]{2,1,0:T(8,128)(2,1)S(1)}, bf16[4,64,256]{2,1,0:T(8,128)(2,1)S(1)}, u32[]{:S(2)}, u32[]{:S(2)}) collective-permute-start(bf16[4,64,256]{2,1,0:T(8,128)(2,1)S(1)} %copy-done.13), channel_id=1, source_target_pairs={{0,4},{4,0},{8,12},{12,8},{16,20},{20,16},{24,28},{28,24},{1,5},{5... | collective-permute-start | bytes 393224 | tf_op jit(solution)/shard_map/ppermute | solution.py:197
  72.1 5.3 %collective-permute-start.13 = (bf16[2,64,256]{2,1,0:T(8,128)(2,1)S(1)}, bf16[2,64,256]{2,1,0:T(8,128)(2,1)S(1)}, u32[]{:S(2)}, u32[]{:S(2)}) collective-permute-start(bf16[2,64,256]{2,1,0:T(8,128)(2,1)S(1)} %get-tuple-element.56), channel_id=1, source_target_pairs={{0,16},{4,20},{8,24},{12,28},{16,0},{20,4},{24,8},{28,12},{1,17},{... | collective-permute-start | bytes 196616 | tf_op jit(solution)/shard_map/ppermute | solution.py:197
  77.5 4.0 %collective-permute-start.14 = (bf16[1,64,256]{2,1,0:T(8,128)(2,1)S(1)}, bf16[1,64,256]{2,1,0:T(8,128)(2,1)S(1)}, u32[]{:S(2)}, u32[]{:S(2)}) collective-permute-start(bf16[1,64,256]{2,1,0:T(8,128)(2,1)S(1)} %get-tuple-element.58), channel_id=1, source_target_pairs={{0,8},{4,12},{8,0},{12,4},{16,24},{20,28},{24,16},{28,20},{1,9},{5... | collective-permute-start | bytes 98312 | tf_op jit(solution)/shard_map/ppermute | solution.py:197
  81.8 3.6 %collective-permute-start.17 = (bf16[64,256]{1,0:T(8,128)(2,1)S(1)}, bf16[64,256]{1,0:T(8,128)(2,1)S(1)}, u32[]{:S(2)}, u32[]{:S(2)}) collective-permute-start(bf16[64,256]{1,0:T(8,128)(2,1)S(1)} %next_block.5.rest_0_), channel_id=1, source_target_pairs={{3,0},{2,1},{1,2},{0,3},{7,4},{6,5},{5,6},{4,7},{11,8},{10,9},{9,1... | collective-permute-start | bytes 98312 | tf_op jit(solution)/shard_map/ppermute | solution.py:40
  81.8 4.0 %collective-permute-start.16 = (bf16[64,256]{1,0:T(8,128)(2,1)S(1)}, bf16[64,256]{1,0:T(8,128)(2,1)S(1)}, u32[]{:S(2)}, u32[]{:S(2)}) collective-permute-start(bf16[64,256]{1,0:T(8,128)(2,1)S(1)} %next_block.5.rest_0_), channel_id=1, source_target_pairs={{2,0},{3,1},{0,2},{1,3},{6,4},{7,5},{4,6},{5,7},{10,8},{11,9},{8,1... | collective-permute-start | bytes 98312 | tf_op jit(solution)/shard_map/ppermute | solution.py:40
  83.2 2.6 %collective-permute-start.15 = (bf16[64,256]{1,0:T(8,128)(2,1)S(1)}, bf16[64,256]{1,0:T(8,128)(2,1)S(1)}, u32[]{:S(2)}, u32[]{:S(2)}) collective-permute-start(bf16[64,256]{1,0:T(8,128)(2,1)S(1)} %next_block.5.rest_0_), channel_id=1, source_target_pairs={{1,0},{0,1},{3,2},{2,3},{5,4},{4,5},{7,6},{6,7},{9,8},{8,9},{11,10... | collective-permute-start | bytes 98312 | tf_op jit(solution)/shard_map/ppermute | solution.py:40
  85.8 8.1 %copy-start = (f32[1024,256]{1,0:T(8,128)S(1)}, f32[1024,256]{1,0:T(8,128)}, u32[]{:S(2)}) copy-start(f32[1024,256]{1,0:T(8,128)} %param.14) | copy-start | bytes 3145732
  88.2 5.8 %copy-start.11 = (s32[8,3,1]{0,2,1:T(1,128)S(1)}, s32[8,3,1]{0,2,1:T(1,128)}, u32[]{:S(2)}) copy-start(s32[8,3,1]{0,2,1:T(1,128)} %param.18) | copy-start | bytes 292
  88.2 15.0 %all-to-all-start.3 = ((s16[8,64,256]{2,1,0:T(8,128)(2,1)}), s16[8,64,256]{2,1,0:T(8,128)(2,1)S(1)}, u32[]{:S(2)}, u32[]{:S(2)}) async-start(s16[8,64,256]{2,1,0:T(8,128)(2,1)} %batch.5), calls=%async_computation.3 | async-start | bytes 524288 | tf_op jit(solution)/shard_map/all_to_all | solution.py:564
